TPU v7x, 128 devices: a whole 4x4x4 slice. The times are simulated.
128 devices in a mesh: seq: 16 (over z_hi, x, core), chan: 8 (over z_lo, y).
Axes of the slice: x: 4, y: 4, z: 4 (z_hi: 2, z_lo: 2; z = z_hi * 2 + z_lo), core: 2. Of those that a mesh axis runs over, the one named last changes fastest.
Arguments:
- hidden_states: bfloat16 [4096, 4096], P('chan', 'seq'), may hold values from -700 to 700
- norm_gain: float32 [4096], P('chan'), may hold values from 0.1 to 1.9
- short_filter: float32 [4096, 128], P('chan'), may hold values from -0.5 to 0.5
- long_filter: bfloat16 [4096, 4096], P('chan', 'seq'), may hold values from -0.09375 to 0.09375
- long_bias: float32 [4096], P('chan'), may hold values from -4 to 4
- gate_stream: bfloat16 [4096, 4096], P('chan', 'seq'), may hold values from -6 to 6
- upstream: bfloat16 [4096, 4096], P(None, 'seq'), may hold values from -6 to 6
Outputs:
- mixed: bfloat16 [4096, 4096], P('chan', 'seq')
- weight_grad: float32 [4096, 4096], P('seq', 'chan')
All inputs are finite; a program needn't handle non-finite values.
Results may differ from a plain program's by a relative error of at most 0.015.
Values may be sent and summed in bfloat16 or wider, within the bound.
No kernel may reach another device: no remote copies, remote signals or barrier semaphores. Data moves between devices by JAX's collectives and lax.ppermute only.
A program may use at most 64 MiB of HBM per device.

v0:
```python
import functools
import math

import jax
import jax.numpy as jnp
import numpy as np
from jax import lax
from jax.experimental import pallas as pl
from jax.experimental.pallas import tpu as pltpu
from jax.sharding import PartitionSpec as P


D = 4096
EPSILON = 1e-05
OUTER = 32
INNER = 128
LENGTH = OUTER * INNER
BF16 = jnp.bfloat16
F32 = jnp.float32


def tables():
    m = np.arange(INNER, dtype=np.float64)
    turn = 2.0 * np.pi * (np.arange(OUTER)[:, None] + 0.25) * m[None, :] / LENGTH
    angle = 2.0 * np.pi * ((m[:, None] * m[None, :]) % INNER) / INNER
    cos, sin = np.cos(angle), np.sin(angle)
    ahead = np.block([[cos, -sin], [sin, cos]])
    back = np.block([[cos, sin], [-sin, cos]])
    parts = []
    for table in (ahead, back):
        upper = table.astype(BF16)
        lower = (table - upper.astype(np.float64)).astype(BF16)
        parts.append(np.concatenate([upper, lower, upper]))
    return [np.cos(turn).astype(np.float32), -np.sin(turn).astype(np.float32), *parts]


def turned(value, step, total, sign):
    re, im = value
    step %= total
    if step == 0:
        return re, im
    if 4 * step == total:
        return (-im, re) if sign > 0 else (im, -re)
    half = math.sqrt(0.5)
    if 8 * step == total:
        return ((re - im) * half, (re + im) * half) if sign > 0 else ((re + im) * half, (im - re) * half)
    if 8 * step == 3 * total:
        if sign > 0:
            return (re + im) * -half, (re - im) * half
        return (im - re) * half, (re + im) * -half
    cos = math.cos(2.0 * math.pi * step / total)
    sin = sign * math.sin(2.0 * math.pi * step / total)
    return re * cos - im * sin, re * sin + im * cos


def transform(values, sign):
    total = len(values)
    if total == 1:
        return values
    even, odd = transform(values[0::2], sign), transform(values[1::2], sign)
    first, second = [], []
    for k in range(total // 2):
        er, ei = even[k]
        dr, di = turned(odd[k], k, total, sign)
        first.append((er + dr, ei + di))
        second.append((er - dr, ei - di))
    return first + second


def in_two_passes(load, store, half_ref, sign):
    for q in range(4):
        for k, value in enumerate(transform([load(4 * p + q) for p in range(8)], sign)):
            half_ref[q, k, 0], half_ref[q, k, 1] = turned(value, q * k, OUTER, sign)
    for k in range(8):
        for j, value in enumerate(transform([(half_ref[q, k, 0], half_ref[q, k, 1]) for q in range(4)], sign)):
            store(k + 8 * j, value)


def groups_of_rows(body):
    for g in range(4):
        body(slice(8 * g, 8 * g + 8), g)


def outer_ahead(time_ref, mid_ref, half_ref, twr_ref, twi_ref):
    def group(rows, g):
        def load(n):
            x = time_ref[n, rows, :]
            angle = 2.0 * math.pi * n / (4 * OUTER)
            return x * math.cos(angle), x * -math.sin(angle)

        def store(k, value):
            re, im = value
            tr, ti = twr_ref[k : k + 1, :], twi_ref[k : k + 1, :]
            mid_ref[k, rows, 0:INNER] = re * tr - im * ti
            mid_ref[k, rows, INNER:] = re * ti + im * tr

        in_two_passes(load, store, half_ref.at[g], -1)

    groups_of_rows(group)


def outer_back(mid_ref, time_ref, half_ref, twr_ref, twi_ref):
    def group(rows, g):
        def load(k):
            re, im = mid_ref[k, rows, 0:INNER], mid_ref[k, rows, INNER:]
            tr, ti = twr_ref[k : k + 1, :], twi_ref[k : k + 1, :]
            return re * tr + im * ti, im * tr - re * ti

        def store(n, value):
            re, im = value
            angle = 2.0 * math.pi * n / (4 * OUTER)
            time_ref[n, rows, :] = re * (math.cos(angle) / LENGTH) - im * (math.sin(angle) / LENGTH)

        in_two_passes(load, store, half_ref.at[g], 1)

    groups_of_rows(group)


def product(rows, table_ref):
    upper = rows.astype(BF16)
    lower = (rows - upper.astype(F32)).astype(BF16)
    return jnp.dot(jnp.concatenate([upper, upper, lower], axis=1), table_ref[...], preferred_element_type=F32)


def complex_product(a, b):
    ar, ai, br, bi = a[:, :INNER], a[:, INNER:], b[:, :INNER], b[:, INNER:]
    return jnp.concatenate([ar * br - ai * bi, ar * bi + ai * br], axis=1)


def chunks(body):
    def step(j, carry):
        body(pl.ds(pl.multiple_of(j * 8, 8), 8))
        return carry

    lax.fori_loop(0, OUTER // 8, step, 0)


def flat(value):
    return value.reshape(value.shape[0] * value.shape[1], value.shape[2])


def column_of(row_ref, first):
    total = row_ref.shape[1]
    lane = lax.broadcasted_iota(jnp.int32, (32, total), 1)
    wanted = lax.broadcasted_iota(jnp.int32, (32, total), 0) + first
    return jnp.sum(jnp.where(lane == wanted, row_ref[...], 0.0), axis=1, keepdims=True)


def filter_kernel(got_ref, taps_ref, bias_ref, twr_ref, twi_ref, ahead, back, spec_ref, time_ref, mid_ref, half_ref):
    first = pl.multiple_of(lax.axis_index("seq") * 32, 32)
    bias = column_of(bias_ref, first)
    own_taps = taps_ref[pl.ds(first, 32), :]
    for b in range(16):
        for h in range(2):
            time_ref[2 * b + h] = got_ref[b, 32:64, h * INNER : (h + 1) * INNER].astype(F32)
    outer_ahead(time_ref, mid_ref, half_ref, twr_ref, twi_ref)

    def combine(ks):
        long = product(flat(mid_ref[ks]), ahead)
        lift = jnp.concatenate([jnp.broadcast_to(bias, (32, INNER)), jnp.zeros((32, INNER), F32)], axis=1)
        long = long + jnp.tile(lift, (8, 1))
        taps = own_taps[None]
        tr, ti = twr_ref[ks, :][:, None, :], twi_ref[ks, :][:, None, :]
        short = product(flat(jnp.concatenate([taps * tr, taps * ti], axis=2)), ahead)
        mid_ref[ks] = product(complex_product(long, short), back).reshape(8, 32, 2 * INNER)

    chunks(combine)
    outer_back(mid_ref, time_ref, half_ref, twr_ref, twi_ref)
    outer_ahead(time_ref, mid_ref, half_ref, twr_ref, twi_ref)

    def finish(ks):
        spec_ref[ks] = product(flat(mid_ref[ks]), ahead).reshape(8, 32, 2 * INNER)

    chunks(finish)


def signal_kernel(
    got_ref, squares_ref, gain_ref, spec_ref, twr_ref, twi_ref, ahead, back, mixed_ref, time_ref, mid_ref, half_ref
):
    first = lax.axis_index("seq") * 32
    gain = jnp.broadcast_to(column_of(gain_ref, first), (32, INNER))
    for b in range(16):
        scale = lax.rsqrt(jnp.sum(squares_ref[b], axis=0, keepdims=True) / D + EPSILON)
        for h in range(2):
            cols = slice(h * INNER, (h + 1) * INNER)
            normed = got_ref[b, 0:32, cols].astype(F32) * scale[:, cols] * gain
            time_ref[2 * b + h] = normed.astype(BF16).astype(F32)
    outer_ahead(time_ref, mid_ref, half_ref, twr_ref, twi_ref)

    def combine(ks):
        spec = product(flat(mid_ref[ks]), ahead)
        joint = complex_product(spec, flat(spec_ref[ks]))
        mid_ref[ks] = product(joint, back).reshape(8, 32, 2 * INNER)

    chunks(combine)
    outer_back(mid_ref, time_ref, half_ref, twr_ref, twi_ref)
    for b in range(16):
        for h in range(2):
            cols = slice(h * INNER, (h + 1) * INNER)
            long_out = time_ref[2 * b + h].astype(BF16).astype(F32)
            mixed_ref[b, :, cols] = (got_ref[b, 64:96, cols].astype(F32) * long_out).astype(BF16)


def vmem(count):
    return [pl.BlockSpec(memory_space=pltpu.VMEM)] * count


SCRATCH = [
    pltpu.VMEM((OUTER, 32, INNER), F32),
    pltpu.VMEM((OUTER, 32, 2 * INNER), F32),
    pltpu.VMEM((4, 4, 8, 2, 8, INNER), F32),
]


def filter_spectrum(got, taps, bias, consts):
    return pl.pallas_call(
        filter_kernel,
        out_shape=jax.ShapeDtypeStruct((OUTER, 32, 2 * INNER), F32),
        in_specs=vmem(7),
        out_specs=vmem(1)[0],
        scratch_shapes=SCRATCH,
        cost_estimate=pl.CostEstimate(flops=2_000_000_000, bytes_accessed=3_000_000, transcendentals=0),
        name="filter_spectrum",
    )(got, taps, bias, *consts)


def gated_convolution(got, squares, gain, spec, consts):
    return pl.pallas_call(
        signal_kernel,
        out_shape=jax.ShapeDtypeStruct((16, 32, 256), BF16),
        in_specs=vmem(8),
        out_specs=vmem(1)[0],
        scratch_shapes=SCRATCH,
        cost_estimate=pl.CostEstimate(flops=1_000_000_000, bytes_accessed=3_000_000, transcendentals=0),
    )(got, squares, gain, spec, *consts)


def pack_kernel(hidden_ref, long_ref, gate_ref, up_ref, payload_ref, squares_ref, sems):
    chan = lax.axis_index("chan")
    sources = [hidden_ref, long_ref, gate_ref, up_ref.at[:, pl.ds(pl.multiple_of(chan * 32, 32), 32), :]]
    copies = [
        pltpu.make_async_copy(source, payload_ref.at[:, 32 * i : 32 * i + 32, :], sems.at[i])
        for i, source in enumerate(sources)
    ]
    for copy in copies:
        copy.start()
    copies[0].wait()
    total = jnp.zeros((8, 256), F32)
    for b in range(16):
        states = payload_ref[b, 0:32, :].astype(F32)
        powers = states * states
        for r in range(4):
            total = total + powers[8 * r : 8 * r + 8]
    squares_ref[...] = total
    for copy in copies[1:]:
        copy.wait()


def pack(hidden, long_filter, gate, upstream):
    return pl.pallas_call(
        pack_kernel,
        out_shape=(jax.ShapeDtypeStruct((16, 128, 256), BF16), jax.ShapeDtypeStruct((8, 256), F32)),
        in_specs=[pl.BlockSpec(memory_space=pl.ANY)] * 4,
        out_specs=tuple(vmem(2)),
        scratch_shapes=[pltpu.SemaphoreType.DMA((4,))],
        name="pack",
    )(hidden, long_filter, gate, upstream)


def place_of(s):
    return s // 8, (s // 2) % 4, s % 2


def over_seq(value, dz, dx, dk):
    pairs = []
    for s in range(16):
        z, x, k = place_of(s)
        pairs.append((s, (z ^ dz) * 8 + ((x + dx) % 4) * 2 + (k ^ dk)))
    return lax.ppermute(value, "seq", pairs)


def over_chan(value, dz, dy):
    pairs = [(c, ((c // 4) ^ dz) * 4 + (c + dy) % 4) for c in range(8)]
    return lax.ppermute(value, "chan", pairs)


def around(block, move):
    right = move(block, 1)
    left = move(block, -1)
    far_a = move(right[:8], 1)
    far_b = move(left[8:], -1)
    return [(block, 0, 0), (right, 3, 0), (left, 1, 0), (far_a, 2, 0), (far_b, 2, 8)]


def gather_seq(own):
    side = over_seq(own, 1, 0, 0)
    pieces = []
    for dz, block in enumerate((own, side)):
        for value, dx, row in around(block, lambda v, d: over_seq(v, 0, d, 0)):
            pieces.append((value, 0, dz, dx, row))
            pieces.append((over_seq(value, 0, 0, 1), 1, dz, dx, row))
    return pieces


def gather_chan(own):
    side = over_chan(own, 1, 0)
    pieces = []
    for dz, block in enumerate((own, side)):
        for value, dy, row in around(block, lambda v, d: over_chan(v, 0, d)):
            pieces.append((value, dz, dy, row))
    return pieces


def whole_rows(refs, keys):
    blocks = {}
    for ref, (*key, row) in zip(refs, keys, strict=True):
        for b in range(ref.shape[0]):
            blocks.setdefault(tuple(key), {})[row + b] = (ref, b)
    values = [jnp.concatenate([rows[b][0][rows[b][1]] for b in range(16)], axis=1) for rows in blocks.values()]
    return jnp.concatenate(values, axis=0), list(blocks)


def grad_kernel(mixed_keys, up_keys, *refs):
    seq, chan = lax.axis_index("seq"), lax.axis_index("chan")
    mixed_refs, up_refs = refs[: len(mixed_keys)], refs[len(mixed_keys) : len(mixed_keys) + len(up_keys)]
    mixed_ref, grad_ref, rows_ref = refs[len(mixed_keys) + len(up_keys) :]
    mixed, sources = whole_rows(mixed_refs, mixed_keys)
    up, owners = whole_rows(up_refs, up_keys)
    total = lax.dot_general(mixed, up, (((1,), (1,)), ((), ())), preferred_element_type=F32)

    def source_place(dk, dz, dx):
        z = lax.bitwise_xor(seq // 8, dz)
        x = lax.bitwise_and(seq // 2 + dx, 3)
        k = lax.bitwise_xor(lax.bitwise_and(seq, 1), dk)
        return pl.ds(pl.multiple_of((z * 8 + x * 2 + k) * 32, 32), 32)

    for i, key in enumerate(sources):
        rows_ref[source_place(*key), :] = total[32 * i : 32 * i + 32]
    for ref, (*key, row) in zip(mixed_refs, mixed_keys, strict=True):
        place = source_place(*key)
        if ref.shape[0] == 16:
            mixed_ref[place, :] = ref[seq]
        else:

            @pl.when(seq // 8 == row // 8)
            def _(ref=ref, place=place):
                mixed_ref[place, :] = ref[lax.bitwise_and(seq, 7)]

    turned_rows = rows_ref[...].T
    for i, (dz, dy) in enumerate(owners):
        owner = lax.bitwise_xor(chan // 4, dz) * 4 + lax.bitwise_and(chan + dy, 3)
        grad_ref[pl.ds(pl.multiple_of(owner * 32, 32), 32), :] = turned_rows[32 * i : 32 * i + 32]


def weight_gradient(mixed, up):
    mixed_keys, up_keys = [piece[1:] for piece in mixed], [piece[1:] for piece in up]
    return pl.pallas_call(
        functools.partial(grad_kernel, mixed_keys, up_keys),
        out_shape=(jax.ShapeDtypeStruct((512, 256), BF16), jax.ShapeDtypeStruct((256, 512), F32)),
        in_specs=vmem(len(mixed) + len(up)),
        out_specs=tuple(vmem(2)),
        scratch_shapes=[pltpu.VMEM((512, 256), F32)],
        cost_estimate=pl.CostEstimate(flops=1_000_000_000, bytes_accessed=7_000_000, transcendentals=0),
        name="weight_gradient",
    )(*[piece[0] for piece in mixed], *[piece[0] for piece in up])


def exchange(value, axis):
    return lax.all_to_all(value, axis, split_axis=0, concat_axis=0, tiled=True)


def step(hidden_states, norm_gain, short_filter, long_filter, long_bias, gate_stream, upstream):
    consts = [jnp.asarray(table) for table in tables()]
    blocks = [value.reshape(16, 32, 256) for value in (hidden_states, long_filter, gate_stream)]
    payload, squares = pack(*blocks, upstream.reshape(16, 256, 256))
    squares = squares + over_chan(squares, 1, 0)
    got = exchange(payload, "seq")
    squares = squares + over_chan(squares, 0, 1)
    squares = squares + over_chan(squares, 0, 2)
    squares = jnp.broadcast_to(squares, (16, 8, 256))
    squares = exchange(squares, "seq")
    spec = filter_spectrum(got, short_filter, long_bias[None, :], consts)
    up = gather_chan(got[:, 96:128])
    mixed = gated_convolution(got, squares, norm_gain[None, :], spec, consts)
    return weight_gradient(gather_seq(mixed), up)


def solution(mesh):
    placed = (
        P("chan", "seq"),
        P("chan"),
        P("chan", None),
        P("chan", "seq"),
        P("chan"),
        P("chan", "seq"),
        P(None, "seq"),
    )
    return jax.shard_map(
        step,
        mesh=mesh,
        in_specs=placed,
        out_specs=(P("chan", "seq"), P("seq", "chan")),
        check_vma=False,
    )
```

profile of v0, /device:TPU:1, one launch (start us, length us, event | category | flops | bytes accessed | tf_op | source)
XLA Modules:
  0.0 115.0 jit_solution(13760627326660950456)
XLA Ops:
  0.6 2.3 %pack.1 = (bf16[16,128,256]{2,1,0:T(8,128)(2,1)}, f32[8,256]{1,0:T(8,128)}) custom-call(bf16[16,32,256]{2,1,0:T(8,128)(2,1)} %bitcast.7, bf16[16,32,256]{2,1,0:T(8,128)(2,1)} %bitcast.8, bf16[16,32,256]{2,1,0:T(8,128)(2,1)} %bitcast.9, bf16[16,256,256]{2,1,0:T(8,128)(2,1)} %bitcast.6), custom_call_target="tpu_custom_call" | custom-call | tf_op jit(solution)/shard_map/pack/pallas_call | solution.py:260
  2.9 9.1 %all-to-all-start = ((bf16[16,128,256]{2,1,0:T(8,128)(2,1)}), bf16[16,128,256]{2,1,0:T(8,128)(2,1)S(1)}, u32[]{:S(2)}, u32[]{:S(2)}) async-start(bf16[16,128,256]{2,1,0:T(8,128)(2,1)} %get-tuple-element.4), calls=%async_computation | async-start | bytes 2097152 | tf_op jit(solution)/shard_map/all_to_all | solution.py:369
  12.0 0.8 collective-permute-start
  12.9 7.3 %collective-permute-done = f32[8,256]{1,0:T(8,128)S(1)} collective-permute-done((f32[8,256]{1,0:T(8,128)S(1)}, f32[8,256]{1,0:T(8,128)S(1)}, u32[]{:S(2)}, u32[]{:S(2)}) %collective-permute-start) | collective-permute-done | bytes 8224 | tf_op jit(solution)/shard_map/ppermute | solution.py:284
  20.2 1.3 %collective-permute-start.1 = (f32[8,256]{1,0:T(8,128)S(1)}, f32[8,256]{1,0:T(8,128)S(1)}, u32[]{:S(2)}, u32[]{:S(2)}) collective-permute-start(f32[8,256]{1,0:T(8,128)S(1)} %add.9), channel_id=1, source_target_pairs={{0,1},{1,2},{2,3},{3,0},{4,5},{5,6},{6,7},{7,4},{8,9},{9,10},{10,1... | collective-permute-start | bytes 24584 | tf_op jit(solution)/shard_map/ppermute | solution.py:284
  21.5 2.8 %collective-permute-done.1 = f32[8,256]{1,0:T(8,128)S(1)} collective-permute-done((f32[8,256]{1,0:T(8,128)S(1)}, f32[8,256]{1,0:T(8,128)S(1)}, u32[]{:S(2)}, u32[]{:S(2)}) %collective-permute-start.1) | collective-permute-done | bytes 8224 | tf_op jit(solution)/shard_map/ppermute | solution.py:284
  24.2 1.6 %collective-permute-start.2 = (f32[8,256]{1,0:T(8,128)S(1)}, f32[8,256]{1,0:T(8,128)S(1)}, u32[]{:S(2)}, u32[]{:S(2)}) collective-permute-start(f32[8,256]{1,0:T(8,128)S(1)} %add.10), channel_id=1, source_target_pairs={{0,2},{1,3},{2,0},{3,1},{4,6},{5,7},{6,4},{7,5},{8,10},{9,11},{10,... | collective-permute-start | bytes 24584 | tf_op jit(solution)/shard_map/ppermute | solution.py:284
  25.9 2.7 %collective-permute-done.2 = f32[8,256]{1,0:T(8,128)S(1)} collective-permute-done((f32[8,256]{1,0:T(8,128)S(1)}, f32[8,256]{1,0:T(8,128)S(1)}, u32[]{:S(2)}, u32[]{:S(2)}) %collective-permute-start.2) | collective-permute-done | bytes 8224 | tf_op jit(solution)/shard_map/ppermute | solution.py:284
  28.5 0.8 all-to-all-done.got_ref
  29.3 0.7 broadcast_in_dim.9
  30.0 14.2 %all-to-all-start.1 = ((f32[16,8,256]{2,1,0:T(8,128)}), f32[16,8,256]{2,1,0:T(8,128)S(1)}, u32[]{:S(2)}, u32[]{:S(2)}) async-start(f32[16,8,256]{2,1,0:T(8,128)} %broadcast_in_dim.9), calls=%async_computation.1 | async-start | bytes 262144 | tf_op jit(solution)/shard_map/all_to_all | solution.py:369
  44.2 1.6 %collective-permute-start.23 = (bf16[16,32,256]{2,1,0:T(8,128)(2,1)S(1)}, bf16[16,32,256]{2,1,0:T(8,128)(2,1)S(1)}, u32[]{:S(2)}, u32[]{:S(2)}) collective-permute-start(bf16[16,32,256]{2,1,0:T(8,128)(2,1)S(1)} %slice.40.refs_20_), channel_id=1, source_target_pairs={{0,3},{1,0},{2,1},{3,2},{4,7},{5,4},{6,5},{7,6},{8,11},{9,8},{10,9... | collective-permute-start | bytes 786440 | tf_op jit(solution)/shard_map/ppermute | solution.py:284
  45.8 7.9 %filter_spectrum.1.spec_ref = f32[32,32,256]{2,1,0:T(8,128)} custom-call(bf16[16,128,256]{2,1,0:T(8,128)(2,1)} %copy-done, f32[512,128]{1,0:T(8,128)} %taps_ref.1, f32[1,512]{1,0:T(1,128)} %bitcast.10, f32[32,128]{1,0:T(8,128)} %constant.8.clone.twr_ref, f32[32,128]{1,0:T(8,128)} %constant.9.clone.twi_ref, bf16[768,256]{1,0:T(8,128)(2,1)} %constant.10.clone.ahead, ...), custom_call_target="tpu_custom_call" | custom-call | flops 2000000000 | bytes 3000000 | tf_op jit(solution)/shard_map/filter_spectrum/pallas_call | solution.py:216
  53.7 0.7 copy-done.28
  54.4 6.0 %shard_map.122.refs_0_ = bf16[16,32,256]{2,1,0:T(8,128)(2,1)} custom-call(bf16[16,128,256]{2,1,0:T(8,128)(2,1)} %copy-done, f32[16,8,256]{2,1,0:T(8,128)} %copy-done.28, f32[1,512]{1,0:T(1,128)} %bitcast.11, f32[32,32,256]{2,1,0:T(8,128)} %filter_spectrum.1.spec_ref, f32[32,128]{1,0:T(8,128)} %constant.8.clone.twr_ref, f32[32,128]{1,0:T(8,128)} %constant.9.clone.twi_ref, ...), custom_call_target="tpu_custom_call" | custom-call | flops 1000000000 | bytes 3000000 | tf_op jit(solution)/shard_map/pallas_call | solution.py:228
  60.4 2.6 %collective-permute-start.6 = (bf16[16,32,256]{2,1,0:T(8,128)(2,1)}, bf16[16,32,256]{2,1,0:T(8,128)(2,1)S(1)}, u32[]{:S(2)}, u32[]{:S(2)}) collective-permute-start(bf16[16,32,256]{2,1,0:T(8,128)(2,1)} %shard_map.122.refs_0_), channel_id=1, source_target_pairs={{0,48},{8,56},{16,0},{24,8},{32,16},{40,24},{48,32},{56,40},{64,11... | collective-permute-start | bytes 786440 | tf_op jit(solution)/shard_map/ppermute | solution.py:279
  63.0 2.8 %collective-permute-start.12 = (bf16[16,32,256]{2,1,0:T(8,128)(2,1)}, bf16[16,32,256]{2,1,0:T(8,128)(2,1)S(1)}, u32[]{:S(2)}, u32[]{:S(2)}) collective-permute-start(bf16[16,32,256]{2,1,0:T(8,128)(2,1)} %shard_map.122.refs_0_), channel_id=1, source_target_pairs={{0,64},{8,72},{16,80},{24,88},{32,96},{40,104},{48,112},{56,120},{... | collective-permute-start | bytes 786440 | tf_op jit(solution)/shard_map/ppermute | solution.py:279
  65.8 1.8 %collective-permute-start.3 = (bf16[16,32,256]{2,1,0:T(8,128)(2,1)}, bf16[16,32,256]{2,1,0:T(8,128)(2,1)S(1)}, u32[]{:S(2)}, u32[]{:S(2)}) collective-permute-start(bf16[16,32,256]{2,1,0:T(8,128)(2,1)} %shard_map.122.refs_0_), channel_id=1, source_target_pairs={{0,8},{8,0},{16,24},{24,16},{32,40},{40,32},{48,56},{56,48},{64,72... | collective-permute-start | bytes 786440 | tf_op jit(solution)/shard_map/ppermute | solution.py:279
  67.7 0.4 collective-permute-done.6.refs_4_
  68.1 2.6 %collective-permute-start.25 = (bf16[8,32,256]{2,1,0:T(8,128)(2,1)S(1)}, bf16[8,32,256]{2,1,0:T(8,128)(2,1)S(1)}, u32[]{:S(2)}, u32[]{:S(2)}) collective-permute-start(bf16[8,32,256]{2,1,0:T(8,128)(2,1)S(1)} %slice.42), channel_id=1, source_target_pairs={{0,3},{1,0},{2,1},{3,2},{4,7},{5,4},{6,5},{7,6},{8,11},{9,8},{10,9... | collective-permute-start | bytes 393224 | tf_op jit(solution)/shard_map/ppermute | solution.py:284
  70.7 0.1 collective-permute-start.24
  70.8 5.8 %collective-permute-done.12.refs_10_ = bf16[16,32,256]{2,1,0:T(8,128)(2,1)S(1)} collective-permute-done((bf16[16,32,256]{2,1,0:T(8,128)(2,1)}, bf16[16,32,256]{2,1,0:T(8,128)(2,1)S(1)}, u32[]{:S(2)}, u32[]{:S(2)}) %collective-permute-start.12) | collective-permute-done | bytes 262176 | tf_op jit(solution)/shard_map/ppermute | solution.py:279
  76.6 0.6 collective-permute-start.10
  77.2 2.6 %collective-permute-start.28 = (bf16[16,32,256]{2,1,0:T(8,128)(2,1)S(1)}, bf16[16,32,256]{2,1,0:T(8,128)(2,1)S(1)}, u32[]{:S(2)}, u32[]{:S(2)}) collective-permute-start(bf16[16,32,256]{2,1,0:T(8,128)(2,1)S(1)} %collective-permute-done.26.refs_25_), channel_id=1, source_target_pairs={{0,3},{1,0},{2,1},{3,2},{4,7},{5,4},{6,5},{7,6},{8,11},{9,8},{10,9... | collective-permute-start | bytes 786440 | tf_op jit(solution)/shard_map/ppermute | solution.py:284
  79.8 0.3 collective-permute-start.16
  80.1 1.2 %collective-permute-start.14 = (bf16[16,32,256]{2,1,0:T(8,128)(2,1)S(1)}, bf16[16,32,256]{2,1,0:T(8,128)(2,1)S(1)}, u32[]{:S(2)}, u32[]{:S(2)}) collective-permute-start(bf16[16,32,256]{2,1,0:T(8,128)(2,1)S(1)} %collective-permute-done.12.refs_10_), channel_id=1, source_target_pairs={{0,16},{8,24},{16,32},{24,40},{32,48},{40,56},{48,0},{56,8},{64,80... | collective-permute-start | bytes 786440 | tf_op jit(solution)/shard_map/ppermute | solution.py:279
  81.3 1.0 collective-permute-start.8
  82.3 3.5 %collective-permute-start.11 = (bf16[8,32,256]{2,1,0:T(8,128)(2,1)S(1)}, bf16[8,32,256]{2,1,0:T(8,128)(2,1)}, u32[]{:S(2)}, u32[]{:S(2)}) collective-permute-start(bf16[8,32,256]{2,1,0:T(8,128)(2,1)S(1)} %collective-permute-done.10.refs_8_), channel_id=1, source_target_pairs={{0,8},{8,0},{16,24},{24,16},{32,40},{40,32},{48,56},{56,48},{64,72... | collective-permute-start | bytes 393224 | tf_op jit(solution)/shard_map/ppermute | solution.py:279
  85.8 3.3 %collective-permute-done.8.refs_6_ = bf16[8,32,256]{2,1,0:T(8,128)(2,1)S(1)} collective-permute-done((bf16[8,32,256]{2,1,0:T(8,128)(2,1)S(1)}, bf16[8,32,256]{2,1,0:T(8,128)(2,1)S(1)}, u32[]{:S(2)}, u32[]{:S(2)}) %collective-permute-start.8) | collective-permute-done | bytes 131104 | tf_op jit(solution)/shard_map/ppermute | solution.py:279
  89.1 3.9 %collective-permute-start.13 = (bf16[16,32,256]{2,1,0:T(8,128)(2,1)S(1)}, bf16[16,32,256]{2,1,0:T(8,128)(2,1)S(1)}, u32[]{:S(2)}, u32[]{:S(2)}) collective-permute-start(bf16[16,32,256]{2,1,0:T(8,128)(2,1)S(1)} %collective-permute-done.12.refs_10_), channel_id=1, source_target_pairs={{0,8},{8,0},{16,24},{24,16},{32,40},{40,32},{48,56},{56,48},{64,72... | collective-permute-start | bytes 786440 | tf_op jit(solution)/shard_map/ppermute | solution.py:279
  93.0 0.1 collective-permute-start.7
  93.1 0.5 collective-permute-start.5
  93.6 0.3 collective-permute-start.9
  93.9 1.2 %collective-permute-done.9.refs_7_ = bf16[8,32,256]{2,1,0:T(8,128)(2,1)S(1)} collective-permute-done((bf16[8,32,256]{2,1,0:T(8,128)(2,1)S(1)}, bf16[8,32,256]{2,1,0:T(8,128)(2,1)S(1)}, u32[]{:S(2)}, u32[]{:S(2)}) %collective-permute-start.9) | collective-permute-done | bytes 131104 | tf_op jit(solution)/shard_map/ppermute | solution.py:279
  95.1 2.9 %collective-permute-start.30 = (bf16[8,32,256]{2,1,0:T(8,128)(2,1)S(1)}, bf16[8,32,256]{2,1,0:T(8,128)(2,1)S(1)}, u32[]{:S(2)}, u32[]{:S(2)}) collective-permute-start(bf16[8,32,256]{2,1,0:T(8,128)(2,1)S(1)} %slice.44), channel_id=1, source_target_pairs={{0,3},{1,0},{2,1},{3,2},{4,7},{5,4},{6,5},{7,6},{8,11},{9,8},{10,9... | collective-permute-start | bytes 393224 | tf_op jit(solution)/shard_map/ppermute | solution.py:284
  98.1 2.8 %collective-permute-start.17 = (bf16[16,32,256]{2,1,0:T(8,128)(2,1)S(1)}, bf16[16,32,256]{2,1,0:T(8,128)(2,1)S(1)}, u32[]{:S(2)}, u32[]{:S(2)}) collective-permute-start(bf16[16,32,256]{2,1,0:T(8,128)(2,1)S(1)} %collective-permute-done.16.refs_14_), channel_id=1, source_target_pairs={{0,8},{8,0},{16,24},{24,16},{32,40},{40,32},{48,56},{56,48},{64,72... | collective-permute-start | bytes 786440 | tf_op jit(solution)/shard_map/ppermute | solution.py:279
  100.8 0.1 collective-permute-start.15
  100.9 1.5 %collective-permute-start.18 = (bf16[8,32,256]{2,1,0:T(8,128)(2,1)S(1)}, bf16[8,32,256]{2,1,0:T(8,128)(2,1)S(1)}, u32[]{:S(2)}, u32[]{:S(2)}) collective-permute-start(bf16[8,32,256]{2,1,0:T(8,128)(2,1)S(1)} %slice.38), channel_id=1, source_target_pairs={{0,16},{8,24},{16,32},{24,40},{32,48},{40,56},{48,0},{56,8},{64,80... | collective-permute-start | bytes 393224 | tf_op jit(solution)/shard_map/ppermute | solution.py:279
  102.4 0.1 collective-permute-start.29
  102.5 2.9 %collective-permute-start.21 = (bf16[8,32,256]{2,1,0:T(8,128)(2,1)S(1)}, bf16[8,32,256]{2,1,0:T(8,128)(2,1)S(1)}, u32[]{:S(2)}, u32[]{:S(2)}) collective-permute-start(bf16[8,32,256]{2,1,0:T(8,128)(2,1)S(1)} %collective-permute-done.20.refs_18_), channel_id=1, source_target_pairs={{0,8},{8,0},{16,24},{24,16},{32,40},{40,32},{48,56},{56,48},{64,72... | collective-permute-start | bytes 393224 | tf_op jit(solution)/shard_map/ppermute | solution.py:279
  105.4 1.4 %collective-permute-done.18.refs_16_ = bf16[8,32,256]{2,1,0:T(8,128)(2,1)S(1)} collective-permute-done((bf16[8,32,256]{2,1,0:T(8,128)(2,1)S(1)}, bf16[8,32,256]{2,1,0:T(8,128)(2,1)S(1)}, u32[]{:S(2)}, u32[]{:S(2)}) %collective-permute-start.18) | collective-permute-done | bytes 131104 | tf_op jit(solution)/shard_map/ppermute | solution.py:279
  106.8 1.3 %collective-permute-start.19 = (bf16[8,32,256]{2,1,0:T(8,128)(2,1)S(1)}, bf16[8,32,256]{2,1,0:T(8,128)(2,1)}, u32[]{:S(2)}, u32[]{:S(2)}) collective-permute-start(bf16[8,32,256]{2,1,0:T(8,128)(2,1)S(1)} %collective-permute-done.18.refs_16_), channel_id=1, source_target_pairs={{0,8},{8,0},{16,24},{24,16},{32,40},{40,32},{48,56},{56,48},{64,72... | collective-permute-start | bytes 393224 | tf_op jit(solution)/shard_map/ppermute | solution.py:279
  108.1 0.0 collective-permute-done.29.refs_28_
  108.2 0.6 copy-done.26
  108.7 0.1 copy-done.16
  108.8 0.1 copy-done.17
  108.9 0.7 copy-done.27
  109.7 5.1 %weight_gradient.1 = (bf16[512,256]{1,0:T(8,128)(2,1)}, f32[256,512]{1,0:T(8,128)}) custom-call(bf16[16,32,256]{2,1,0:T(8,128)(2,1)} %shard_map.122.refs_0_, bf16[16,32,256]{2,1,0:T(8,128)(2,1)} %copy-done.12, bf16[16,32,256]{2,1,0:T(8,128)(2,1)} %copy-done.5, bf16[16,32,256]{2,1,0:T(8,128)(2,1)} %copy-done.15, bf16[16,32,256]{2,1,0:T(8,128)(2,1)} %copy-done.4, ...), custom_call_target="tpu_custom_call" | custom-call | flops 1000000000 | bytes 7000000 | tf_op jit(solution)/shard_map/weight_gradient/pallas_call | solution.py:357
  (95 shorter events, 0.3 us)
Async XLA Ops:
  2.9 26.4 %all-to-all-start = ((bf16[16,128,256]{2,1,0:T(8,128)(2,1)}), bf16[16,128,256]{2,1,0:T(8,128)(2,1)S(1)}, u32[]{:S(2)}, u32[]{:S(2)}) async-start(bf16[16,128,256]{2,1,0:T(8,128)(2,1)} %get-tuple-element.4), calls=%async_computation | async-start | bytes 2097152 | tf_op jit(solution)/shard_map/all_to_all | solution.py:369
  12.0 8.1 %collective-permute-start = (f32[8,256]{1,0:T(8,128)S(1)}, f32[8,256]{1,0:T(8,128)S(1)}, u32[]{:S(2)}, u32[]{:S(2)}) collective-permute-start(f32[8,256]{1,0:T(8,128)S(1)} %copy-done.29), channel_id=1, source_target_pairs={{0,4},{1,5},{2,6},{3,7},{4,0},{5,1},{6,2},{7,3},{8,12},{9,13},{10,... | collective-permute-start | bytes 24584 | tf_op jit(solution)/shard_map/ppermute | solution.py:284
  20.2 4.1 %collective-permute-start.1 = (f32[8,256]{1,0:T(8,128)S(1)}, f32[8,256]{1,0:T(8,128)S(1)}, u32[]{:S(2)}, u32[]{:S(2)}) collective-permute-start(f32[8,256]{1,0:T(8,128)S(1)} %add.9), channel_id=1, source_target_pairs={{0,1},{1,2},{2,3},{3,0},{4,5},{5,6},{6,7},{7,4},{8,9},{9,10},{10,1... | collective-permute-start | bytes 24584 | tf_op jit(solution)/shard_map/ppermute | solution.py:284
  24.2 4.3 %collective-permute-start.2 = (f32[8,256]{1,0:T(8,128)S(1)}, f32[8,256]{1,0:T(8,128)S(1)}, u32[]{:S(2)}, u32[]{:S(2)}) collective-permute-start(f32[8,256]{1,0:T(8,128)S(1)} %add.10), channel_id=1, source_target_pairs={{0,2},{1,3},{2,0},{3,1},{4,6},{5,7},{6,4},{7,5},{8,10},{9,11},{10,... | collective-permute-start | bytes 24584 | tf_op jit(solution)/shard_map/ppermute | solution.py:284
  29.3 16.5 %copy-start = (bf16[16,128,256]{2,1,0:T(8,128)(2,1)}, bf16[16,128,256]{2,1,0:T(8,128)(2,1)S(1)}, u32[]{:S(2)}) copy-start(bf16[16,128,256]{2,1,0:T(8,128)(2,1)S(1)} %all-to-all-done.got_ref) | copy-start | bytes 3145732
  30.0 23.7 %all-to-all-start.1 = ((f32[16,8,256]{2,1,0:T(8,128)}), f32[16,8,256]{2,1,0:T(8,128)S(1)}, u32[]{:S(2)}, u32[]{:S(2)}) async-start(f32[16,8,256]{2,1,0:T(8,128)} %broadcast_in_dim.9), calls=%async_computation.1 | async-start | bytes 262144 | tf_op jit(solution)/shard_map/all_to_all | solution.py:369
  44.2 18.8 %copy-start.1 = (bf16[16,32,256]{2,1,0:T(8,128)(2,1)}, bf16[16,32,256]{2,1,0:T(8,128)(2,1)S(1)}, u32[]{:S(2)}) copy-start(bf16[16,32,256]{2,1,0:T(8,128)(2,1)S(1)} %slice.40.refs_20_) | copy-start | bytes 786436
  44.2 21.6 %collective-permute-start.23 = (bf16[16,32,256]{2,1,0:T(8,128)(2,1)S(1)}, bf16[16,32,256]{2,1,0:T(8,128)(2,1)S(1)}, u32[]{:S(2)}, u32[]{:S(2)}) collective-permute-start(bf16[16,32,256]{2,1,0:T(8,128)(2,1)S(1)} %slice.40.refs_20_), channel_id=1, source_target_pairs={{0,3},{1,0},{2,1},{3,2},{4,7},{5,4},{6,5},{7,6},{8,11},{9,8},{10,9... | collective-permute-start | bytes 786440 | tf_op jit(solution)/shard_map/ppermute | solution.py:284
  45.8 20.0 %collective-permute-start.22 = (bf16[16,32,256]{2,1,0:T(8,128)(2,1)S(1)}, bf16[16,32,256]{2,1,0:T(8,128)(2,1)S(1)}, u32[]{:S(2)}, u32[]{:S(2)}) collective-permute-start(bf16[16,32,256]{2,1,0:T(8,128)(2,1)S(1)} %slice.40.refs_20_), channel_id=1, source_target_pairs={{0,1},{1,2},{2,3},{3,0},{4,5},{5,6},{6,7},{7,4},{8,9},{9,10},{10,1... | collective-permute-start | bytes 786440 | tf_op jit(solution)/shard_map/ppermute | solution.py:284
  60.4 7.7 %collective-permute-start.6 = (bf16[16,32,256]{2,1,0:T(8,128)(2,1)}, bf16[16,32,256]{2,1,0:T(8,128)(2,1)S(1)}, u32[]{:S(2)}, u32[]{:S(2)}) collective-permute-start(bf16[16,32,256]{2,1,0:T(8,128)(2,1)} %shard_map.122.refs_0_), channel_id=1, source_target_pairs={{0,48},{8,56},{16,0},{24,8},{32,16},{40,24},{48,32},{56,40},{64,11... | collective-permute-start | bytes 786440 | tf_op jit(solution)/shard_map/ppermute | solution.py:279
  63.0 7.7 %collective-permute-start.26 = (bf16[16,32,256]{2,1,0:T(8,128)(2,1)S(1)}, bf16[16,32,256]{2,1,0:T(8,128)(2,1)S(1)}, u32[]{:S(2)}, u32[]{:S(2)}) collective-permute-start(bf16[16,32,256]{2,1,0:T(8,128)(2,1)S(1)} %slice.40.refs_20_), channel_id=1, source_target_pairs={{0,4},{1,5},{2,6},{3,7},{4,0},{5,1},{6,2},{7,3},{8,12},{9,13},{10,... | collective-permute-start | bytes 786440 | tf_op jit(solution)/shard_map/ppermute | solution.py:284
  63.0 13.7 %collective-permute-start.12 = (bf16[16,32,256]{2,1,0:T(8,128)(2,1)}, bf16[16,32,256]{2,1,0:T(8,128)(2,1)S(1)}, u32[]{:S(2)}, u32[]{:S(2)}) collective-permute-start(bf16[16,32,256]{2,1,0:T(8,128)(2,1)} %shard_map.122.refs_0_), channel_id=1, source_target_pairs={{0,64},{8,72},{16,80},{24,88},{32,96},{40,104},{48,112},{56,120},{... | collective-permute-start | bytes 786440 | tf_op jit(solution)/shard_map/ppermute | solution.py:279
  65.8 43.8 %copy-start.2 = (bf16[16,32,256]{2,1,0:T(8,128)(2,1)}, bf16[16,32,256]{2,1,0:T(8,128)(2,1)S(1)}, u32[]{:S(2)}) copy-start(bf16[16,32,256]{2,1,0:T(8,128)(2,1)S(1)} %collective-permute-done.23.refs_22_) | copy-start | bytes 786436
  65.8 11.4 %collective-permute-start.4 = (bf16[16,32,256]{2,1,0:T(8,128)(2,1)}, bf16[16,32,256]{2,1,0:T(8,128)(2,1)S(1)}, u32[]{:S(2)}, u32[]{:S(2)}) collective-permute-start(bf16[16,32,256]{2,1,0:T(8,128)(2,1)} %shard_map.122.refs_0_), channel_id=1, source_target_pairs={{0,16},{8,24},{16,32},{24,40},{32,48},{40,56},{48,0},{56,8},{64,80... | collective-permute-start | bytes 786440 | tf_op jit(solution)/shard_map/ppermute | solution.py:279
  65.8 43.8 %copy-start.3 = (bf16[16,32,256]{2,1,0:T(8,128)(2,1)}, bf16[16,32,256]{2,1,0:T(8,128)(2,1)S(1)}, u32[]{:S(2)}) copy-start(bf16[16,32,256]{2,1,0:T(8,128)(2,1)S(1)} %collective-permute-done.22.refs_21_) | copy-start | bytes 786436
  65.8 14.0 %collective-permute-start.3 = (bf16[16,32,256]{2,1,0:T(8,128)(2,1)}, bf16[16,32,256]{2,1,0:T(8,128)(2,1)S(1)}, u32[]{:S(2)}, u32[]{:S(2)}) collective-permute-start(bf16[16,32,256]{2,1,0:T(8,128)(2,1)} %shard_map.122.refs_0_), channel_id=1, source_target_pairs={{0,8},{8,0},{16,24},{24,16},{32,40},{40,32},{48,56},{56,48},{64,72... | collective-permute-start | bytes 786440 | tf_op jit(solution)/shard_map/ppermute | solution.py:279
  68.1 41.5 %copy-start.4 = (bf16[16,32,256]{2,1,0:T(8,128)(2,1)}, bf16[16,32,256]{2,1,0:T(8,128)(2,1)S(1)}, u32[]{:S(2)}) copy-start(bf16[16,32,256]{2,1,0:T(8,128)(2,1)S(1)} %collective-permute-done.6.refs_4_) | copy-start | bytes 786436
  68.1 12.1 %collective-permute-start.25 = (bf16[8,32,256]{2,1,0:T(8,128)(2,1)S(1)}, bf16[8,32,256]{2,1,0:T(8,128)(2,1)S(1)}, u32[]{:S(2)}, u32[]{:S(2)}) collective-permute-start(bf16[8,32,256]{2,1,0:T(8,128)(2,1)S(1)} %slice.42), channel_id=1, source_target_pairs={{0,3},{1,0},{2,1},{3,2},{4,7},{5,4},{6,5},{7,6},{8,11},{9,8},{10,9... | collective-permute-start | bytes 393224 | tf_op jit(solution)/shard_map/ppermute | solution.py:284
  70.7 38.9 %copy-start.10 = (bf16[16,32,256]{2,1,0:T(8,128)(2,1)}, bf16[16,32,256]{2,1,0:T(8,128)(2,1)S(1)}, u32[]{:S(2)}) copy-start(bf16[16,32,256]{2,1,0:T(8,128)(2,1)S(1)} %collective-permute-done.26.refs_25_) | copy-start | bytes 786436
  70.7 10.6 %collective-permute-start.24 = (bf16[8,32,256]{2,1,0:T(8,128)(2,1)S(1)}, bf16[8,32,256]{2,1,0:T(8,128)(2,1)S(1)}, u32[]{:S(2)}, u32[]{:S(2)}) collective-permute-start(bf16[8,32,256]{2,1,0:T(8,128)(2,1)S(1)} %slice.41), channel_id=1, source_target_pairs={{0,1},{1,2},{2,3},{3,0},{4,5},{5,6},{6,7},{7,4},{8,9},{9,10},{10,1... | collective-permute-start | bytes 393224 | tf_op jit(solution)/shard_map/ppermute | solution.py:284
  76.6 33.0 %copy-start.11 = (bf16[16,32,256]{2,1,0:T(8,128)(2,1)}, bf16[16,32,256]{2,1,0:T(8,128)(2,1)S(1)}, u32[]{:S(2)}) copy-start(bf16[16,32,256]{2,1,0:T(8,128)(2,1)S(1)} %collective-permute-done.12.refs_10_) | copy-start | bytes 786436
  76.6 5.7 %collective-permute-start.10 = (bf16[8,32,256]{2,1,0:T(8,128)(2,1)S(1)}, bf16[8,32,256]{2,1,0:T(8,128)(2,1)S(1)}, u32[]{:S(2)}, u32[]{:S(2)}) collective-permute-start(bf16[8,32,256]{2,1,0:T(8,128)(2,1)S(1)} %slice.37), channel_id=1, source_target_pairs={{0,48},{8,56},{16,0},{24,8},{32,16},{40,24},{48,32},{56,40},{64,11... | collective-permute-start | bytes 393224 | tf_op jit(solution)/shard_map/ppermute | solution.py:279
  77.2 32.4 %copy-start.5 = (bf16[16,32,256]{2,1,0:T(8,128)(2,1)}, bf16[16,32,256]{2,1,0:T(8,128)(2,1)S(1)}, u32[]{:S(2)}) copy-start(bf16[16,32,256]{2,1,0:T(8,128)(2,1)S(1)} %collective-permute-done.4.refs_2_) | copy-start | bytes 786436
  77.2 15.7 %collective-permute-start.28 = (bf16[16,32,256]{2,1,0:T(8,128)(2,1)S(1)}, bf16[16,32,256]{2,1,0:T(8,128)(2,1)S(1)}, u32[]{:S(2)}, u32[]{:S(2)}) collective-permute-start(bf16[16,32,256]{2,1,0:T(8,128)(2,1)S(1)} %collective-permute-done.26.refs_25_), channel_id=1, source_target_pairs={{0,3},{1,0},{2,1},{3,2},{4,7},{5,4},{6,5},{7,6},{8,11},{9,8},{10,9... | collective-permute-start | bytes 786440 | tf_op jit(solution)/shard_map/ppermute | solution.py:284
  79.8 29.8 %copy-start.12 = (bf16[16,32,256]{2,1,0:T(8,128)(2,1)}, bf16[16,32,256]{2,1,0:T(8,128)(2,1)S(1)}, u32[]{:S(2)}) copy-start(bf16[16,32,256]{2,1,0:T(8,128)(2,1)S(1)} %collective-permute-done.3.refs_1_) | copy-start | bytes 786436
  79.8 13.3 %collective-permute-start.16 = (bf16[16,32,256]{2,1,0:T(8,128)(2,1)S(1)}, bf16[16,32,256]{2,1,0:T(8,128)(2,1)S(1)}, u32[]{:S(2)}, u32[]{:S(2)}) collective-permute-start(bf16[16,32,256]{2,1,0:T(8,128)(2,1)S(1)} %collective-permute-done.12.refs_10_), channel_id=1, source_target_pairs={{0,48},{8,56},{16,0},{24,8},{32,16},{40,24},{48,32},{56,40},{64,11... | collective-permute-start | bytes 786440 | tf_op jit(solution)/shard_map/ppermute | solution.py:279
  80.1 29.5 %copy-start.18 = (bf16[8,32,256]{2,1,0:T(8,128)(2,1)}, bf16[8,32,256]{2,1,0:T(8,128)(2,1)S(1)}, u32[]{:S(2)}) copy-start(bf16[8,32,256]{2,1,0:T(8,128)(2,1)S(1)} %collective-permute-done.25.refs_24_) | copy-start | bytes 393220
  80.1 13.5 %collective-permute-start.14 = (bf16[16,32,256]{2,1,0:T(8,128)(2,1)S(1)}, bf16[16,32,256]{2,1,0:T(8,128)(2,1)S(1)}, u32[]{:S(2)}, u32[]{:S(2)}) collective-permute-start(bf16[16,32,256]{2,1,0:T(8,128)(2,1)S(1)} %collective-permute-done.12.refs_10_), channel_id=1, source_target_pairs={{0,16},{8,24},{16,32},{24,40},{32,48},{40,56},{48,0},{56,8},{64,80... | collective-permute-start | bytes 786440 | tf_op jit(solution)/shard_map/ppermute | solution.py:279
  81.3 7.7 %collective-permute-start.8 = (bf16[8,32,256]{2,1,0:T(8,128)(2,1)S(1)}, bf16[8,32,256]{2,1,0:T(8,128)(2,1)S(1)}, u32[]{:S(2)}, u32[]{:S(2)}) collective-permute-start(bf16[8,32,256]{2,1,0:T(8,128)(2,1)S(1)} %slice.36), channel_id=1, source_target_pairs={{0,16},{8,24},{16,32},{24,40},{32,48},{40,56},{48,0},{56,8},{64,80... | collective-permute-start | bytes 393224 | tf_op jit(solution)/shard_map/ppermute | solution.py:279
  82.3 6.8 %collective-permute-start.11 = (bf16[8,32,256]{2,1,0:T(8,128)(2,1)S(1)}, bf16[8,32,256]{2,1,0:T(8,128)(2,1)}, u32[]{:S(2)}, u32[]{:S(2)}) collective-permute-start(bf16[8,32,256]{2,1,0:T(8,128)(2,1)S(1)} %collective-permute-done.10.refs_8_), channel_id=1, source_target_pairs={{0,8},{8,0},{16,24},{24,16},{32,40},{40,32},{48,56},{56,48},{64,72... | collective-permute-start | bytes 393224 | tf_op jit(solution)/shard_map/ppermute | solution.py:279
  89.1 9.0 %collective-permute-start.27 = (bf16[16,32,256]{2,1,0:T(8,128)(2,1)S(1)}, bf16[16,32,256]{2,1,0:T(8,128)(2,1)S(1)}, u32[]{:S(2)}, u32[]{:S(2)}) collective-permute-start(bf16[16,32,256]{2,1,0:T(8,128)(2,1)S(1)} %collective-permute-done.26.refs_25_), channel_id=1, source_target_pairs={{0,1},{1,2},{2,3},{3,0},{4,5},{5,6},{6,7},{7,4},{8,9},{9,10},{10,1... | collective-permute-start | bytes 786440 | tf_op jit(solution)/shard_map/ppermute | solution.py:284
  89.1 9.0 %collective-permute-start.13 = (bf16[16,32,256]{2,1,0:T(8,128)(2,1)S(1)}, bf16[16,32,256]{2,1,0:T(8,128)(2,1)S(1)}, u32[]{:S(2)}, u32[]{:S(2)}) collective-permute-start(bf16[16,32,256]{2,1,0:T(8,128)(2,1)S(1)} %collective-permute-done.12.refs_10_), channel_id=1, source_target_pairs={{0,8},{8,0},{16,24},{24,16},{32,40},{40,32},{48,56},{56,48},{64,72... | collective-permute-start | bytes 786440 | tf_op jit(solution)/shard_map/ppermute | solution.py:279
  93.0 16.7 %copy-start.6 = (bf16[16,32,256]{2,1,0:T(8,128)(2,1)}, bf16[16,32,256]{2,1,0:T(8,128)(2,1)S(1)}, u32[]{:S(2)}) copy-start(bf16[16,32,256]{2,1,0:T(8,128)(2,1)S(1)} %collective-permute-done.28.refs_27_) | copy-start | bytes 786436
  93.0 7.9 %collective-permute-start.7 = (bf16[16,32,256]{2,1,0:T(8,128)(2,1)S(1)}, bf16[16,32,256]{2,1,0:T(8,128)(2,1)S(1)}, u32[]{:S(2)}, u32[]{:S(2)}) collective-permute-start(bf16[16,32,256]{2,1,0:T(8,128)(2,1)S(1)} %collective-permute-done.6.refs_4_), channel_id=1, source_target_pairs={{0,8},{8,0},{16,24},{24,16},{32,40},{40,32},{48,56},{56,48},{64,72... | collective-permute-start | bytes 786440 | tf_op jit(solution)/shard_map/ppermute | solution.py:279
  93.1 16.6 %copy-start.7 = (bf16[16,32,256]{2,1,0:T(8,128)(2,1)}, bf16[16,32,256]{2,1,0:T(8,128)(2,1)S(1)}, u32[]{:S(2)}) copy-start(bf16[16,32,256]{2,1,0:T(8,128)(2,1)S(1)} %collective-permute-done.16.refs_14_) | copy-start | bytes 786436
  93.1 7.9 %collective-permute-start.5 = (bf16[16,32,256]{2,1,0:T(8,128)(2,1)S(1)}, bf16[16,32,256]{2,1,0:T(8,128)(2,1)S(1)}, u32[]{:S(2)}, u32[]{:S(2)}) collective-permute-start(bf16[16,32,256]{2,1,0:T(8,128)(2,1)S(1)} %collective-permute-done.4.refs_2_), channel_id=1, source_target_pairs={{0,8},{8,0},{16,24},{24,16},{32,40},{40,32},{48,56},{56,48},{64,72... | collective-permute-start | bytes 786440 | tf_op jit(solution)/shard_map/ppermute | solution.py:279
  93.6 16.1 %copy-start.8 = (bf16[16,32,256]{2,1,0:T(8,128)(2,1)}, bf16[16,32,256]{2,1,0:T(8,128)(2,1)S(1)}, u32[]{:S(2)}) copy-start(bf16[16,32,256]{2,1,0:T(8,128)(2,1)S(1)} %collective-permute-done.14.refs_12_) | copy-start | bytes 786436
  93.6 1.6 %collective-permute-start.9 = (bf16[8,32,256]{2,1,0:T(8,128)(2,1)S(1)}, bf16[8,32,256]{2,1,0:T(8,128)(2,1)S(1)}, u32[]{:S(2)}, u32[]{:S(2)}) collective-permute-start(bf16[8,32,256]{2,1,0:T(8,128)(2,1)S(1)} %collective-permute-done.8.refs_6_), channel_id=1, source_target_pairs={{0,8},{8,0},{16,24},{24,16},{32,40},{40,32},{48,56},{56,48},{64,72... | collective-permute-start | bytes 393224 | tf_op jit(solution)/shard_map/ppermute | solution.py:279
  95.1 7.3 %collective-permute-start.30 = (bf16[8,32,256]{2,1,0:T(8,128)(2,1)S(1)}, bf16[8,32,256]{2,1,0:T(8,128)(2,1)S(1)}, u32[]{:S(2)}, u32[]{:S(2)}) collective-permute-start(bf16[8,32,256]{2,1,0:T(8,128)(2,1)S(1)} %slice.44), channel_id=1, source_target_pairs={{0,3},{1,0},{2,1},{3,2},{4,7},{5,4},{6,5},{7,6},{8,11},{9,8},{10,9... | collective-permute-start | bytes 393224 | tf_op jit(solution)/shard_map/ppermute | solution.py:284
  98.0 11.7 %copy-start.9 = (bf16[16,32,256]{2,1,0:T(8,128)(2,1)}, bf16[16,32,256]{2,1,0:T(8,128)(2,1)S(1)}, u32[]{:S(2)}) copy-start(bf16[16,32,256]{2,1,0:T(8,128)(2,1)S(1)} %collective-permute-done.27.refs_26_) | copy-start | bytes 786436
  98.0 4.5 %collective-permute-start.20 = (bf16[8,32,256]{2,1,0:T(8,128)(2,1)S(1)}, bf16[8,32,256]{2,1,0:T(8,128)(2,1)S(1)}, u32[]{:S(2)}, u32[]{:S(2)}) collective-permute-start(bf16[8,32,256]{2,1,0:T(8,128)(2,1)S(1)} %slice.39), channel_id=1, source_target_pairs={{0,48},{8,56},{16,0},{24,8},{32,16},{40,24},{48,32},{56,40},{64,11... | collective-permute-start | bytes 393224 | tf_op jit(solution)/shard_map/ppermute | solution.py:279
  98.1 11.6 %copy-start.13 = (bf16[16,32,256]{2,1,0:T(8,128)(2,1)}, bf16[16,32,256]{2,1,0:T(8,128)(2,1)S(1)}, u32[]{:S(2)}) copy-start(bf16[16,32,256]{2,1,0:T(8,128)(2,1)S(1)} %collective-permute-done.13.refs_11_) | copy-start | bytes 786436
  98.1 10.0 %collective-permute-start.17 = (bf16[16,32,256]{2,1,0:T(8,128)(2,1)S(1)}, bf16[16,32,256]{2,1,0:T(8,128)(2,1)S(1)}, u32[]{:S(2)}, u32[]{:S(2)}) collective-permute-start(bf16[16,32,256]{2,1,0:T(8,128)(2,1)S(1)} %collective-permute-done.16.refs_14_), channel_id=1, source_target_pairs={{0,8},{8,0},{16,24},{24,16},{32,40},{40,32},{48,56},{56,48},{64,72... | collective-permute-start | bytes 786440 | tf_op jit(solution)/shard_map/ppermute | solution.py:279
  100.8 7.3 %collective-permute-start.15 = (bf16[16,32,256]{2,1,0:T(8,128)(2,1)S(1)}, bf16[16,32,256]{2,1,0:T(8,128)(2,1)S(1)}, u32[]{:S(2)}, u32[]{:S(2)}) collective-permute-start(bf16[16,32,256]{2,1,0:T(8,128)(2,1)S(1)} %collective-permute-done.14.refs_12_), channel_id=1, source_target_pairs={{0,8},{8,0},{16,24},{24,16},{32,40},{40,32},{48,56},{56,48},{64,72... | collective-permute-start | bytes 786440 | tf_op jit(solution)/shard_map/ppermute | solution.py:279
  100.9 5.9 %collective-permute-start.18 = (bf16[8,32,256]{2,1,0:T(8,128)(2,1)S(1)}, bf16[8,32,256]{2,1,0:T(8,128)(2,1)S(1)}, u32[]{:S(2)}, u32[]{:S(2)}) collective-permute-start(bf16[8,32,256]{2,1,0:T(8,128)(2,1)S(1)} %slice.38), channel_id=1, source_target_pairs={{0,16},{8,24},{16,32},{24,40},{32,48},{40,56},{48,0},{56,8},{64,80... | collective-permute-start | bytes 393224 | tf_op jit(solution)/shard_map/ppermute | solution.py:279
  102.4 5.7 %collective-permute-start.29 = (bf16[8,32,256]{2,1,0:T(8,128)(2,1)S(1)}, bf16[8,32,256]{2,1,0:T(8,128)(2,1)S(1)}, u32[]{:S(2)}, u32[]{:S(2)}) collective-permute-start(bf16[8,32,256]{2,1,0:T(8,128)(2,1)S(1)} %slice.43), channel_id=1, source_target_pairs={{0,1},{1,2},{2,3},{3,0},{4,5},{5,6},{6,7},{7,4},{8,9},{9,10},{10,1... | collective-permute-start | bytes 393224 | tf_op jit(solution)/shard_map/ppermute | solution.py:284
  102.5 5.6 %collective-permute-start.21 = (bf16[8,32,256]{2,1,0:T(8,128)(2,1)S(1)}, bf16[8,32,256]{2,1,0:T(8,128)(2,1)S(1)}, u32[]{:S(2)}, u32[]{:S(2)}) collective-permute-start(bf16[8,32,256]{2,1,0:T(8,128)(2,1)S(1)} %collective-permute-done.20.refs_18_), channel_id=1, source_target_pairs={{0,8},{8,0},{16,24},{24,16},{32,40},{40,32},{48,56},{56,48},{64,72... | collective-permute-start | bytes 393224 | tf_op jit(solution)/shard_map/ppermute | solution.py:279
  106.8 2.8 %collective-permute-start.19 = (bf16[8,32,256]{2,1,0:T(8,128)(2,1)S(1)}, bf16[8,32,256]{2,1,0:T(8,128)(2,1)}, u32[]{:S(2)}, u32[]{:S(2)}) collective-permute-start(bf16[8,32,256]{2,1,0:T(8,128)(2,1)S(1)} %collective-permute-done.18.refs_16_), channel_id=1, source_target_pairs={{0,8},{8,0},{16,24},{24,16},{32,40},{40,32},{48,56},{56,48},{64,72... | collective-permute-start | bytes 393224 | tf_op jit(solution)/shard_map/ppermute | solution.py:279
  (15 other events, 75.5 us)
where the time goes:
time: 116 us; the launch traced here: 115 us
  starting transfers between devices  63.8 us (55%)
  waiting for transfers between devices  25.7 us (22%)
  Pallas kernels  21.3 us (18%)
  local copies, waits for them, and re-layouts  2.97 us (3%)
  between operations  1.2 us (1%)
    ppermute x19, starting transfers between devices, over_seq(): return lax.ppermute(value, 'seq', pairs)  26.9 us
    all_to_all x2, starting transfers between devices, exchange(): return lax.all_to_all(value, axis, split_axis=0, concat_axis=0, tiled=True)  23.3 us
    ppermute x12, starting transfers between devices, over_chan(): return lax.ppermute(value, 'chan', pairs)  13.6 us
    ppermute x12, waiting for transfers between devices, over_chan(): return lax.ppermute(value, 'chan', pairs)  12.8 us
    ppermute x19, waiting for transfers between devices, over_seq(): return lax.ppermute(value, 'seq', pairs)  12.2 us
    pallas_call x1, Pallas kernels, filter_spectrum(): pl.pallas_call(filter_kernel, out_shape=jax.ShapeDtypeStruct((OUTER, 32,...  7.88 us
    pallas_call x1, Pallas kernels, gated_convolution(): pl.pallas_call(signal_kernel, out_shape=jax.ShapeDtypeStruct((16, 32, 256...  6.04 us
    pallas_call x1, Pallas kernels, weight_gradient(): pl.pallas_call(functools.partial(grad_kernel, mixed_keys, up_keys), out_s...  5.11 us
  transfers between devices with their start and end apart: 33, of which 9 were waited for; matrix products, arithmetic and copies ran while one was open for 0% of the time, Pallas kernels for 12%

commit v1 on v0

--- a/solution.py
+++ b/solution.py
@@ -31,7 +31,7 @@
         upper = table.astype(BF16)
         lower = (table - upper.astype(np.float64)).astype(BF16)
         parts.append(np.concatenate([upper, lower, upper]))
-    return [np.cos(turn).astype(np.float32), -np.sin(turn).astype(np.float32), *parts]
+    return [np.stack([np.cos(turn), -np.sin(turn)]).astype(np.float32), np.stack(parts)]
 
 
 def turned(value, step, total, sign):
@@ -146,14 +146,20 @@
     return jnp.sum(jnp.where(lane == wanted, row_ref[...], 0.0), axis=1, keepdims=True)
 
 
-def filter_kernel(got_ref, taps_ref, bias_ref, twr_ref, twi_ref, ahead, back, spec_ref, time_ref, mid_ref, half_ref):
+def filter_kernel(
+    got_ref, taps_ref, bias_ref, turn_hbm, inner_hbm, spec_ref, time_ref, mid_ref, half_ref, turn_ref, inner_ref, sems
+):
+    turn_copy, inner_copy = fetch((turn_hbm, inner_hbm), (turn_ref, inner_ref), sems)
+    twr_ref, twi_ref, ahead, back = turn_ref.at[0], turn_ref.at[1], inner_ref.at[0], inner_ref.at[1]
     first = pl.multiple_of(lax.axis_index("seq") * 32, 32)
     bias = column_of(bias_ref, first)
     own_taps = taps_ref[pl.ds(first, 32), :]
     for b in range(16):
         for h in range(2):
-            time_ref[2 * b + h] = got_ref[b, 32:64, h * INNER : (h + 1) * INNER].astype(F32)
+            time_ref[2 * b + h] = got_ref[b, 0:32, h * INNER : (h + 1) * INNER].astype(F32)
+    turn_copy.wait()
     outer_ahead(time_ref, mid_ref, half_ref, twr_ref, twi_ref)
+    inner_copy.wait()
 
     def combine(ks):
         long = product(flat(mid_ref[ks]), ahead)
@@ -175,17 +181,29 @@
 
 
 def signal_kernel(
-    got_ref, squares_ref, gain_ref, spec_ref, twr_ref, twi_ref, ahead, back, mixed_ref, time_ref, mid_ref, half_ref
+    normed_ref,
+    got_ref,
+    spec_any,
+    turn_hbm,
+    inner_hbm,
+    mixed_ref,
+    time_ref,
+    mid_ref,
+    half_ref,
+    turn_ref,
+    inner_ref,
+    sems,
+    spec_ref,
 ):
-    first = lax.axis_index("seq") * 32
-    gain = jnp.broadcast_to(column_of(gain_ref, first), (32, INNER))
+    copies = fetch((turn_hbm, inner_hbm, spec_any), (turn_ref, inner_ref, spec_ref), sems)
+    twr_ref, twi_ref, ahead, back = turn_ref.at[0], turn_ref.at[1], inner_ref.at[0], inner_ref.at[1]
     for b in range(16):
-        scale = lax.rsqrt(jnp.sum(squares_ref[b], axis=0, keepdims=True) / D + EPSILON)
         for h in range(2):
-            cols = slice(h * INNER, (h + 1) * INNER)
-            normed = got_ref[b, 0:32, cols].astype(F32) * scale[:, cols] * gain
-            time_ref[2 * b + h] = normed.astype(BF16).astype(F32)
+            time_ref[2 * b + h] = normed_ref[b, :, h * INNER : (h + 1) * INNER].astype(F32)
+    copies[0].wait()
     outer_ahead(time_ref, mid_ref, half_ref, twr_ref, twi_ref)
+    copies[1].wait()
+    copies[2].wait()
 
     def combine(ks):
         spec = product(flat(mid_ref[ks]), ahead)
@@ -198,17 +216,35 @@
         for h in range(2):
             cols = slice(h * INNER, (h + 1) * INNER)
             long_out = time_ref[2 * b + h].astype(BF16).astype(F32)
-            mixed_ref[b, :, cols] = (got_ref[b, 64:96, cols].astype(F32) * long_out).astype(BF16)
+            mixed_ref[b, :, cols] = (got_ref[b, 32:64, cols].astype(F32) * long_out).astype(BF16)
 
 
 def vmem(count):
     return [pl.BlockSpec(memory_space=pltpu.VMEM)] * count
+
+
+def hbm(count):
+    return [pl.BlockSpec(memory_space=pltpu.HBM)] * count
+
+
+def stay(value):
+    return pltpu.with_memory_space_constraint(value, pltpu.HBM)
+
+
+def fetch(sources, targets, sems):
+    copies = [pltpu.make_async_copy(source, target, sems.at[i]) for i, (source, target) in enumerate(zip(sources, targets))]
+    for copy in copies:
+        copy.start()
+    return copies
 
 
 SCRATCH = [
     pltpu.VMEM((OUTER, 32, INNER), F32),
     pltpu.VMEM((OUTER, 32, 2 * INNER), F32),
     pltpu.VMEM((4, 4, 8, 2, 8, INNER), F32),
+    pltpu.VMEM((2, OUTER, INNER), F32),
+    pltpu.VMEM((2, 6 * INNER, 2 * INNER), BF16),
+    pltpu.SemaphoreType.DMA((3,)),
 ]
 
 
@@ -216,38 +252,39 @@
     return pl.pallas_call(
         filter_kernel,
         out_shape=jax.ShapeDtypeStruct((OUTER, 32, 2 * INNER), F32),
-        in_specs=vmem(7),
+        in_specs=vmem(3) + hbm(2),
         out_specs=vmem(1)[0],
         scratch_shapes=SCRATCH,
         cost_estimate=pl.CostEstimate(flops=2_000_000_000, bytes_accessed=3_000_000, transcendentals=0),
+        compiler_params=limit(8),
         name="filter_spectrum",
-    )(got, taps, bias, *consts)
-
-
-def gated_convolution(got, squares, gain, spec, consts):
+    )(got, taps, bias, *[stay(value) for value in consts])
+
+
+def gated_convolution(normed, got, spec, consts):
     return pl.pallas_call(
         signal_kernel,
         out_shape=jax.ShapeDtypeStruct((16, 32, 256), BF16),
-        in_specs=vmem(8),
+        in_specs=[*vmem(2), pl.BlockSpec(memory_space=pl.ANY), *hbm(2)],
         out_specs=vmem(1)[0],
-        scratch_shapes=SCRATCH,
+        scratch_shapes=[*SCRATCH, pltpu.VMEM((OUTER, 32, 2 * INNER), F32)],
         cost_estimate=pl.CostEstimate(flops=1_000_000_000, bytes_accessed=3_000_000, transcendentals=0),
-    )(got, squares, gain, spec, *consts)
-
-
-def pack_kernel(hidden_ref, long_ref, gate_ref, up_ref, payload_ref, squares_ref, sems):
+        compiler_params=limit(8),
+    )(normed, got, stay(spec), *[stay(value) for value in consts])
+
+
+def pack_kernel(hidden_ref, long_ref, gate_ref, up_ref, payload_ref, squares_ref, hidden, sems):
     chan = lax.axis_index("chan")
-    sources = [hidden_ref, long_ref, gate_ref, up_ref.at[:, pl.ds(pl.multiple_of(chan * 32, 32), 32), :]]
-    copies = [
-        pltpu.make_async_copy(source, payload_ref.at[:, 32 * i : 32 * i + 32, :], sems.at[i])
-        for i, source in enumerate(sources)
-    ]
+    sources = [long_ref, gate_ref, up_ref.at[:, pl.ds(pl.multiple_of(chan * 32, 32), 32), :]]
+    copies = [pltpu.make_async_copy(hidden_ref, hidden, sems.at[3])]
+    for i, source in enumerate(sources):
+        copies.append(pltpu.make_async_copy(source, payload_ref.at[:, 32 * i : 32 * i + 32, :], sems.at[i]))
     for copy in copies:
         copy.start()
     copies[0].wait()
     total = jnp.zeros((8, 256), F32)
     for b in range(16):
-        states = payload_ref[b, 0:32, :].astype(F32)
+        states = hidden[b].astype(F32)
         powers = states * states
         for r in range(4):
             total = total + powers[8 * r : 8 * r + 8]
@@ -256,15 +293,20 @@
         copy.wait()
 
 
+def limit(mib):
+    return pltpu.CompilerParams(vmem_limit_bytes=mib * 2**20)
+
+
 def pack(hidden, long_filter, gate, upstream):
     return pl.pallas_call(
         pack_kernel,
-        out_shape=(jax.ShapeDtypeStruct((16, 128, 256), BF16), jax.ShapeDtypeStruct((8, 256), F32)),
-        in_specs=[pl.BlockSpec(memory_space=pl.ANY)] * 4,
+        out_shape=(jax.ShapeDtypeStruct((16, 96, 256), BF16), jax.ShapeDtypeStruct((8, 256), F32)),
+        in_specs=hbm(4),
         out_specs=tuple(vmem(2)),
-        scratch_shapes=[pltpu.SemaphoreType.DMA((4,))],
+        scratch_shapes=[pltpu.VMEM((16, 32, 256), BF16), pltpu.SemaphoreType.DMA((4,))],
+        compiler_params=limit(6),
         name="pack",
-    )(hidden, long_filter, gate, upstream)
+    )(*[stay(value) for value in (hidden, long_filter, gate, upstream)])
 
 
 def place_of(s):
@@ -284,49 +326,38 @@
     return lax.ppermute(value, "chan", pairs)
 
 
-def around(block, move):
-    right = move(block, 1)
-    left = move(block, -1)
-    far_a = move(right[:8], 1)
-    far_b = move(left[8:], -1)
-    return [(block, 0, 0), (right, 3, 0), (left, 1, 0), (far_a, 2, 0), (far_b, 2, 8)]
-
-
 def gather_seq(own):
     side = over_seq(own, 1, 0, 0)
+    near = {(0, 0): own, (1, 0): side}
+    for dx in (3, 1, 2):
+        near[0, dx] = over_seq(own, 0, -dx, 0)
+    for dx in (3, 1):
+        near[1, dx] = over_seq(side, 0, -dx, 0)
+    near[1, 2] = over_seq(near[0, 2], 1, 0, 0)
     pieces = []
-    for dz, block in enumerate((own, side)):
-        for value, dx, row in around(block, lambda v, d: over_seq(v, 0, d, 0)):
-            pieces.append((value, 0, dz, dx, row))
-            pieces.append((over_seq(value, 0, 0, 1), 1, dz, dx, row))
+    for (dz, dx), value in near.items():
+        pieces += [(value, 0, dz, dx), (over_seq(value, 0, 0, 1), 1, dz, dx)]
     return pieces
 
 
 def gather_chan(own):
     side = over_chan(own, 1, 0)
-    pieces = []
+    pieces = [(own, 0, 0), (side, 1, 0)]
     for dz, block in enumerate((own, side)):
-        for value, dy, row in around(block, lambda v, d: over_chan(v, 0, d)):
-            pieces.append((value, dz, dy, row))
+        for dy in (3, 1, 2):
+            pieces.append((over_chan(block, 0, -dy), dz, dy))
     return pieces
 
 
-def whole_rows(refs, keys):
-    blocks = {}
-    for ref, (*key, row) in zip(refs, keys, strict=True):
-        for b in range(ref.shape[0]):
-            blocks.setdefault(tuple(key), {})[row + b] = (ref, b)
-    values = [jnp.concatenate([rows[b][0][rows[b][1]] for b in range(16)], axis=1) for rows in blocks.values()]
-    return jnp.concatenate(values, axis=0), list(blocks)
+def whole_rows(refs):
+    return jnp.concatenate([jnp.concatenate([ref[b] for b in range(16)], axis=1) for ref in refs], axis=0)
 
 
 def grad_kernel(mixed_keys, up_keys, *refs):
     seq, chan = lax.axis_index("seq"), lax.axis_index("chan")
     mixed_refs, up_refs = refs[: len(mixed_keys)], refs[len(mixed_keys) : len(mixed_keys) + len(up_keys)]
     mixed_ref, grad_ref, rows_ref = refs[len(mixed_keys) + len(up_keys) :]
-    mixed, sources = whole_rows(mixed_refs, mixed_keys)
-    up, owners = whole_rows(up_refs, up_keys)
-    total = lax.dot_general(mixed, up, (((1,), (1,)), ((), ())), preferred_element_type=F32)
+    total = lax.dot_general(whole_rows(mixed_refs), whole_rows(up_refs), (((1,), (1,)), ((), ())), preferred_element_type=F32)
 
     def source_place(dk, dz, dx):
         z = lax.bitwise_xor(seq // 8, dz)
@@ -334,20 +365,12 @@
         k = lax.bitwise_xor(lax.bitwise_and(seq, 1), dk)
         return pl.ds(pl.multiple_of((z * 8 + x * 2 + k) * 32, 32), 32)
 
-    for i, key in enumerate(sources):
-        rows_ref[source_place(*key), :] = total[32 * i : 32 * i + 32]
-    for ref, (*key, row) in zip(mixed_refs, mixed_keys, strict=True):
+    for i, (ref, key) in enumerate(zip(mixed_refs, mixed_keys, strict=True)):
         place = source_place(*key)
-        if ref.shape[0] == 16:
-            mixed_ref[place, :] = ref[seq]
-        else:
-
-            @pl.when(seq // 8 == row // 8)
-            def _(ref=ref, place=place):
-                mixed_ref[place, :] = ref[lax.bitwise_and(seq, 7)]
-
+        rows_ref[place, :] = total[32 * i : 32 * i + 32]
+        mixed_ref[place, :] = ref[seq]
     turned_rows = rows_ref[...].T
-    for i, (dz, dy) in enumerate(owners):
+    for i, (dz, dy) in enumerate(up_keys):
         owner = lax.bitwise_xor(chan // 4, dz) * 4 + lax.bitwise_and(chan + dy, 3)
         grad_ref[pl.ds(pl.multiple_of(owner * 32, 32), 32), :] = turned_rows[32 * i : 32 * i + 32]
 
@@ -361,6 +384,7 @@
         out_specs=tuple(vmem(2)),
         scratch_shapes=[pltpu.VMEM((512, 256), F32)],
         cost_estimate=pl.CostEstimate(flops=1_000_000_000, bytes_accessed=7_000_000, transcendentals=0),
+        compiler_params=limit(16),
         name="weight_gradient",
     )(*[piece[0] for piece in mixed], *[piece[0] for piece in up])
 
@@ -377,11 +401,12 @@
     got = exchange(payload, "seq")
     squares = squares + over_chan(squares, 0, 1)
     squares = squares + over_chan(squares, 0, 2)
-    squares = jnp.broadcast_to(squares, (16, 8, 256))
-    squares = exchange(squares, "seq")
+    scale = lax.rsqrt(jnp.sum(squares, axis=0) / D + EPSILON)
+    normed = (hidden_states.astype(F32) * scale[None, :] * norm_gain[:, None]).astype(BF16)
+    normed = exchange(normed.reshape(16, 32, 256), "seq")
     spec = filter_spectrum(got, short_filter, long_bias[None, :], consts)
-    up = gather_chan(got[:, 96:128])
-    mixed = gated_convolution(got, squares, norm_gain[None, :], spec, consts)
+    up = gather_chan(got[:, 64:96])
+    mixed = gated_convolution(normed, got, spec, consts)
     return weight_gradient(gather_seq(mixed), up)
 
 

time: 116 us -> 96.5 us (0.83)
  waiting for transfers between devices: 25.7 us -> 17.9 us
  Pallas kernels: 21.3 us -> 15 us
  starting transfers between devices: 63.8 us -> 60.6 us
  local copies, waits for them, and re-layouts: 2.97 us -> 1.01 us
    ppermute x19 -> x15, waiting for transfers between devices: 12.2 us -> 6.62 us  [over_seq(): return lax.ppermute(value, 'seq', pairs)]
    ppermute x12 -> x10, starting transfers between devices: 13.6 us -> 10.1 us  [over_chan(): return lax.ppermute(value, 'chan', pairs)]
    pallas_call x1, Pallas kernels: 5.11 us -> 2.29 us  [weight_gradient(): pl.pallas_call(functools.partial(grad_kernel, mixed_keys, up_keys), out_s...]
    ppermute x12 -> x10, waiting for transfers between devices: 12.8 us -> 10.6 us  [over_chan(): return lax.ppermute(value, 'chan', pairs)]
    pallas_call x1, Pallas kernels: 7.88 us -> 6.1 us  [filter_spectrum(): pl.pallas_call(filter_kernel, out_shape=jax.ShapeDtypeStruct((OUTER, 32,...]
    pallas_call x1, Pallas kernels: 6.04 us -> 4.43 us  [gated_convolution(): pl.pallas_call(signal_kernel, out_shape=jax.ShapeDtypeStruct((16, 32, 256...]
    all_to_all x2, starting transfers between devices: 23.3 us -> 24.6 us  [exchange(): return lax.all_to_all(value, axis, split_axis=0, concat_axis=0, tiled=True)]
    unnamed x60 -> x10, local copies, waits for them, and re-layouts: 2.17 us -> 0.99 us
  transfers between devices with their start and end apart: 33 -> 27, of which waited for: 9 -> 9; matrix products, arithmetic and copies ran while one was open for 0% -> 1% of each run, Pallas kernels for 12% -> 11%
where the time goes in v1:
time: 96.5 us; the launch traced here: 96.2 us
  starting transfers between devices  60.6 us (63%)
  waiting for transfers between devices  17.9 us (19%)
  Pallas kernels  15 us (16%)
  local copies, waits for them, and re-layouts  1.01 us (1%)
    ppermute x15, starting transfers between devices, over_seq(): return lax.ppermute(value, 'seq', pairs)  25.9 us
    all_to_all x2, starting transfers between devices, exchange(): return lax.all_to_all(value, axis, split_axis=0, concat_axis=0, tiled=True)  24.6 us
    ppermute x10, waiting for transfers between devices, over_chan(): return lax.ppermute(value, 'chan', pairs)  10.6 us
    ppermute x10, starting transfers between devices, over_chan(): return lax.ppermute(value, 'chan', pairs)  10.1 us
    ppermute x15, waiting for transfers between devices, over_seq(): return lax.ppermute(value, 'seq', pairs)  6.62 us
    pallas_call x1, Pallas kernels, filter_spectrum(): pl.pallas_call(filter_kernel, out_shape=jax.ShapeDtypeStruct((OUTER, 32,...  6.1 us
    pallas_call x1, Pallas kernels, gated_convolution(): pl.pallas_call(signal_kernel, out_shape=jax.ShapeDtypeStruct((16, 32, 256...  4.43 us
    pallas_call x1, Pallas kernels, weight_gradient(): pl.pallas_call(functools.partial(grad_kernel, mixed_keys, up_keys), out_s...  2.29 us
  transfers between devices with their start and end apart: 27, of which 9 were waited for; matrix products, arithmetic and copies ran while one was open for 1% of the time, Pallas kernels for 11%

profile of v1, /device:TPU:1, one launch (start us, length us, event | category | flops | bytes accessed | tf_op | source)
XLA Modules:
  0.0 96.2 jit_solution(7883674939888895459)
XLA Ops:
  0.7 2.2 %pack.1 = (bf16[16,96,256]{2,1,0:T(8,128)(2,1)}, f32[8,256]{1,0:T(8,128)S(1)}) custom-call(bf16[16,32,256]{2,1,0:T(8,128)(2,1)} %bitcast.8, bf16[16,32,256]{2,1,0:T(8,128)(2,1)} %bitcast.9, bf16[16,32,256]{2,1,0:T(8,128)(2,1)} %bitcast.10, bf16[16,256,256]{2,1,0:T(8,128)(2,1)} %bitcast.7), custom_call_target="tpu_custom_call" | custom-call | tf_op jit(solution)/shard_map/pack/pallas_call | solution.py:301
  2.8 0.0 copy-start
  2.8 0.0 copy-start.1
  2.8 9.3 %all-to-all-start.1 = ((bf16[16,96,256]{2,1,0:T(8,128)(2,1)}), bf16[16,96,256]{2,1,0:T(8,128)(2,1)S(1)}, u32[]{:S(2)}, u32[]{:S(2)}) async-start(bf16[16,96,256]{2,1,0:T(8,128)(2,1)} %get-tuple-element.5), calls=%async_computation.1 | async-start | bytes 1572864 | tf_op jit(solution)/shard_map/all_to_all | solution.py:393
  12.1 0.7 collective-permute-start
  12.8 3.8 %collective-permute-done = f32[8,256]{1,0:T(8,128)S(1)} collective-permute-done((f32[8,256]{1,0:T(8,128)S(1)}, f32[8,256]{1,0:T(8,128)S(1)}, u32[]{:S(2)}, u32[]{:S(2)}) %collective-permute-start) | collective-permute-done | bytes 8224 | tf_op jit(solution)/shard_map/ppermute | solution.py:326
  16.6 1.3 %collective-permute-start.1 = (f32[8,256]{1,0:T(8,128)S(1)}, f32[8,256]{1,0:T(8,128)S(1)}, u32[]{:S(2)}, u32[]{:S(2)}) collective-permute-start(f32[8,256]{1,0:T(8,128)S(1)} %add.19), channel_id=1, source_target_pairs={{0,1},{1,2},{2,3},{3,0},{4,5},{5,6},{6,7},{7,4},{8,9},{9,10},{10,1... | collective-permute-start | bytes 24584 | tf_op jit(solution)/shard_map/ppermute | solution.py:326
  17.9 2.8 %collective-permute-done.1 = f32[8,256]{1,0:T(8,128)S(1)} collective-permute-done((f32[8,256]{1,0:T(8,128)S(1)}, f32[8,256]{1,0:T(8,128)S(1)}, u32[]{:S(2)}, u32[]{:S(2)}) %collective-permute-start.1) | collective-permute-done | bytes 8224 | tf_op jit(solution)/shard_map/ppermute | solution.py:326
  20.7 1.6 %collective-permute-start.2 = (f32[8,256]{1,0:T(8,128)S(1)}, f32[8,256]{1,0:T(8,128)S(1)}, u32[]{:S(2)}, u32[]{:S(2)}) collective-permute-start(f32[8,256]{1,0:T(8,128)S(1)} %add.20), channel_id=1, source_target_pairs={{0,2},{1,3},{2,0},{3,1},{4,6},{5,7},{6,4},{7,5},{8,10},{9,11},{10,... | collective-permute-start | bytes 24584 | tf_op jit(solution)/shard_map/ppermute | solution.py:326
  22.3 2.4 %collective-permute-done.2 = f32[8,256]{1,0:T(8,128)S(1)} collective-permute-done((f32[8,256]{1,0:T(8,128)S(1)}, f32[8,256]{1,0:T(8,128)S(1)}, u32[]{:S(2)}, u32[]{:S(2)}) %collective-permute-start.2) | collective-permute-done | bytes 8224 | tf_op jit(solution)/shard_map/ppermute | solution.py:326
  24.8 0.8 multiply_convert_fusion
  25.6 0.7 all-to-all-done.1.got_ref
  26.3 15.3 %all-to-all-start = ((bf16[16,32,256]{2,1,0:T(8,128)(2,1)}), bf16[16,32,256]{2,1,0:T(8,128)(2,1)S(1)}, u32[]{:S(2)}, u32[]{:S(2)}) async-start(bf16[16,32,256]{2,1,0:T(8,128)(2,1)} %bitcast.4), calls=%async_computation | async-start | bytes 524288 | tf_op jit(solution)/shard_map/all_to_all | solution.py:393
  41.7 1.8 %collective-permute-start.21 = (bf16[16,32,256]{2,1,0:T(8,128)(2,1)S(1)}, bf16[16,32,256]{2,1,0:T(8,128)(2,1)S(1)}, u32[]{:S(2)}, u32[]{:S(2)}) collective-permute-start(bf16[16,32,256]{2,1,0:T(8,128)(2,1)S(1)} %slice.4.refs_16_), channel_id=1, source_target_pairs={{0,2},{1,3},{2,0},{3,1},{4,6},{5,7},{6,4},{7,5},{8,10},{9,11},{10,... | collective-permute-start | bytes 786440 | tf_op jit(solution)/shard_map/ppermute | solution.py:326
  43.4 0.8 collective-permute-start.20
  44.2 0.7 collective-permute-start.19
  44.9 0.0 collective-permute-start.18
  44.9 6.1 %filter_spectrum.1.spec_any = f32[32,32,256]{2,1,0:T(8,128)S(1)} custom-call(bf16[16,96,256]{2,1,0:T(8,128)(2,1)S(1)} %all-to-all-done.1.got_ref, f32[512,128]{1,0:T(8,128)S(1)} %copy-done, f32[1,512]{1,0:T(1,128)S(1)} %bitcast.6, f32[2,32,128]{2,1,0:T(8,128)} %constant.11.clone.turn_hbm, bf16[2,768,256]{2,1,0:T(8,128)(2,1)} %constant.12.clone.inner_hbm), custom_call_target="tpu_custom_call" | custom-call | flops 2000000000 | bytes 3000000 | tf_op jit(solution)/shard_map/filter_spectrum/pallas_call | solution.py:252
  51.0 1.0 %copy-done.2 = f32[32,32,256]{2,1,0:T(8,128)} copy-done((f32[32,32,256]{2,1,0:T(8,128)}, f32[32,32,256]{2,1,0:T(8,128)S(1)}, u32[]{:S(2)}) %copy-start.2) | copy-done | bytes 1048600
  52.0 4.4 %shard_map.104.refs_0_ = bf16[16,32,256]{2,1,0:T(8,128)(2,1)S(1)} custom-call(bf16[16,32,256]{2,1,0:T(8,128)(2,1)S(1)} %all-to-all-done.normed_ref, bf16[16,96,256]{2,1,0:T(8,128)(2,1)S(1)} %all-to-all-done.1.got_ref, f32[32,32,256]{2,1,0:T(8,128)} %copy-done.2, f32[2,32,128]{2,1,0:T(8,128)} %constant.11.clone.turn_hbm, ...), custom_call_target="tpu_custom_call" | custom-call | flops 1000000000 | bytes 3000000 | tf_op jit(solution)/shard_map/pallas_call | solution.py:265
  56.5 2.9 %collective-permute-start.10 = (bf16[16,32,256]{2,1,0:T(8,128)(2,1)S(1)}, bf16[16,32,256]{2,1,0:T(8,128)(2,1)S(1)}, u32[]{:S(2)}, u32[]{:S(2)}) collective-permute-start(bf16[16,32,256]{2,1,0:T(8,128)(2,1)S(1)} %shard_map.104.refs_0_), channel_id=1, source_target_pairs={{0,32},{8,40},{16,48},{24,56},{32,0},{40,8},{48,16},{56,24},{64,96... | collective-permute-start | bytes 786440 | tf_op jit(solution)/shard_map/ppermute | solution.py:321
  59.4 0.0 collective-permute-done.21.refs_20_
  59.4 0.9 collective-permute-start.8
  60.3 0.0 collective-permute-done.20.refs_19_
  60.3 0.6 collective-permute-start.6
  60.9 2.9 %collective-permute-start.4 = (bf16[16,32,256]{2,1,0:T(8,128)(2,1)S(1)}, bf16[16,32,256]{2,1,0:T(8,128)(2,1)S(1)}, u32[]{:S(2)}, u32[]{:S(2)}) collective-permute-start(bf16[16,32,256]{2,1,0:T(8,128)(2,1)S(1)} %shard_map.104.refs_0_), channel_id=1, source_target_pairs={{0,64},{8,72},{16,80},{24,88},{32,96},{40,104},{48,112},{56,120},{... | collective-permute-start | bytes 786440 | tf_op jit(solution)/shard_map/ppermute | solution.py:321
  63.8 0.0 collective-permute-done.18.refs_17_
  63.8 2.6 %collective-permute-start.3 = (bf16[16,32,256]{2,1,0:T(8,128)(2,1)S(1)}, bf16[16,32,256]{2,1,0:T(8,128)(2,1)S(1)}, u32[]{:S(2)}, u32[]{:S(2)}) collective-permute-start(bf16[16,32,256]{2,1,0:T(8,128)(2,1)S(1)} %shard_map.104.refs_0_), channel_id=1, source_target_pairs={{0,8},{8,0},{16,24},{24,16},{32,40},{40,32},{48,56},{56,48},{64,72... | collective-permute-start | bytes 786440 | tf_op jit(solution)/shard_map/ppermute | solution.py:321
  66.4 1.2 %collective-permute-start.24 = (bf16[16,32,256]{2,1,0:T(8,128)(2,1)S(1)}, bf16[16,32,256]{2,1,0:T(8,128)(2,1)S(1)}, u32[]{:S(2)}, u32[]{:S(2)}) collective-permute-start(bf16[16,32,256]{2,1,0:T(8,128)(2,1)S(1)} %collective-permute-done.18.refs_17_), channel_id=1, source_target_pairs={{0,2},{1,3},{2,0},{3,1},{4,6},{5,7},{6,4},{7,5},{8,10},{9,11},{10,... | collective-permute-start | bytes 786440 | tf_op jit(solution)/shard_map/ppermute | solution.py:326
  67.6 3.4 %collective-permute-done.8.refs_6_ = bf16[16,32,256]{2,1,0:T(8,128)(2,1)S(1)} collective-permute-done((bf16[16,32,256]{2,1,0:T(8,128)(2,1)S(1)}, bf16[16,32,256]{2,1,0:T(8,128)(2,1)S(1)}, u32[]{:S(2)}, u32[]{:S(2)}) %collective-permute-start.8) | collective-permute-done | bytes 262176 | tf_op jit(solution)/shard_map/ppermute | solution.py:321
  71.0 2.0 %collective-permute-start.23 = (bf16[16,32,256]{2,1,0:T(8,128)(2,1)S(1)}, bf16[16,32,256]{2,1,0:T(8,128)(2,1)S(1)}, u32[]{:S(2)}, u32[]{:S(2)}) collective-permute-start(bf16[16,32,256]{2,1,0:T(8,128)(2,1)S(1)} %collective-permute-done.18.refs_17_), channel_id=1, source_target_pairs={{0,3},{1,0},{2,1},{3,2},{4,7},{5,4},{6,5},{7,6},{8,11},{9,8},{10,9... | collective-permute-start | bytes 786440 | tf_op jit(solution)/shard_map/ppermute | solution.py:326
  73.0 0.0 collective-permute-done.6.refs_4_
  73.0 2.9 %collective-permute-start.16 = (bf16[16,32,256]{2,1,0:T(8,128)(2,1)S(1)}, bf16[16,32,256]{2,1,0:T(8,128)(2,1)S(1)}, u32[]{:S(2)}, u32[]{:S(2)}) collective-permute-start(bf16[16,32,256]{2,1,0:T(8,128)(2,1)S(1)} %collective-permute-done.10.refs_8_), channel_id=1, source_target_pairs={{0,64},{8,72},{16,80},{24,88},{32,96},{40,104},{48,112},{56,120},{... | collective-permute-start | bytes 786440 | tf_op jit(solution)/shard_map/ppermute | solution.py:321
  75.9 2.1 %collective-permute-start.11 = (bf16[16,32,256]{2,1,0:T(8,128)(2,1)S(1)}, bf16[16,32,256]{2,1,0:T(8,128)(2,1)S(1)}, u32[]{:S(2)}, u32[]{:S(2)}) collective-permute-start(bf16[16,32,256]{2,1,0:T(8,128)(2,1)S(1)} %collective-permute-done.10.refs_8_), channel_id=1, source_target_pairs={{0,8},{8,0},{16,24},{24,16},{32,40},{40,32},{48,56},{56,48},{64,72... | collective-permute-start | bytes 786440 | tf_op jit(solution)/shard_map/ppermute | solution.py:321
  78.0 0.0 collective-permute-done.24.refs_23_
  78.0 0.1 collective-permute-start.9
  78.1 1.6 %collective-permute-done.23.refs_22_ = bf16[16,32,256]{2,1,0:T(8,128)(2,1)S(1)} collective-permute-done((bf16[16,32,256]{2,1,0:T(8,128)(2,1)S(1)}, bf16[16,32,256]{2,1,0:T(8,128)(2,1)S(1)}, u32[]{:S(2)}, u32[]{:S(2)}) %collective-permute-start.23) | collective-permute-done | bytes 262176 | tf_op jit(solution)/shard_map/ppermute | solution.py:326
  79.7 3.0 %collective-permute-start.14 = (bf16[16,32,256]{2,1,0:T(8,128)(2,1)S(1)}, bf16[16,32,256]{2,1,0:T(8,128)(2,1)S(1)}, u32[]{:S(2)}, u32[]{:S(2)}) collective-permute-start(bf16[16,32,256]{2,1,0:T(8,128)(2,1)S(1)} %collective-permute-done.4.refs_2_), channel_id=1, source_target_pairs={{0,48},{8,56},{16,0},{24,8},{32,16},{40,24},{48,32},{56,40},{64,11... | collective-permute-start | bytes 786440 | tf_op jit(solution)/shard_map/ppermute | solution.py:321
  82.8 0.8 collective-permute-start.12
  83.5 1.9 %collective-permute-start.5 = (bf16[16,32,256]{2,1,0:T(8,128)(2,1)S(1)}, bf16[16,32,256]{2,1,0:T(8,128)(2,1)S(1)}, u32[]{:S(2)}, u32[]{:S(2)}) collective-permute-start(bf16[16,32,256]{2,1,0:T(8,128)(2,1)S(1)} %collective-permute-done.4.refs_2_), channel_id=1, source_target_pairs={{0,8},{8,0},{16,24},{24,16},{32,40},{40,32},{48,56},{56,48},{64,72... | collective-permute-start | bytes 786440 | tf_op jit(solution)/shard_map/ppermute | solution.py:321
  85.4 0.1 collective-permute-start.7
  85.5 0.4 collective-permute-start.17
  86.0 1.1 %collective-permute-done.14.refs_12_ = bf16[16,32,256]{2,1,0:T(8,128)(2,1)S(1)} collective-permute-done((bf16[16,32,256]{2,1,0:T(8,128)(2,1)S(1)}, bf16[16,32,256]{2,1,0:T(8,128)(2,1)S(1)}, u32[]{:S(2)}, u32[]{:S(2)}) %collective-permute-start.14) | collective-permute-done | bytes 262176 | tf_op jit(solution)/shard_map/ppermute | solution.py:321
  87.1 2.2 %collective-permute-start.15 = (bf16[16,32,256]{2,1,0:T(8,128)(2,1)S(1)}, bf16[16,32,256]{2,1,0:T(8,128)(2,1)S(1)}, u32[]{:S(2)}, u32[]{:S(2)}) collective-permute-start(bf16[16,32,256]{2,1,0:T(8,128)(2,1)S(1)} %collective-permute-done.14.refs_12_), channel_id=1, source_target_pairs={{0,8},{8,0},{16,24},{24,16},{32,40},{40,32},{48,56},{56,48},{64,72... | collective-permute-start | bytes 786440 | tf_op jit(solution)/shard_map/ppermute | solution.py:321
  89.3 0.9 collective-permute-done.12.refs_10_
  90.2 2.5 %collective-permute-start.13 = (bf16[16,32,256]{2,1,0:T(8,128)(2,1)S(1)}, bf16[16,32,256]{2,1,0:T(8,128)(2,1)S(1)}, u32[]{:S(2)}, u32[]{:S(2)}) collective-permute-start(bf16[16,32,256]{2,1,0:T(8,128)(2,1)S(1)} %collective-permute-done.12.refs_10_), channel_id=1, source_target_pairs={{0,8},{8,0},{16,24},{24,16},{32,40},{40,32},{48,56},{56,48},{64,72... | collective-permute-start | bytes 786440 | tf_op jit(solution)/shard_map/ppermute | solution.py:321
  92.7 1.1 %collective-permute-done.13.refs_11_ = bf16[16,32,256]{2,1,0:T(8,128)(2,1)S(1)} collective-permute-done((bf16[16,32,256]{2,1,0:T(8,128)(2,1)S(1)}, bf16[16,32,256]{2,1,0:T(8,128)(2,1)S(1)}, u32[]{:S(2)}, u32[]{:S(2)}) %collective-permute-start.13) | collective-permute-done | bytes 262176 | tf_op jit(solution)/shard_map/ppermute | solution.py:321
  93.9 2.3 %weight_gradient.1 = (bf16[512,256]{1,0:T(8,128)(2,1)}, f32[256,512]{1,0:T(8,128)}) custom-call(bf16[16,32,256]{2,1,0:T(8,128)(2,1)S(1)} %shard_map.104.refs_0_, bf16[16,32,256]{2,1,0:T(8,128)(2,1)S(1)} %collective-permute-done.3.refs_1_, bf16[16,32,256]{2,1,0:T(8,128)(2,1)S(1)} %collective-permute-done.4.refs_2_, ...), custom_call_target="tpu_custom_call" | custom-call | flops 1000000000 | bytes 7000000 | tf_op jit(solution)/shard_map/weight_gradient/pallas_call | solution.py:380
  (26 shorter events, 0.1 us)
Async XLA Ops:
  0.6 24.1 %copy-start.3 = (bf16[512,256]{1,0:T(8,128)(2,1)S(1)}, bf16[512,256]{1,0:T(8,128)(2,1)}, u32[]{:S(2)}) copy-start(bf16[512,256]{1,0:T(8,128)(2,1)} %param.9) | copy-start | bytes 786436
  0.6 24.1 %copy-start.4 = (f32[512]{0:T(512)S(1)}, f32[512]{0:T(512)}, u32[]{:S(2)}) copy-start(f32[512]{0:T(512)} %param.10) | copy-start | bytes 6148
  2.8 42.1 %copy-start = (f32[512,128]{1,0:T(8,128)S(1)}, f32[512,128]{1,0:T(8,128)}, u32[]{:S(2)}) copy-start(f32[512,128]{1,0:T(8,128)} %taps_ref.1) | copy-start | bytes 786436
  2.8 42.1 %copy-start.1 = (f32[512]{0:T(512)S(1)}, f32[512]{0:T(512)}, u32[]{:S(2)}) copy-start(f32[512]{0:T(512)} %param.13) | copy-start | bytes 6148
  2.8 23.5 %all-to-all-start.1 = ((bf16[16,96,256]{2,1,0:T(8,128)(2,1)}), bf16[16,96,256]{2,1,0:T(8,128)(2,1)S(1)}, u32[]{:S(2)}, u32[]{:S(2)}) async-start(bf16[16,96,256]{2,1,0:T(8,128)(2,1)} %get-tuple-element.5), calls=%async_computation.1 | async-start | bytes 1572864 | tf_op jit(solution)/shard_map/all_to_all | solution.py:393
  12.1 4.5 %collective-permute-start = (f32[8,256]{1,0:T(8,128)S(1)}, f32[8,256]{1,0:T(8,128)S(1)}, u32[]{:S(2)}, u32[]{:S(2)}) collective-permute-start(f32[8,256]{1,0:T(8,128)S(1)} %get-tuple-element.4), channel_id=1, source_target_pairs={{0,4},{1,5},{2,6},{3,7},{4,0},{5,1},{6,2},{7,3},{8,12},{9,13},{10,... | collective-permute-start | bytes 24584 | tf_op jit(solution)/shard_map/ppermute | solution.py:326
  16.6 4.1 %collective-permute-start.1 = (f32[8,256]{1,0:T(8,128)S(1)}, f32[8,256]{1,0:T(8,128)S(1)}, u32[]{:S(2)}, u32[]{:S(2)}) collective-permute-start(f32[8,256]{1,0:T(8,128)S(1)} %add.19), channel_id=1, source_target_pairs={{0,1},{1,2},{2,3},{3,0},{4,5},{5,6},{6,7},{7,4},{8,9},{9,10},{10,1... | collective-permute-start | bytes 24584 | tf_op jit(solution)/shard_map/ppermute | solution.py:326
  20.7 4.0 %collective-permute-start.2 = (f32[8,256]{1,0:T(8,128)S(1)}, f32[8,256]{1,0:T(8,128)S(1)}, u32[]{:S(2)}, u32[]{:S(2)}) collective-permute-start(f32[8,256]{1,0:T(8,128)S(1)} %add.20), channel_id=1, source_target_pairs={{0,2},{1,3},{2,0},{3,1},{4,6},{5,7},{6,4},{7,5},{8,10},{9,11},{10,... | collective-permute-start | bytes 24584 | tf_op jit(solution)/shard_map/ppermute | solution.py:326
  26.3 25.7 %all-to-all-start = ((bf16[16,32,256]{2,1,0:T(8,128)(2,1)}), bf16[16,32,256]{2,1,0:T(8,128)(2,1)S(1)}, u32[]{:S(2)}, u32[]{:S(2)}) async-start(bf16[16,32,256]{2,1,0:T(8,128)(2,1)} %bitcast.4), calls=%async_computation | async-start | bytes 524288 | tf_op jit(solution)/shard_map/all_to_all | solution.py:393
  41.7 17.7 %collective-permute-start.21 = (bf16[16,32,256]{2,1,0:T(8,128)(2,1)S(1)}, bf16[16,32,256]{2,1,0:T(8,128)(2,1)S(1)}, u32[]{:S(2)}, u32[]{:S(2)}) collective-permute-start(bf16[16,32,256]{2,1,0:T(8,128)(2,1)S(1)} %slice.4.refs_16_), channel_id=1, source_target_pairs={{0,2},{1,3},{2,0},{3,1},{4,6},{5,7},{6,4},{7,5},{8,10},{9,11},{10,... | collective-permute-start | bytes 786440 | tf_op jit(solution)/shard_map/ppermute | solution.py:326
  43.4 16.8 %collective-permute-start.20 = (bf16[16,32,256]{2,1,0:T(8,128)(2,1)S(1)}, bf16[16,32,256]{2,1,0:T(8,128)(2,1)S(1)}, u32[]{:S(2)}, u32[]{:S(2)}) collective-permute-start(bf16[16,32,256]{2,1,0:T(8,128)(2,1)S(1)} %slice.4.refs_16_), channel_id=1, source_target_pairs={{0,3},{1,0},{2,1},{3,2},{4,7},{5,4},{6,5},{7,6},{8,11},{9,8},{10,9... | collective-permute-start | bytes 786440 | tf_op jit(solution)/shard_map/ppermute | solution.py:326
  44.2 16.7 %collective-permute-start.19 = (bf16[16,32,256]{2,1,0:T(8,128)(2,1)S(1)}, bf16[16,32,256]{2,1,0:T(8,128)(2,1)S(1)}, u32[]{:S(2)}, u32[]{:S(2)}) collective-permute-start(bf16[16,32,256]{2,1,0:T(8,128)(2,1)S(1)} %slice.4.refs_16_), channel_id=1, source_target_pairs={{0,1},{1,2},{2,3},{3,0},{4,5},{5,6},{6,7},{7,4},{8,9},{9,10},{10,1... | collective-permute-start | bytes 786440 | tf_op jit(solution)/shard_map/ppermute | solution.py:326
  44.9 18.8 %collective-permute-start.18 = (bf16[16,32,256]{2,1,0:T(8,128)(2,1)S(1)}, bf16[16,32,256]{2,1,0:T(8,128)(2,1)S(1)}, u32[]{:S(2)}, u32[]{:S(2)}) collective-permute-start(bf16[16,32,256]{2,1,0:T(8,128)(2,1)S(1)} %slice.4.refs_16_), channel_id=1, source_target_pairs={{0,4},{1,5},{2,6},{3,7},{4,0},{5,1},{6,2},{7,3},{8,12},{9,13},{10,... | collective-permute-start | bytes 786440 | tf_op jit(solution)/shard_map/ppermute | solution.py:326
  51.0 1.0 %copy-start.2 = (f32[32,32,256]{2,1,0:T(8,128)}, f32[32,32,256]{2,1,0:T(8,128)S(1)}, u32[]{:S(2)}) copy-start(f32[32,32,256]{2,1,0:T(8,128)S(1)} %filter_spectrum.1.spec_any) | copy-start | bytes 3145732
  56.5 9.9 %collective-permute-start.10 = (bf16[16,32,256]{2,1,0:T(8,128)(2,1)S(1)}, bf16[16,32,256]{2,1,0:T(8,128)(2,1)S(1)}, u32[]{:S(2)}, u32[]{:S(2)}) collective-permute-start(bf16[16,32,256]{2,1,0:T(8,128)(2,1)S(1)} %shard_map.104.refs_0_), channel_id=1, source_target_pairs={{0,32},{8,40},{16,48},{24,56},{32,0},{40,8},{48,16},{56,24},{64,96... | collective-permute-start | bytes 786440 | tf_op jit(solution)/shard_map/ppermute | solution.py:321
  59.4 11.6 %collective-permute-start.8 = (bf16[16,32,256]{2,1,0:T(8,128)(2,1)S(1)}, bf16[16,32,256]{2,1,0:T(8,128)(2,1)S(1)}, u32[]{:S(2)}, u32[]{:S(2)}) collective-permute-start(bf16[16,32,256]{2,1,0:T(8,128)(2,1)S(1)} %shard_map.104.refs_0_), channel_id=1, source_target_pairs={{0,48},{8,56},{16,0},{24,8},{32,16},{40,24},{48,32},{56,40},{64,11... | collective-permute-start | bytes 786440 | tf_op jit(solution)/shard_map/ppermute | solution.py:321
  60.3 12.7 %collective-permute-start.6 = (bf16[16,32,256]{2,1,0:T(8,128)(2,1)S(1)}, bf16[16,32,256]{2,1,0:T(8,128)(2,1)S(1)}, u32[]{:S(2)}, u32[]{:S(2)}) collective-permute-start(bf16[16,32,256]{2,1,0:T(8,128)(2,1)S(1)} %shard_map.104.refs_0_), channel_id=1, source_target_pairs={{0,16},{8,24},{16,32},{24,40},{32,48},{40,56},{48,0},{56,8},{64,80... | collective-permute-start | bytes 786440 | tf_op jit(solution)/shard_map/ppermute | solution.py:321
  60.9 12.2 %collective-permute-start.4 = (bf16[16,32,256]{2,1,0:T(8,128)(2,1)S(1)}, bf16[16,32,256]{2,1,0:T(8,128)(2,1)S(1)}, u32[]{:S(2)}, u32[]{:S(2)}) collective-permute-start(bf16[16,32,256]{2,1,0:T(8,128)(2,1)S(1)} %shard_map.104.refs_0_), channel_id=1, source_target_pairs={{0,64},{8,72},{16,80},{24,88},{32,96},{40,104},{48,112},{56,120},{... | collective-permute-start | bytes 786440 | tf_op jit(solution)/shard_map/ppermute | solution.py:321
  63.8 12.2 %collective-permute-start.3 = (bf16[16,32,256]{2,1,0:T(8,128)(2,1)S(1)}, bf16[16,32,256]{2,1,0:T(8,128)(2,1)S(1)}, u32[]{:S(2)}, u32[]{:S(2)}) collective-permute-start(bf16[16,32,256]{2,1,0:T(8,128)(2,1)S(1)} %shard_map.104.refs_0_), channel_id=1, source_target_pairs={{0,8},{8,0},{16,24},{24,16},{32,40},{40,32},{48,56},{56,48},{64,72... | collective-permute-start | bytes 786440 | tf_op jit(solution)/shard_map/ppermute | solution.py:321
  66.4 11.6 %collective-permute-start.24 = (bf16[16,32,256]{2,1,0:T(8,128)(2,1)S(1)}, bf16[16,32,256]{2,1,0:T(8,128)(2,1)S(1)}, u32[]{:S(2)}, u32[]{:S(2)}) collective-permute-start(bf16[16,32,256]{2,1,0:T(8,128)(2,1)S(1)} %collective-permute-done.18.refs_17_), channel_id=1, source_target_pairs={{0,2},{1,3},{2,0},{3,1},{4,6},{5,7},{6,4},{7,5},{8,10},{9,11},{10,... | collective-permute-start | bytes 786440 | tf_op jit(solution)/shard_map/ppermute | solution.py:326
  71.0 8.7 %collective-permute-start.23 = (bf16[16,32,256]{2,1,0:T(8,128)(2,1)S(1)}, bf16[16,32,256]{2,1,0:T(8,128)(2,1)S(1)}, u32[]{:S(2)}, u32[]{:S(2)}) collective-permute-start(bf16[16,32,256]{2,1,0:T(8,128)(2,1)S(1)} %collective-permute-done.18.refs_17_), channel_id=1, source_target_pairs={{0,3},{1,0},{2,1},{3,2},{4,7},{5,4},{6,5},{7,6},{8,11},{9,8},{10,9... | collective-permute-start | bytes 786440 | tf_op jit(solution)/shard_map/ppermute | solution.py:326
  73.0 9.7 %collective-permute-start.22 = (bf16[16,32,256]{2,1,0:T(8,128)(2,1)S(1)}, bf16[16,32,256]{2,1,0:T(8,128)(2,1)S(1)}, u32[]{:S(2)}, u32[]{:S(2)}) collective-permute-start(bf16[16,32,256]{2,1,0:T(8,128)(2,1)S(1)} %collective-permute-done.18.refs_17_), channel_id=1, source_target_pairs={{0,1},{1,2},{2,3},{3,0},{4,5},{5,6},{6,7},{7,4},{8,9},{9,10},{10,1... | collective-permute-start | bytes 786440 | tf_op jit(solution)/shard_map/ppermute | solution.py:326
  73.0 10.5 %collective-permute-start.16 = (bf16[16,32,256]{2,1,0:T(8,128)(2,1)S(1)}, bf16[16,32,256]{2,1,0:T(8,128)(2,1)S(1)}, u32[]{:S(2)}, u32[]{:S(2)}) collective-permute-start(bf16[16,32,256]{2,1,0:T(8,128)(2,1)S(1)} %collective-permute-done.10.refs_8_), channel_id=1, source_target_pairs={{0,64},{8,72},{16,80},{24,88},{32,96},{40,104},{48,112},{56,120},{... | collective-permute-start | bytes 786440 | tf_op jit(solution)/shard_map/ppermute | solution.py:321
  75.9 9.5 %collective-permute-start.11 = (bf16[16,32,256]{2,1,0:T(8,128)(2,1)S(1)}, bf16[16,32,256]{2,1,0:T(8,128)(2,1)S(1)}, u32[]{:S(2)}, u32[]{:S(2)}) collective-permute-start(bf16[16,32,256]{2,1,0:T(8,128)(2,1)S(1)} %collective-permute-done.10.refs_8_), channel_id=1, source_target_pairs={{0,8},{8,0},{16,24},{24,16},{32,40},{40,32},{48,56},{56,48},{64,72... | collective-permute-start | bytes 786440 | tf_op jit(solution)/shard_map/ppermute | solution.py:321
  78.0 7.5 %collective-permute-start.9 = (bf16[16,32,256]{2,1,0:T(8,128)(2,1)S(1)}, bf16[16,32,256]{2,1,0:T(8,128)(2,1)S(1)}, u32[]{:S(2)}, u32[]{:S(2)}) collective-permute-start(bf16[16,32,256]{2,1,0:T(8,128)(2,1)S(1)} %collective-permute-done.8.refs_6_), channel_id=1, source_target_pairs={{0,8},{8,0},{16,24},{24,16},{32,40},{40,32},{48,56},{56,48},{64,72... | collective-permute-start | bytes 786440 | tf_op jit(solution)/shard_map/ppermute | solution.py:321
  79.7 7.3 %collective-permute-start.14 = (bf16[16,32,256]{2,1,0:T(8,128)(2,1)S(1)}, bf16[16,32,256]{2,1,0:T(8,128)(2,1)S(1)}, u32[]{:S(2)}, u32[]{:S(2)}) collective-permute-start(bf16[16,32,256]{2,1,0:T(8,128)(2,1)S(1)} %collective-permute-done.4.refs_2_), channel_id=1, source_target_pairs={{0,48},{8,56},{16,0},{24,8},{32,16},{40,24},{48,32},{56,40},{64,11... | collective-permute-start | bytes 786440 | tf_op jit(solution)/shard_map/ppermute | solution.py:321
  82.8 7.4 %collective-permute-start.12 = (bf16[16,32,256]{2,1,0:T(8,128)(2,1)S(1)}, bf16[16,32,256]{2,1,0:T(8,128)(2,1)S(1)}, u32[]{:S(2)}, u32[]{:S(2)}) collective-permute-start(bf16[16,32,256]{2,1,0:T(8,128)(2,1)S(1)} %collective-permute-done.4.refs_2_), channel_id=1, source_target_pairs={{0,16},{8,24},{16,32},{24,40},{32,48},{40,56},{48,0},{56,8},{64,80... | collective-permute-start | bytes 786440 | tf_op jit(solution)/shard_map/ppermute | solution.py:321
  83.5 9.2 %collective-permute-start.5 = (bf16[16,32,256]{2,1,0:T(8,128)(2,1)S(1)}, bf16[16,32,256]{2,1,0:T(8,128)(2,1)S(1)}, u32[]{:S(2)}, u32[]{:S(2)}) collective-permute-start(bf16[16,32,256]{2,1,0:T(8,128)(2,1)S(1)} %collective-permute-done.4.refs_2_), channel_id=1, source_target_pairs={{0,8},{8,0},{16,24},{24,16},{32,40},{40,32},{48,56},{56,48},{64,72... | collective-permute-start | bytes 786440 | tf_op jit(solution)/shard_map/ppermute | solution.py:321
  85.4 7.3 %collective-permute-start.7 = (bf16[16,32,256]{2,1,0:T(8,128)(2,1)S(1)}, bf16[16,32,256]{2,1,0:T(8,128)(2,1)S(1)}, u32[]{:S(2)}, u32[]{:S(2)}) collective-permute-start(bf16[16,32,256]{2,1,0:T(8,128)(2,1)S(1)} %collective-permute-done.6.refs_4_), channel_id=1, source_target_pairs={{0,8},{8,0},{16,24},{24,16},{32,40},{40,32},{48,56},{56,48},{64,72... | collective-permute-start | bytes 786440 | tf_op jit(solution)/shard_map/ppermute | solution.py:321
  85.5 7.2 %collective-permute-start.17 = (bf16[16,32,256]{2,1,0:T(8,128)(2,1)S(1)}, bf16[16,32,256]{2,1,0:T(8,128)(2,1)S(1)}, u32[]{:S(2)}, u32[]{:S(2)}) collective-permute-start(bf16[16,32,256]{2,1,0:T(8,128)(2,1)S(1)} %collective-permute-done.16.refs_14_), channel_id=1, source_target_pairs={{0,8},{8,0},{16,24},{24,16},{32,40},{40,32},{48,56},{56,48},{64,72... | collective-permute-start | bytes 786440 | tf_op jit(solution)/shard_map/ppermute | solution.py:321
  87.1 5.7 %collective-permute-start.15 = (bf16[16,32,256]{2,1,0:T(8,128)(2,1)S(1)}, bf16[16,32,256]{2,1,0:T(8,128)(2,1)S(1)}, u32[]{:S(2)}, u32[]{:S(2)}) collective-permute-start(bf16[16,32,256]{2,1,0:T(8,128)(2,1)S(1)} %collective-permute-done.14.refs_12_), channel_id=1, source_target_pairs={{0,8},{8,0},{16,24},{24,16},{32,40},{40,32},{48,56},{56,48},{64,72... | collective-permute-start | bytes 786440 | tf_op jit(solution)/shard_map/ppermute | solution.py:321
  90.2 3.7 %collective-permute-start.13 = (bf16[16,32,256]{2,1,0:T(8,128)(2,1)S(1)}, bf16[16,32,256]{2,1,0:T(8,128)(2,1)S(1)}, u32[]{:S(2)}, u32[]{:S(2)}) collective-permute-start(bf16[16,32,256]{2,1,0:T(8,128)(2,1)S(1)} %collective-permute-done.12.refs_10_), channel_id=1, source_target_pairs={{0,8},{8,0},{16,24},{24,16},{32,40},{40,32},{48,56},{56,48},{64,72... | collective-permute-start | bytes 786440 | tf_op jit(solution)/shard_map/ppermute | solution.py:321

commit v2 on v1

--- a/solution.py
+++ b/solution.py
@@ -147,7 +147,20 @@
 
 
 def filter_kernel(
-    got_ref, taps_ref, bias_ref, turn_hbm, inner_hbm, spec_ref, time_ref, mid_ref, half_ref, turn_ref, inner_ref, sems
+    got_ref,
+    taps_ref,
+    bias_ref,
+    turn_hbm,
+    inner_hbm,
+    spec_hbm,
+    time_ref,
+    mid_ref,
+    half_ref,
+    turn_ref,
+    inner_ref,
+    sems,
+    spec_ref,
+    out_sems,
 ):
     turn_copy, inner_copy = fetch((turn_hbm, inner_hbm), (turn_ref, inner_ref), sems)
     twr_ref, twi_ref, ahead, back = turn_ref.at[0], turn_ref.at[1], inner_ref.at[0], inner_ref.at[1]
@@ -174,32 +187,24 @@
     outer_back(mid_ref, time_ref, half_ref, twr_ref, twi_ref)
     outer_ahead(time_ref, mid_ref, half_ref, twr_ref, twi_ref)
 
-    def finish(ks):
+    copies = []
+    for j in range(OUTER // 8):
+        ks = slice(8 * j, 8 * j + 8)
         spec_ref[ks] = product(flat(mid_ref[ks]), ahead).reshape(8, 32, 2 * INNER)
-
-    chunks(finish)
+        copies.append(pltpu.make_async_copy(spec_ref.at[ks], spec_hbm.at[ks], out_sems.at[j]))
+        copies[-1].start()
+    for copy in copies:
+        copy.wait()
 
 
 def signal_kernel(
-    normed_ref,
-    got_ref,
-    spec_any,
-    turn_hbm,
-    inner_hbm,
-    mixed_ref,
-    time_ref,
-    mid_ref,
-    half_ref,
-    turn_ref,
-    inner_ref,
-    sems,
-    spec_ref,
+    got_ref, spec_hbm, turn_hbm, inner_hbm, mixed_ref, time_ref, mid_ref, half_ref, turn_ref, inner_ref, sems, spec_ref
 ):
-    copies = fetch((turn_hbm, inner_hbm, spec_any), (turn_ref, inner_ref, spec_ref), sems)
+    copies = fetch((turn_hbm, inner_hbm, spec_hbm), (turn_ref, inner_ref, spec_ref), sems)
     twr_ref, twi_ref, ahead, back = turn_ref.at[0], turn_ref.at[1], inner_ref.at[0], inner_ref.at[1]
     for b in range(16):
         for h in range(2):
-            time_ref[2 * b + h] = normed_ref[b, :, h * INNER : (h + 1) * INNER].astype(F32)
+            time_ref[2 * b + h] = got_ref[b, 0:32, h * INNER : (h + 1) * INNER].astype(F32)
     copies[0].wait()
     outer_ahead(time_ref, mid_ref, half_ref, twr_ref, twi_ref)
     copies[1].wait()
@@ -251,62 +256,92 @@
 def filter_spectrum(got, taps, bias, consts):
     return pl.pallas_call(
         filter_kernel,
-        out_shape=jax.ShapeDtypeStruct((OUTER, 32, 2 * INNER), F32),
+        out_shape=pltpu.HBM((OUTER, 32, 2 * INNER), F32),
         in_specs=vmem(3) + hbm(2),
-        out_specs=vmem(1)[0],
-        scratch_shapes=SCRATCH,
+        out_specs=hbm(1)[0],
+        scratch_shapes=[*SCRATCH, pltpu.VMEM((OUTER, 32, 2 * INNER), F32), pltpu.SemaphoreType.DMA((4,))],
         cost_estimate=pl.CostEstimate(flops=2_000_000_000, bytes_accessed=3_000_000, transcendentals=0),
         compiler_params=limit(8),
         name="filter_spectrum",
     )(got, taps, bias, *[stay(value) for value in consts])
 
 
-def gated_convolution(normed, got, spec, consts):
+def gated_convolution(got, spec, consts):
     return pl.pallas_call(
         signal_kernel,
         out_shape=jax.ShapeDtypeStruct((16, 32, 256), BF16),
-        in_specs=[*vmem(2), pl.BlockSpec(memory_space=pl.ANY), *hbm(2)],
+        in_specs=vmem(1) + hbm(3),
         out_specs=vmem(1)[0],
         scratch_shapes=[*SCRATCH, pltpu.VMEM((OUTER, 32, 2 * INNER), F32)],
         cost_estimate=pl.CostEstimate(flops=1_000_000_000, bytes_accessed=3_000_000, transcendentals=0),
         compiler_params=limit(8),
-    )(normed, got, stay(spec), *[stay(value) for value in consts])
-
-
-def pack_kernel(hidden_ref, long_ref, gate_ref, up_ref, payload_ref, squares_ref, hidden, sems):
+    )(got, stay(spec), *[stay(value) for value in consts])
+
+
+def pack_kernel(hidden_hbm, long_ref, up_ref, gain_hbm, payload_ref, squares_ref, lifted_ref, hidden, gain_ref, sems):
     chan = lax.axis_index("chan")
-    sources = [long_ref, gate_ref, up_ref.at[:, pl.ds(pl.multiple_of(chan * 32, 32), 32), :]]
-    copies = [pltpu.make_async_copy(hidden_ref, hidden, sems.at[3])]
-    for i, source in enumerate(sources):
-        copies.append(pltpu.make_async_copy(source, payload_ref.at[:, 32 * i : 32 * i + 32, :], sems.at[i]))
-    for copy in copies:
-        copy.start()
+    own_up = up_ref.at[:, pl.ds(pl.multiple_of(chan * 32, 32), 32), :]
+    targets = [gain_ref, hidden, payload_ref.at[:, 0:32, :], payload_ref.at[:, 32:64, :]]
+    copies = fetch([gain_hbm, hidden_hbm, long_ref, own_up], targets, sems)
     copies[0].wait()
+    gains = [jnp.broadcast_to(gain_ref[q : q + 1, :], (INNER, INNER)).T for q in range(4)]
+    copies[1].wait()
     total = jnp.zeros((8, 256), F32)
     for b in range(16):
         states = hidden[b].astype(F32)
         powers = states * states
         for r in range(4):
             total = total + powers[8 * r : 8 * r + 8]
+        gain = gains[b // 4][32 * (b % 4) : 32 * (b % 4) + 32]
+        lifted_ref[b] = states * jnp.concatenate([gain, gain], axis=1)
     squares_ref[...] = total
-    for copy in copies[1:]:
+    for copy in copies[2:]:
         copy.wait()
+
+
+def norm_kernel(lifted_ref, s0, s1, s2, s3, gate_hbm, payload_ref, sems):
+    (copy,) = fetch([gate_hbm], [payload_ref.at[:, 32:64, :]], sems)
+    squares = (s0[...] + s1[...]) + (s2[...] + s3[...])
+    scale = lax.rsqrt(jnp.sum(squares, axis=0, keepdims=True) / D + EPSILON)
+    for b in range(16):
+        payload_ref[b, 0:32, :] = (lifted_ref[b] * scale).astype(BF16)
+    copy.wait()
 
 
 def limit(mib):
     return pltpu.CompilerParams(vmem_limit_bytes=mib * 2**20)
 
 
-def pack(hidden, long_filter, gate, upstream):
+def pack(hidden, long_filter, upstream, gain):
     return pl.pallas_call(
         pack_kernel,
-        out_shape=(jax.ShapeDtypeStruct((16, 96, 256), BF16), jax.ShapeDtypeStruct((8, 256), F32)),
+        out_shape=(
+            jax.ShapeDtypeStruct((16, 64, 256), BF16),
+            jax.ShapeDtypeStruct((8, 256), F32),
+            jax.ShapeDtypeStruct((16, 32, 256), F32),
+        ),
         in_specs=hbm(4),
-        out_specs=tuple(vmem(2)),
-        scratch_shapes=[pltpu.VMEM((16, 32, 256), BF16), pltpu.SemaphoreType.DMA((4,))],
+        out_specs=tuple(vmem(3)),
+        scratch_shapes=[
+            pltpu.VMEM((16, 32, 256), BF16),
+            pltpu.VMEM((4, INNER), F32),
+            pltpu.SemaphoreType.DMA((4,)),
+        ],
         compiler_params=limit(6),
         name="pack",
-    )(*[stay(value) for value in (hidden, long_filter, gate, upstream)])
+    )(stay(hidden), stay(long_filter), stay(upstream), stay(gain))
+
+
+def normalise(lifted, squares, gate):
+    return pl.pallas_call(
+        norm_kernel,
+        out_shape=jax.ShapeDtypeStruct((16, 64, 256), BF16),
+        in_specs=vmem(5) + hbm(1),
+        out_specs=vmem(1)[0],
+        scratch_shapes=[pltpu.SemaphoreType.DMA((1,))],
+        compiler_params=limit(6),
+        name="normalise",
+    )(lifted, *squares, stay(gate))
 
 
 def place_of(s):
@@ -395,18 +430,18 @@
 
 def step(hidden_states, norm_gain, short_filter, long_filter, long_bias, gate_stream, upstream):
     consts = [jnp.asarray(table) for table in tables()]
-    blocks = [value.reshape(16, 32, 256) for value in (hidden_states, long_filter, gate_stream)]
-    payload, squares = pack(*blocks, upstream.reshape(16, 256, 256))
+    hidden, filt, gate = [value.reshape(16, 32, 256) for value in (hidden_states, long_filter, gate_stream)]
+    payload, squares, lifted = pack(hidden, filt, upstream.reshape(16, 256, 256), norm_gain.reshape(4, INNER))
     squares = squares + over_chan(squares, 1, 0)
     got = exchange(payload, "seq")
-    squares = squares + over_chan(squares, 0, 1)
-    squares = squares + over_chan(squares, 0, 2)
-    scale = lax.rsqrt(jnp.sum(squares, axis=0) / D + EPSILON)
-    normed = (hidden_states.astype(F32) * scale[None, :] * norm_gain[:, None]).astype(BF16)
-    normed = exchange(normed.reshape(16, 32, 256), "seq")
+    parts = [squares]
+    for dy in (1, 3, 2):
+        parts.append(over_chan(squares, 0, dy))
+    payload = normalise(lifted, parts, gate)
+    signal = exchange(payload, "seq")
     spec = filter_spectrum(got, short_filter, long_bias[None, :], consts)
-    up = gather_chan(got[:, 64:96])
-    mixed = gated_convolution(normed, got, spec, consts)
+    up = gather_chan(got[:, 32:64])
+    mixed = gated_convolution(signal, spec, consts)
     return weight_gradient(gather_seq(mixed), up)
 
 

time: 96.5 us -> 93.6 us (0.970)
  starting transfers between devices: 60.6 us -> 53.1 us
  waiting for transfers between devices: 17.9 us -> 22.6 us
  Pallas kernels: 15 us -> 16.7 us
  local copies, waits for them, and re-layouts: 1.01 us -> 0.03 us
    ppermute x15, waiting for transfers between devices: 6.62 us -> 12.9 us  [over_seq(): return lax.ppermute(value, 'seq', pairs)]
    ppermute x15, starting transfers between devices: 25.9 us -> 20.8 us  [over_seq(): return lax.ppermute(value, 'seq', pairs)]
    ppermute x10 -> x11, waiting for transfers between devices: 10.6 us -> 7.04 us  [over_chan(): return lax.ppermute(value, 'chan', pairs)]
    all_to_all x2, waiting for transfers between devices: 0.71 us -> 2.7 us  [exchange(): return lax.all_to_all(value, axis, split_axis=0, concat_axis=0, tiled=True)]
    pallas_call x2 -> x3, Pallas kernels: 8.26 us -> 10 us  [the longest x1 6.3 us: filter_spectrum(): pl.pallas_call(filter_kernel, out_shape=pltpu.HBM((OUTER, 32, 2 * INNER),...]
    all_to_all x2, starting transfers between devices: 24.6 us -> 23.2 us  [exchange(): return lax.all_to_all(value, axis, split_axis=0, concat_axis=0, tiled=True)]
    ppermute x10 -> x11, starting transfers between devices: 10.1 us -> 9.03 us  [over_chan(): return lax.ppermute(value, 'chan', pairs)]
    unnamed x10 -> x4, local copies, waits for them, and re-layouts: 0.99 us -> 0.01 us
  transfers between devices with their start and end apart: 27 -> 28, of which waited for: 9 -> 11; matrix products, arithmetic and copies ran while one was open for 1% -> 0% of each run, Pallas kernels for 11% -> 13%
where the time goes in v2:
time: 93.6 us; the launch traced here: 93.2 us
  starting transfers between devices  53.1 us (57%)
  waiting for transfers between devices  22.6 us (24%)
  Pallas kernels  16.7 us (18%)
    all_to_all x2, starting transfers between devices, exchange(): return lax.all_to_all(value, axis, split_axis=0, concat_axis=0, tiled=True)  23.2 us
    ppermute x15, starting transfers between devices, over_seq(): return lax.ppermute(value, 'seq', pairs)  20.8 us
    ppermute x15, waiting for transfers between devices, over_seq(): return lax.ppermute(value, 'seq', pairs)  12.9 us
    ppermute x11, starting transfers between devices, over_chan(): return lax.ppermute(value, 'chan', pairs)  9.03 us
    ppermute x11, waiting for transfers between devices, over_chan(): return lax.ppermute(value, 'chan', pairs)  7.04 us
    pallas_call x1, Pallas kernels, filter_spectrum(): pl.pallas_call(filter_kernel, out_shape=pltpu.HBM((OUTER, 32, 2 * INNER),...  6.3 us
    pallas_call x1, Pallas kernels, gated_convolution(): pl.pallas_call(signal_kernel, out_shape=jax.ShapeDtypeStruct((16, 32, 256...  4.43 us
    all_to_all x2, waiting for transfers between devices, exchange(): return lax.all_to_all(value, axis, split_axis=0, concat_axis=0, tiled=True)  2.7 us
  transfers between devices with their start and end apart: 28, of which 11 were waited for; matrix products, arithmetic and copies ran while one was open for 0% of the time, Pallas kernels for 13%

profile of v2, /device:TPU:1, one launch (start us, length us, event | category | flops | bytes accessed | tf_op | source)
XLA Modules:
  0.0 93.2 jit_solution(10007261772176148595)
XLA Ops:
  0.6 2.0 %pack.1 = (bf16[16,64,256]{2,1,0:T(8,128)(2,1)}, f32[8,256]{1,0:T(8,128)S(1)}, f32[16,32,256]{2,1,0:T(8,128)S(1)}) custom-call(bf16[16,32,256]{2,1,0:T(8,128)(2,1)} %bitcast.8, bf16[16,32,256]{2,1,0:T(8,128)(2,1)} %bitcast.9, bf16[16,256,256]{2,1,0:T(8,128)(2,1)} %bitcast.7, f32[4,128]{1,0:T(4,128)} %bitcast.11), custom_call_target="tpu_custom_call" | custom-call | tf_op jit(solution)/shard_map/pack/pallas_call | solution.py:316
  2.6 0.0 copy-start
  2.6 0.0 copy-start.1
  2.6 9.3 %all-to-all-start.1 = ((bf16[16,64,256]{2,1,0:T(8,128)(2,1)}), bf16[16,64,256]{2,1,0:T(8,128)(2,1)S(1)}, u32[]{:S(2)}, u32[]{:S(2)}) async-start(bf16[16,64,256]{2,1,0:T(8,128)(2,1)} %get-tuple-element.7), calls=%async_computation.1 | async-start | bytes 1048576 | tf_op jit(solution)/shard_map/all_to_all | solution.py:428
  11.9 0.7 collective-permute-start
  12.6 2.5 %collective-permute-done = f32[8,256]{1,0:T(8,128)S(1)} collective-permute-done((f32[8,256]{1,0:T(8,128)S(1)}, f32[8,256]{1,0:T(8,128)S(1)}, u32[]{:S(2)}, u32[]{:S(2)}) %collective-permute-start) | collective-permute-done | bytes 8224 | tf_op jit(solution)/shard_map/ppermute | solution.py:361
  15.2 2.9 %collective-permute-start.3 = (f32[8,256]{1,0:T(8,128)S(1)}, f32[8,256]{1,0:T(8,128)S(1)}, u32[]{:S(2)}, u32[]{:S(2)}) collective-permute-start(f32[8,256]{1,0:T(8,128)S(1)} %add.3.s0), channel_id=1, source_target_pairs={{0,2},{1,3},{2,0},{3,1},{4,6},{5,7},{6,4},{7,5},{8,10},{9,11},{10,... | collective-permute-start | bytes 24584 | tf_op jit(solution)/shard_map/ppermute | solution.py:361
  18.1 0.8 collective-permute-start.2
  18.8 0.7 collective-permute-start.1
  19.5 1.3 %collective-permute-done.2.s2 = f32[8,256]{1,0:T(8,128)S(1)} collective-permute-done((f32[8,256]{1,0:T(8,128)S(1)}, f32[8,256]{1,0:T(8,128)S(1)}, u32[]{:S(2)}, u32[]{:S(2)}) %collective-permute-start.2) | collective-permute-done | bytes 8224 | tf_op jit(solution)/shard_map/ppermute | solution.py:361
  20.9 2.0 %collective-permute-done.1.s1 = f32[8,256]{1,0:T(8,128)S(1)} collective-permute-done((f32[8,256]{1,0:T(8,128)S(1)}, f32[8,256]{1,0:T(8,128)S(1)}, u32[]{:S(2)}, u32[]{:S(2)}) %collective-permute-start.1) | collective-permute-done | bytes 8224 | tf_op jit(solution)/shard_map/ppermute | solution.py:361
  22.9 1.8 %normalise.1 = bf16[16,64,256]{2,1,0:T(8,128)(2,1)} custom-call(f32[16,32,256]{2,1,0:T(8,128)S(1)} %get-tuple-element.5.lifted_ref, f32[8,256]{1,0:T(8,128)S(1)} %add.3.s0, f32[8,256]{1,0:T(8,128)S(1)} %collective-permute-done.1.s1, f32[8,256]{1,0:T(8,128)S(1)} %collective-permute-done.2.s2, f32[8,256]{1,0:T(8,128)S(1)} %collective-permute-done.3.s3, ...), custom_call_target="tpu_custom_call" | custom-call | tf_op jit(solution)/shard_map/normalise/pallas_call | solution.py:336
  24.6 14.0 %all-to-all-start = ((bf16[16,64,256]{2,1,0:T(8,128)(2,1)}), bf16[16,64,256]{2,1,0:T(8,128)(2,1)S(1)}, u32[]{:S(2)}, u32[]{:S(2)}) async-start(bf16[16,64,256]{2,1,0:T(8,128)(2,1)} %normalise.1), calls=%async_computation | async-start | bytes 1048576 | tf_op jit(solution)/shard_map/all_to_all | solution.py:428
  38.6 0.3 collective-permute-start.22
  38.9 1.7 %collective-permute-start.21 = (bf16[16,32,256]{2,1,0:T(8,128)(2,1)S(1)}, bf16[16,32,256]{2,1,0:T(8,128)(2,1)S(1)}, u32[]{:S(2)}, u32[]{:S(2)}) collective-permute-start(bf16[16,32,256]{2,1,0:T(8,128)(2,1)S(1)} %slice.4.refs_16_), channel_id=1, source_target_pairs={{0,3},{1,0},{2,1},{3,2},{4,7},{5,4},{6,5},{7,6},{8,11},{9,8},{10,9... | collective-permute-start | bytes 786440 | tf_op jit(solution)/shard_map/ppermute | solution.py:361
  40.6 0.0 collective-permute-start.19
  40.6 6.3 %filter_spectrum.1.spec_hbm = f32[32,32,256]{2,1,0:T(8,128)} custom-call(bf16[16,64,256]{2,1,0:T(8,128)(2,1)S(1)} %all-to-all-done.1.got_ref, f32[512,128]{1,0:T(8,128)S(1)} %copy-done, f32[1,512]{1,0:T(1,128)S(1)} %bitcast.6, f32[2,32,128]{2,1,0:T(8,128)} %constant.4.clone.turn_hbm, bf16[2,768,256]{2,1,0:T(8,128)(2,1)} %constant.5.clone.inner_hbm), custom_call_target="tpu_custom_call" | custom-call | flops 2000000000 | bytes 3000000 | tf_op jit(solution)/shard_map/filter_spectrum/pallas_call | solution.py:257
  46.9 2.7 %all-to-all-done.got_ref = bf16[16,64,256]{2,1,0:T(8,128)(2,1)S(1)} async-done(((bf16[16,64,256]{2,1,0:T(8,128)(2,1)}), bf16[16,64,256]{2,1,0:T(8,128)(2,1)S(1)}, u32[]{:S(2)}, u32[]{:S(2)}) %all-to-all-start) | async-done | bytes 524320 | tf_op jit(solution)/shard_map/all_to_all | solution.py:428
  49.6 4.4 %shard_map.104.refs_0_ = bf16[16,32,256]{2,1,0:T(8,128)(2,1)S(1)} custom-call(bf16[16,64,256]{2,1,0:T(8,128)(2,1)S(1)} %all-to-all-done.got_ref, f32[32,32,256]{2,1,0:T(8,128)} %filter_spectrum.1.spec_hbm, f32[2,32,128]{2,1,0:T(8,128)} %constant.4.clone.turn_hbm, bf16[2,768,256]{2,1,0:T(8,128)(2,1)} %constant.5.clone.inner_hbm), custom_call_target="tpu_custom_call" | custom-call | flops 1000000000 | bytes 3000000 | tf_op jit(solution)/shard_map/pallas_call | solution.py:270
  54.0 2.1 %collective-permute-start.11 = (bf16[16,32,256]{2,1,0:T(8,128)(2,1)S(1)}, bf16[16,32,256]{2,1,0:T(8,128)(2,1)S(1)}, u32[]{:S(2)}, u32[]{:S(2)}) collective-permute-start(bf16[16,32,256]{2,1,0:T(8,128)(2,1)S(1)} %shard_map.104.refs_0_), channel_id=1, source_target_pairs={{0,32},{8,40},{16,48},{24,56},{32,0},{40,8},{48,16},{56,24},{64,96... | collective-permute-start | bytes 786440 | tf_op jit(solution)/shard_map/ppermute | solution.py:356
  56.2 0.9 collective-permute-start.9
  57.1 0.6 collective-permute-start.7
  57.7 0.0 collective-permute-done.20.refs_18_
  57.7 0.9 collective-permute-start.5
  58.6 2.4 %collective-permute-start.4 = (bf16[16,32,256]{2,1,0:T(8,128)(2,1)S(1)}, bf16[16,32,256]{2,1,0:T(8,128)(2,1)S(1)}, u32[]{:S(2)}, u32[]{:S(2)}) collective-permute-start(bf16[16,32,256]{2,1,0:T(8,128)(2,1)S(1)} %shard_map.104.refs_0_), channel_id=1, source_target_pairs={{0,8},{8,0},{16,24},{24,16},{32,40},{40,32},{48,56},{56,48},{64,72... | collective-permute-start | bytes 786440 | tf_op jit(solution)/shard_map/ppermute | solution.py:356
  61.0 1.3 %collective-permute-done.11.refs_8_ = bf16[16,32,256]{2,1,0:T(8,128)(2,1)S(1)} collective-permute-done((bf16[16,32,256]{2,1,0:T(8,128)(2,1)S(1)}, bf16[16,32,256]{2,1,0:T(8,128)(2,1)S(1)}, u32[]{:S(2)}, u32[]{:S(2)}) %collective-permute-start.11) | collective-permute-done | bytes 262176 | tf_op jit(solution)/shard_map/ppermute | solution.py:356
  62.3 1.4 %collective-permute-start.25 = (bf16[16,32,256]{2,1,0:T(8,128)(2,1)S(1)}, bf16[16,32,256]{2,1,0:T(8,128)(2,1)S(1)}, u32[]{:S(2)}, u32[]{:S(2)}) collective-permute-start(bf16[16,32,256]{2,1,0:T(8,128)(2,1)S(1)} %collective-permute-done.19.refs_17_), channel_id=1, source_target_pairs={{0,2},{1,3},{2,0},{3,1},{4,6},{5,7},{6,4},{7,5},{8,10},{9,11},{10,... | collective-permute-start | bytes 786440 | tf_op jit(solution)/shard_map/ppermute | solution.py:361
  63.8 4.7 %collective-permute-done.9.refs_6_ = bf16[16,32,256]{2,1,0:T(8,128)(2,1)S(1)} collective-permute-done((bf16[16,32,256]{2,1,0:T(8,128)(2,1)S(1)}, bf16[16,32,256]{2,1,0:T(8,128)(2,1)S(1)}, u32[]{:S(2)}, u32[]{:S(2)}) %collective-permute-start.9) | collective-permute-done | bytes 262176 | tf_op jit(solution)/shard_map/ppermute | solution.py:356
  68.5 0.1 collective-permute-start.24
  68.6 0.9 %collective-permute-done.7.refs_4_ = bf16[16,32,256]{2,1,0:T(8,128)(2,1)S(1)} collective-permute-done((bf16[16,32,256]{2,1,0:T(8,128)(2,1)S(1)}, bf16[16,32,256]{2,1,0:T(8,128)(2,1)S(1)}, u32[]{:S(2)}, u32[]{:S(2)}) %collective-permute-start.7) | collective-permute-done | bytes 262176 | tf_op jit(solution)/shard_map/ppermute | solution.py:356
  69.6 0.4 collective-permute-start.23
  70.0 0.0 collective-permute-done.5.refs_2_
  70.0 1.5 %collective-permute-start.17 = (bf16[16,32,256]{2,1,0:T(8,128)(2,1)S(1)}, bf16[16,32,256]{2,1,0:T(8,128)(2,1)S(1)}, u32[]{:S(2)}, u32[]{:S(2)}) collective-permute-start(bf16[16,32,256]{2,1,0:T(8,128)(2,1)S(1)} %collective-permute-done.11.refs_8_), channel_id=1, source_target_pairs={{0,64},{8,72},{16,80},{24,88},{32,96},{40,104},{48,112},{56,120},{... | collective-permute-start | bytes 786440 | tf_op jit(solution)/shard_map/ppermute | solution.py:356
  71.5 0.0 collective-permute-done.4.refs_1_
  71.5 2.1 %collective-permute-start.12 = (bf16[16,32,256]{2,1,0:T(8,128)(2,1)S(1)}, bf16[16,32,256]{2,1,0:T(8,128)(2,1)S(1)}, u32[]{:S(2)}, u32[]{:S(2)}) collective-permute-start(bf16[16,32,256]{2,1,0:T(8,128)(2,1)S(1)} %collective-permute-done.11.refs_8_), channel_id=1, source_target_pairs={{0,8},{8,0},{16,24},{24,16},{32,40},{40,32},{48,56},{56,48},{64,72... | collective-permute-start | bytes 786440 | tf_op jit(solution)/shard_map/ppermute | solution.py:356
  73.6 0.0 collective-permute-done.25.refs_23_
  73.6 3.0 %collective-permute-start.10 = (bf16[16,32,256]{2,1,0:T(8,128)(2,1)S(1)}, bf16[16,32,256]{2,1,0:T(8,128)(2,1)S(1)}, u32[]{:S(2)}, u32[]{:S(2)}) collective-permute-start(bf16[16,32,256]{2,1,0:T(8,128)(2,1)S(1)} %collective-permute-done.9.refs_6_), channel_id=1, source_target_pairs={{0,8},{8,0},{16,24},{24,16},{32,40},{40,32},{48,56},{56,48},{64,72... | collective-permute-start | bytes 786440 | tf_op jit(solution)/shard_map/ppermute | solution.py:356
  76.6 2.0 %collective-permute-start.15 = (bf16[16,32,256]{2,1,0:T(8,128)(2,1)S(1)}, bf16[16,32,256]{2,1,0:T(8,128)(2,1)S(1)}, u32[]{:S(2)}, u32[]{:S(2)}) collective-permute-start(bf16[16,32,256]{2,1,0:T(8,128)(2,1)S(1)} %collective-permute-done.5.refs_2_), channel_id=1, source_target_pairs={{0,48},{8,56},{16,0},{24,8},{32,16},{40,24},{48,32},{56,40},{64,11... | collective-permute-start | bytes 786440 | tf_op jit(solution)/shard_map/ppermute | solution.py:356
  78.6 1.2 %collective-permute-done.23.refs_21_ = bf16[16,32,256]{2,1,0:T(8,128)(2,1)S(1)} collective-permute-done((bf16[16,32,256]{2,1,0:T(8,128)(2,1)S(1)}, bf16[16,32,256]{2,1,0:T(8,128)(2,1)S(1)}, u32[]{:S(2)}, u32[]{:S(2)}) %collective-permute-start.23) | collective-permute-done | bytes 262176 | tf_op jit(solution)/shard_map/ppermute | solution.py:361
  79.8 1.2 %collective-permute-start.6 = (bf16[16,32,256]{2,1,0:T(8,128)(2,1)S(1)}, bf16[16,32,256]{2,1,0:T(8,128)(2,1)S(1)}, u32[]{:S(2)}, u32[]{:S(2)}) collective-permute-start(bf16[16,32,256]{2,1,0:T(8,128)(2,1)S(1)} %collective-permute-done.5.refs_2_), channel_id=1, source_target_pairs={{0,8},{8,0},{16,24},{24,16},{32,40},{40,32},{48,56},{56,48},{64,72... | collective-permute-start | bytes 786440 | tf_op jit(solution)/shard_map/ppermute | solution.py:356
  81.0 0.1 collective-permute-start.8
  81.1 0.4 collective-permute-start.18
  81.6 2.2 %collective-permute-done.15.refs_12_ = bf16[16,32,256]{2,1,0:T(8,128)(2,1)S(1)} collective-permute-done((bf16[16,32,256]{2,1,0:T(8,128)(2,1)S(1)}, bf16[16,32,256]{2,1,0:T(8,128)(2,1)S(1)}, u32[]{:S(2)}, u32[]{:S(2)}) %collective-permute-start.15) | collective-permute-done | bytes 262176 | tf_op jit(solution)/shard_map/ppermute | solution.py:356
  83.8 1.6 %collective-permute-start.16 = (bf16[16,32,256]{2,1,0:T(8,128)(2,1)S(1)}, bf16[16,32,256]{2,1,0:T(8,128)(2,1)S(1)}, u32[]{:S(2)}, u32[]{:S(2)}) collective-permute-start(bf16[16,32,256]{2,1,0:T(8,128)(2,1)S(1)} %collective-permute-done.15.refs_12_), channel_id=1, source_target_pairs={{0,8},{8,0},{16,24},{24,16},{32,40},{40,32},{48,56},{56,48},{64,72... | collective-permute-start | bytes 786440 | tf_op jit(solution)/shard_map/ppermute | solution.py:356
  85.4 2.4 %collective-permute-done.13.refs_10_ = bf16[16,32,256]{2,1,0:T(8,128)(2,1)S(1)} collective-permute-done((bf16[16,32,256]{2,1,0:T(8,128)(2,1)S(1)}, bf16[16,32,256]{2,1,0:T(8,128)(2,1)S(1)}, u32[]{:S(2)}, u32[]{:S(2)}) %collective-permute-start.13) | collective-permute-done | bytes 262176 | tf_op jit(solution)/shard_map/ppermute | solution.py:356
  87.8 1.9 %collective-permute-start.14 = (bf16[16,32,256]{2,1,0:T(8,128)(2,1)S(1)}, bf16[16,32,256]{2,1,0:T(8,128)(2,1)S(1)}, u32[]{:S(2)}, u32[]{:S(2)}) collective-permute-start(bf16[16,32,256]{2,1,0:T(8,128)(2,1)S(1)} %collective-permute-done.13.refs_10_), channel_id=1, source_target_pairs={{0,8},{8,0},{16,24},{24,16},{32,40},{40,32},{48,56},{56,48},{64,72... | collective-permute-start | bytes 786440 | tf_op jit(solution)/shard_map/ppermute | solution.py:356
  89.7 1.1 %collective-permute-done.14.refs_11_ = bf16[16,32,256]{2,1,0:T(8,128)(2,1)S(1)} collective-permute-done((bf16[16,32,256]{2,1,0:T(8,128)(2,1)S(1)}, bf16[16,32,256]{2,1,0:T(8,128)(2,1)S(1)}, u32[]{:S(2)}, u32[]{:S(2)}) %collective-permute-start.14) | collective-permute-done | bytes 262176 | tf_op jit(solution)/shard_map/ppermute | solution.py:356
  90.9 2.3 %weight_gradient.1 = (bf16[512,256]{1,0:T(8,128)(2,1)}, f32[256,512]{1,0:T(8,128)}) custom-call(bf16[16,32,256]{2,1,0:T(8,128)(2,1)S(1)} %shard_map.104.refs_0_, bf16[16,32,256]{2,1,0:T(8,128)(2,1)S(1)} %collective-permute-done.4.refs_1_, bf16[16,32,256]{2,1,0:T(8,128)(2,1)S(1)} %collective-permute-done.5.refs_2_, ...), custom_call_target="tpu_custom_call" | custom-call | flops 1000000000 | bytes 7000000 | tf_op jit(solution)/shard_map/weight_gradient/pallas_call | solution.py:415
  (19 shorter events, 0.1 us)
Async XLA Ops:
  2.6 38.0 %copy-start = (f32[512,128]{1,0:T(8,128)S(1)}, f32[512,128]{1,0:T(8,128)}, u32[]{:S(2)}) copy-start(f32[512,128]{1,0:T(8,128)} %taps_ref.1) | copy-start | bytes 786436
  2.6 38.0 %copy-start.1 = (f32[512]{0:T(512)S(1)}, f32[512]{0:T(512)}, u32[]{:S(2)}) copy-start(f32[512]{0:T(512)} %param.13) | copy-start | bytes 6148
  2.6 22.0 %all-to-all-start.1 = ((bf16[16,64,256]{2,1,0:T(8,128)(2,1)}), bf16[16,64,256]{2,1,0:T(8,128)(2,1)S(1)}, u32[]{:S(2)}, u32[]{:S(2)}) async-start(bf16[16,64,256]{2,1,0:T(8,128)(2,1)} %get-tuple-element.7), calls=%async_computation.1 | async-start | bytes 1048576 | tf_op jit(solution)/shard_map/all_to_all | solution.py:428
  11.9 3.3 %collective-permute-start = (f32[8,256]{1,0:T(8,128)S(1)}, f32[8,256]{1,0:T(8,128)S(1)}, u32[]{:S(2)}, u32[]{:S(2)}) collective-permute-start(f32[8,256]{1,0:T(8,128)S(1)} %get-tuple-element.6), channel_id=1, source_target_pairs={{0,4},{1,5},{2,6},{3,7},{4,0},{5,1},{6,2},{7,3},{8,12},{9,13},{10,... | collective-permute-start | bytes 24584 | tf_op jit(solution)/shard_map/ppermute | solution.py:361
  15.2 4.4 %collective-permute-start.3 = (f32[8,256]{1,0:T(8,128)S(1)}, f32[8,256]{1,0:T(8,128)S(1)}, u32[]{:S(2)}, u32[]{:S(2)}) collective-permute-start(f32[8,256]{1,0:T(8,128)S(1)} %add.3.s0), channel_id=1, source_target_pairs={{0,2},{1,3},{2,0},{3,1},{4,6},{5,7},{6,4},{7,5},{8,10},{9,11},{10,... | collective-permute-start | bytes 24584 | tf_op jit(solution)/shard_map/ppermute | solution.py:361
  18.1 2.8 %collective-permute-start.2 = (f32[8,256]{1,0:T(8,128)S(1)}, f32[8,256]{1,0:T(8,128)S(1)}, u32[]{:S(2)}, u32[]{:S(2)}) collective-permute-start(f32[8,256]{1,0:T(8,128)S(1)} %add.3.s0), channel_id=1, source_target_pairs={{0,3},{1,0},{2,1},{3,2},{4,7},{5,4},{6,5},{7,6},{8,11},{9,8},{10,9... | collective-permute-start | bytes 24584 | tf_op jit(solution)/shard_map/ppermute | solution.py:361
  18.8 4.0 %collective-permute-start.1 = (f32[8,256]{1,0:T(8,128)S(1)}, f32[8,256]{1,0:T(8,128)S(1)}, u32[]{:S(2)}, u32[]{:S(2)}) collective-permute-start(f32[8,256]{1,0:T(8,128)S(1)} %add.3.s0), channel_id=1, source_target_pairs={{0,1},{1,2},{2,3},{3,0},{4,5},{5,6},{6,7},{7,4},{8,9},{9,10},{10,1... | collective-permute-start | bytes 24584 | tf_op jit(solution)/shard_map/ppermute | solution.py:361
  24.6 25.0 %all-to-all-start = ((bf16[16,64,256]{2,1,0:T(8,128)(2,1)}), bf16[16,64,256]{2,1,0:T(8,128)(2,1)S(1)}, u32[]{:S(2)}, u32[]{:S(2)}) async-start(bf16[16,64,256]{2,1,0:T(8,128)(2,1)} %normalise.1), calls=%async_computation | async-start | bytes 1048576 | tf_op jit(solution)/shard_map/all_to_all | solution.py:428
  38.6 17.6 %collective-permute-start.22 = (bf16[16,32,256]{2,1,0:T(8,128)(2,1)S(1)}, bf16[16,32,256]{2,1,0:T(8,128)(2,1)S(1)}, u32[]{:S(2)}, u32[]{:S(2)}) collective-permute-start(bf16[16,32,256]{2,1,0:T(8,128)(2,1)S(1)} %slice.4.refs_16_), channel_id=1, source_target_pairs={{0,2},{1,3},{2,0},{3,1},{4,6},{5,7},{6,4},{7,5},{8,10},{9,11},{10,... | collective-permute-start | bytes 786440 | tf_op jit(solution)/shard_map/ppermute | solution.py:361
  38.9 18.2 %collective-permute-start.21 = (bf16[16,32,256]{2,1,0:T(8,128)(2,1)S(1)}, bf16[16,32,256]{2,1,0:T(8,128)(2,1)S(1)}, u32[]{:S(2)}, u32[]{:S(2)}) collective-permute-start(bf16[16,32,256]{2,1,0:T(8,128)(2,1)S(1)} %slice.4.refs_16_), channel_id=1, source_target_pairs={{0,3},{1,0},{2,1},{3,2},{4,7},{5,4},{6,5},{7,6},{8,11},{9,8},{10,9... | collective-permute-start | bytes 786440 | tf_op jit(solution)/shard_map/ppermute | solution.py:361
  40.6 17.1 %collective-permute-start.20 = (bf16[16,32,256]{2,1,0:T(8,128)(2,1)S(1)}, bf16[16,32,256]{2,1,0:T(8,128)(2,1)S(1)}, u32[]{:S(2)}, u32[]{:S(2)}) collective-permute-start(bf16[16,32,256]{2,1,0:T(8,128)(2,1)S(1)} %slice.4.refs_16_), channel_id=1, source_target_pairs={{0,1},{1,2},{2,3},{3,0},{4,5},{5,6},{6,7},{7,4},{8,9},{9,10},{10,1... | collective-permute-start | bytes 786440 | tf_op jit(solution)/shard_map/ppermute | solution.py:361
  40.6 18.0 %collective-permute-start.19 = (bf16[16,32,256]{2,1,0:T(8,128)(2,1)S(1)}, bf16[16,32,256]{2,1,0:T(8,128)(2,1)S(1)}, u32[]{:S(2)}, u32[]{:S(2)}) collective-permute-start(bf16[16,32,256]{2,1,0:T(8,128)(2,1)S(1)} %slice.4.refs_16_), channel_id=1, source_target_pairs={{0,4},{1,5},{2,6},{3,7},{4,0},{5,1},{6,2},{7,3},{8,12},{9,13},{10,... | collective-permute-start | bytes 786440 | tf_op jit(solution)/shard_map/ppermute | solution.py:361
  54.0 8.3 %collective-permute-start.11 = (bf16[16,32,256]{2,1,0:T(8,128)(2,1)S(1)}, bf16[16,32,256]{2,1,0:T(8,128)(2,1)S(1)}, u32[]{:S(2)}, u32[]{:S(2)}) collective-permute-start(bf16[16,32,256]{2,1,0:T(8,128)(2,1)S(1)} %shard_map.104.refs_0_), channel_id=1, source_target_pairs={{0,32},{8,40},{16,48},{24,56},{32,0},{40,8},{48,16},{56,24},{64,96... | collective-permute-start | bytes 786440 | tf_op jit(solution)/shard_map/ppermute | solution.py:356
  56.2 12.3 %collective-permute-start.9 = (bf16[16,32,256]{2,1,0:T(8,128)(2,1)S(1)}, bf16[16,32,256]{2,1,0:T(8,128)(2,1)S(1)}, u32[]{:S(2)}, u32[]{:S(2)}) collective-permute-start(bf16[16,32,256]{2,1,0:T(8,128)(2,1)S(1)} %shard_map.104.refs_0_), channel_id=1, source_target_pairs={{0,48},{8,56},{16,0},{24,8},{32,16},{40,24},{48,32},{56,40},{64,11... | collective-permute-start | bytes 786440 | tf_op jit(solution)/shard_map/ppermute | solution.py:356
  57.1 12.5 %collective-permute-start.7 = (bf16[16,32,256]{2,1,0:T(8,128)(2,1)S(1)}, bf16[16,32,256]{2,1,0:T(8,128)(2,1)S(1)}, u32[]{:S(2)}, u32[]{:S(2)}) collective-permute-start(bf16[16,32,256]{2,1,0:T(8,128)(2,1)S(1)} %shard_map.104.refs_0_), channel_id=1, source_target_pairs={{0,16},{8,24},{16,32},{24,40},{32,48},{40,56},{48,0},{56,8},{64,80... | collective-permute-start | bytes 786440 | tf_op jit(solution)/shard_map/ppermute | solution.py:356
  57.7 12.3 %collective-permute-start.5 = (bf16[16,32,256]{2,1,0:T(8,128)(2,1)S(1)}, bf16[16,32,256]{2,1,0:T(8,128)(2,1)S(1)}, u32[]{:S(2)}, u32[]{:S(2)}) collective-permute-start(bf16[16,32,256]{2,1,0:T(8,128)(2,1)S(1)} %shard_map.104.refs_0_), channel_id=1, source_target_pairs={{0,64},{8,72},{16,80},{24,88},{32,96},{40,104},{48,112},{56,120},{... | collective-permute-start | bytes 786440 | tf_op jit(solution)/shard_map/ppermute | solution.py:356
  58.6 12.9 %collective-permute-start.4 = (bf16[16,32,256]{2,1,0:T(8,128)(2,1)S(1)}, bf16[16,32,256]{2,1,0:T(8,128)(2,1)S(1)}, u32[]{:S(2)}, u32[]{:S(2)}) collective-permute-start(bf16[16,32,256]{2,1,0:T(8,128)(2,1)S(1)} %shard_map.104.refs_0_), channel_id=1, source_target_pairs={{0,8},{8,0},{16,24},{24,16},{32,40},{40,32},{48,56},{56,48},{64,72... | collective-permute-start | bytes 786440 | tf_op jit(solution)/shard_map/ppermute | solution.py:356
  62.3 11.3 %collective-permute-start.25 = (bf16[16,32,256]{2,1,0:T(8,128)(2,1)S(1)}, bf16[16,32,256]{2,1,0:T(8,128)(2,1)S(1)}, u32[]{:S(2)}, u32[]{:S(2)}) collective-permute-start(bf16[16,32,256]{2,1,0:T(8,128)(2,1)S(1)} %collective-permute-done.19.refs_17_), channel_id=1, source_target_pairs={{0,2},{1,3},{2,0},{3,1},{4,6},{5,7},{6,4},{7,5},{8,10},{9,11},{10,... | collective-permute-start | bytes 786440 | tf_op jit(solution)/shard_map/ppermute | solution.py:361
  68.5 8.1 %collective-permute-start.24 = (bf16[16,32,256]{2,1,0:T(8,128)(2,1)S(1)}, bf16[16,32,256]{2,1,0:T(8,128)(2,1)S(1)}, u32[]{:S(2)}, u32[]{:S(2)}) collective-permute-start(bf16[16,32,256]{2,1,0:T(8,128)(2,1)S(1)} %collective-permute-done.19.refs_17_), channel_id=1, source_target_pairs={{0,3},{1,0},{2,1},{3,2},{4,7},{5,4},{6,5},{7,6},{8,11},{9,8},{10,9... | collective-permute-start | bytes 786440 | tf_op jit(solution)/shard_map/ppermute | solution.py:361
  69.6 10.2 %collective-permute-start.23 = (bf16[16,32,256]{2,1,0:T(8,128)(2,1)S(1)}, bf16[16,32,256]{2,1,0:T(8,128)(2,1)S(1)}, u32[]{:S(2)}, u32[]{:S(2)}) collective-permute-start(bf16[16,32,256]{2,1,0:T(8,128)(2,1)S(1)} %collective-permute-done.19.refs_17_), channel_id=1, source_target_pairs={{0,1},{1,2},{2,3},{3,0},{4,5},{5,6},{6,7},{7,4},{8,9},{9,10},{10,1... | collective-permute-start | bytes 786440 | tf_op jit(solution)/shard_map/ppermute | solution.py:361
  70.0 9.8 %collective-permute-start.17 = (bf16[16,32,256]{2,1,0:T(8,128)(2,1)S(1)}, bf16[16,32,256]{2,1,0:T(8,128)(2,1)S(1)}, u32[]{:S(2)}, u32[]{:S(2)}) collective-permute-start(bf16[16,32,256]{2,1,0:T(8,128)(2,1)S(1)} %collective-permute-done.11.refs_8_), channel_id=1, source_target_pairs={{0,64},{8,72},{16,80},{24,88},{32,96},{40,104},{48,112},{56,120},{... | collective-permute-start | bytes 786440 | tf_op jit(solution)/shard_map/ppermute | solution.py:356
  71.5 9.5 %collective-permute-start.12 = (bf16[16,32,256]{2,1,0:T(8,128)(2,1)S(1)}, bf16[16,32,256]{2,1,0:T(8,128)(2,1)S(1)}, u32[]{:S(2)}, u32[]{:S(2)}) collective-permute-start(bf16[16,32,256]{2,1,0:T(8,128)(2,1)S(1)} %collective-permute-done.11.refs_8_), channel_id=1, source_target_pairs={{0,8},{8,0},{16,24},{24,16},{32,40},{40,32},{48,56},{56,48},{64,72... | collective-permute-start | bytes 786440 | tf_op jit(solution)/shard_map/ppermute | solution.py:356
  73.6 7.5 %collective-permute-start.10 = (bf16[16,32,256]{2,1,0:T(8,128)(2,1)S(1)}, bf16[16,32,256]{2,1,0:T(8,128)(2,1)S(1)}, u32[]{:S(2)}, u32[]{:S(2)}) collective-permute-start(bf16[16,32,256]{2,1,0:T(8,128)(2,1)S(1)} %collective-permute-done.9.refs_6_), channel_id=1, source_target_pairs={{0,8},{8,0},{16,24},{24,16},{32,40},{40,32},{48,56},{56,48},{64,72... | collective-permute-start | bytes 786440 | tf_op jit(solution)/shard_map/ppermute | solution.py:356
  76.6 7.2 %collective-permute-start.15 = (bf16[16,32,256]{2,1,0:T(8,128)(2,1)S(1)}, bf16[16,32,256]{2,1,0:T(8,128)(2,1)S(1)}, u32[]{:S(2)}, u32[]{:S(2)}) collective-permute-start(bf16[16,32,256]{2,1,0:T(8,128)(2,1)S(1)} %collective-permute-done.5.refs_2_), channel_id=1, source_target_pairs={{0,48},{8,56},{16,0},{24,8},{32,16},{40,24},{48,32},{56,40},{64,11... | collective-permute-start | bytes 786440 | tf_op jit(solution)/shard_map/ppermute | solution.py:356
  79.8 8.0 %collective-permute-start.13 = (bf16[16,32,256]{2,1,0:T(8,128)(2,1)S(1)}, bf16[16,32,256]{2,1,0:T(8,128)(2,1)S(1)}, u32[]{:S(2)}, u32[]{:S(2)}) collective-permute-start(bf16[16,32,256]{2,1,0:T(8,128)(2,1)S(1)} %collective-permute-done.5.refs_2_), channel_id=1, source_target_pairs={{0,16},{8,24},{16,32},{24,40},{32,48},{40,56},{48,0},{56,8},{64,80... | collective-permute-start | bytes 786440 | tf_op jit(solution)/shard_map/ppermute | solution.py:356
  79.8 9.9 %collective-permute-start.6 = (bf16[16,32,256]{2,1,0:T(8,128)(2,1)S(1)}, bf16[16,32,256]{2,1,0:T(8,128)(2,1)S(1)}, u32[]{:S(2)}, u32[]{:S(2)}) collective-permute-start(bf16[16,32,256]{2,1,0:T(8,128)(2,1)S(1)} %collective-permute-done.5.refs_2_), channel_id=1, source_target_pairs={{0,8},{8,0},{16,24},{24,16},{32,40},{40,32},{48,56},{56,48},{64,72... | collective-permute-start | bytes 786440 | tf_op jit(solution)/shard_map/ppermute | solution.py:356
  81.0 8.7 %collective-permute-start.8 = (bf16[16,32,256]{2,1,0:T(8,128)(2,1)S(1)}, bf16[16,32,256]{2,1,0:T(8,128)(2,1)S(1)}, u32[]{:S(2)}, u32[]{:S(2)}) collective-permute-start(bf16[16,32,256]{2,1,0:T(8,128)(2,1)S(1)} %collective-permute-done.7.refs_4_), channel_id=1, source_target_pairs={{0,8},{8,0},{16,24},{24,16},{32,40},{40,32},{48,56},{56,48},{64,72... | collective-permute-start | bytes 786440 | tf_op jit(solution)/shard_map/ppermute | solution.py:356
  81.1 8.6 %collective-permute-start.18 = (bf16[16,32,256]{2,1,0:T(8,128)(2,1)S(1)}, bf16[16,32,256]{2,1,0:T(8,128)(2,1)S(1)}, u32[]{:S(2)}, u32[]{:S(2)}) collective-permute-start(bf16[16,32,256]{2,1,0:T(8,128)(2,1)S(1)} %collective-permute-done.17.refs_14_), channel_id=1, source_target_pairs={{0,8},{8,0},{16,24},{24,16},{32,40},{40,32},{48,56},{56,48},{64,72... | collective-permute-start | bytes 786440 | tf_op jit(solution)/shard_map/ppermute | solution.py:356
  83.8 6.0 %collective-permute-start.16 = (bf16[16,32,256]{2,1,0:T(8,128)(2,1)S(1)}, bf16[16,32,256]{2,1,0:T(8,128)(2,1)S(1)}, u32[]{:S(2)}, u32[]{:S(2)}) collective-permute-start(bf16[16,32,256]{2,1,0:T(8,128)(2,1)S(1)} %collective-permute-done.15.refs_12_), channel_id=1, source_target_pairs={{0,8},{8,0},{16,24},{24,16},{32,40},{40,32},{48,56},{56,48},{64,72... | collective-permute-start | bytes 786440 | tf_op jit(solution)/shard_map/ppermute | solution.py:356
  87.8 3.1 %collective-permute-start.14 = (bf16[16,32,256]{2,1,0:T(8,128)(2,1)S(1)}, bf16[16,32,256]{2,1,0:T(8,128)(2,1)S(1)}, u32[]{:S(2)}, u32[]{:S(2)}) collective-permute-start(bf16[16,32,256]{2,1,0:T(8,128)(2,1)S(1)} %collective-permute-done.13.refs_10_), channel_id=1, source_target_pairs={{0,8},{8,0},{16,24},{24,16},{32,40},{40,32},{48,56},{56,48},{64,72... | collective-permute-start | bytes 786440 | tf_op jit(solution)/shard_map/ppermute | solution.py:356

commit v3 on v2

--- a/solution.py
+++ b/solution.py
@@ -280,9 +280,10 @@
 
 def pack_kernel(hidden_hbm, long_ref, up_ref, gain_hbm, payload_ref, squares_ref, lifted_ref, hidden, gain_ref, sems):
     chan = lax.axis_index("chan")
-    own_up = up_ref.at[:, pl.ds(pl.multiple_of(chan * 32, 32), 32), :]
-    targets = [gain_ref, hidden, payload_ref.at[:, 0:32, :], payload_ref.at[:, 32:64, :]]
-    copies = fetch([gain_hbm, hidden_hbm, long_ref, own_up], targets, sems)
+    pair = [pl.ds(pl.multiple_of((lax.bitwise_and(chan, 3) + 4 * z) * 32, 32), 32) for z in range(2)]
+    sources = [gain_hbm, hidden_hbm, long_ref, up_ref.at[:, pair[0], :], up_ref.at[:, pair[1], :]]
+    targets = [gain_ref, hidden, *[payload_ref.at[:, 32 * i : 32 * i + 32, :] for i in range(3)]]
+    copies = fetch(sources, targets, sems)
     copies[0].wait()
     gains = [jnp.broadcast_to(gain_ref[q : q + 1, :], (INNER, INNER)).T for q in range(4)]
     copies[1].wait()
@@ -316,7 +317,7 @@
     return pl.pallas_call(
         pack_kernel,
         out_shape=(
-            jax.ShapeDtypeStruct((16, 64, 256), BF16),
+            jax.ShapeDtypeStruct((16, 96, 256), BF16),
             jax.ShapeDtypeStruct((8, 256), F32),
             jax.ShapeDtypeStruct((16, 32, 256), F32),
         ),
@@ -325,7 +326,7 @@
         scratch_shapes=[
             pltpu.VMEM((16, 32, 256), BF16),
             pltpu.VMEM((4, INNER), F32),
-            pltpu.SemaphoreType.DMA((4,)),
+            pltpu.SemaphoreType.DMA((5,)),
         ],
         compiler_params=limit(6),
         name="pack",
@@ -376,11 +377,9 @@
 
 
 def gather_chan(own):
-    side = over_chan(own, 1, 0)
-    pieces = [(own, 0, 0), (side, 1, 0)]
-    for dz, block in enumerate((own, side)):
-        for dy in (3, 1, 2):
-            pieces.append((over_chan(block, 0, -dy), dz, dy))
+    pieces = [(own, 0)]
+    for dy in (3, 1, 2):
+        pieces.append((over_chan(own, 0, -dy), dy))
     return pieces
 
 
@@ -405,9 +404,10 @@
         rows_ref[place, :] = total[32 * i : 32 * i + 32]
         mixed_ref[place, :] = ref[seq]
     turned_rows = rows_ref[...].T
-    for i, (dz, dy) in enumerate(up_keys):
-        owner = lax.bitwise_xor(chan // 4, dz) * 4 + lax.bitwise_and(chan + dy, 3)
-        grad_ref[pl.ds(pl.multiple_of(owner * 32, 32), 32), :] = turned_rows[32 * i : 32 * i + 32]
+    for i, (dy,) in enumerate(up_keys):
+        for z in range(2):
+            place = pl.ds(pl.multiple_of((4 * z + lax.bitwise_and(chan + dy, 3)) * 32, 32), 32)
+            grad_ref[place, :] = turned_rows[64 * i + 32 * z : 64 * i + 32 * z + 32]
 
 
 def weight_gradient(mixed, up):
@@ -440,7 +440,7 @@
     payload = normalise(lifted, parts, gate)
     signal = exchange(payload, "seq")
     spec = filter_spectrum(got, short_filter, long_bias[None, :], consts)
-    up = gather_chan(got[:, 32:64])
+    up = gather_chan(got[:, 32:96])
     mixed = gated_convolution(signal, spec, consts)
     return weight_gradient(gather_seq(mixed), up)
 

time: 93.6 us -> 100 us (1.068)
  waiting for transfers between devices: 22.6 us -> 36.8 us
  starting transfers between devices: 53.1 us -> 45.4 us
    ppermute x15, waiting for transfers between devices: 12.9 us -> 22.9 us  [over_seq(): return lax.ppermute(value, 'seq', pairs)]
    ppermute x15, starting transfers between devices: 20.8 us -> 13.8 us  [over_seq(): return lax.ppermute(value, 'seq', pairs)]
    all_to_all x2, waiting for transfers between devices: 2.7 us -> 5.22 us  [exchange(): return lax.all_to_all(value, axis, split_axis=0, concat_axis=0, tiled=True)]
    ppermute x11 -> x7, starting transfers between devices: 9.03 us -> 7.07 us  [over_chan(): return lax.ppermute(value, 'chan', pairs)]
    ppermute x11 -> x7, waiting for transfers between devices: 7.04 us -> 8.76 us  [over_chan(): return lax.ppermute(value, 'chan', pairs)]
    all_to_all x2, starting transfers between devices: 23.2 us -> 24.5 us  [exchange(): return lax.all_to_all(value, axis, split_axis=0, concat_axis=0, tiled=True)]
  transfers between devices with their start and end apart: 28 -> 24, of which waited for: 11 -> 14; matrix products, arithmetic and copies ran while one was open for 0% -> 0% of each run, Pallas kernels for 13% -> 8%
where the time goes in v3:
time: 100 us
  starting transfers between devices  45.4 us (45%)
  waiting for transfers between devices  36.8 us (37%)
  Pallas kernels  16.9 us (17%)
    all_to_all x2, starting transfers between devices, exchange(): return lax.all_to_all(value, axis, split_axis=0, concat_axis=0, tiled=True)  24.5 us
    ppermute x15, waiting for transfers between devices, over_seq(): return lax.ppermute(value, 'seq', pairs)  22.9 us
    ppermute x15, starting transfers between devices, over_seq(): return lax.ppermute(value, 'seq', pairs)  13.8 us
    ppermute x7, waiting for transfers between devices, over_chan(): return lax.ppermute(value, 'chan', pairs)  8.76 us
    ppermute x7, starting transfers between devices, over_chan(): return lax.ppermute(value, 'chan', pairs)  7.07 us
    pallas_call x1, Pallas kernels, filter_spectrum(): pl.pallas_call(filter_kernel, out_shape=pltpu.HBM((OUTER, 32, 2 * INNER),...  6.3 us
    all_to_all x2, waiting for transfers between devices, exchange(): return lax.all_to_all(value, axis, split_axis=0, concat_axis=0, tiled=True)  5.22 us
    pallas_call x1, Pallas kernels, gated_convolution(): pl.pallas_call(signal_kernel, out_shape=jax.ShapeDtypeStruct((16, 32, 256...  4.43 us
  transfers between devices with their start and end apart: 24, of which 14 were waited for; matrix products, arithmetic and copies ran while one was open for 0% of the time, Pallas kernels for 8%

profile of v3, /device:TPU:1, one launch (start us, length us, event | category | flops | bytes accessed | tf_op | source)
XLA Modules:
  0.0 100.0 jit_solution(14784436360196503960)
XLA Ops:
  0.6 2.1 %pack.1 = (bf16[16,96,256]{2,1,0:T(8,128)(2,1)}, f32[8,256]{1,0:T(8,128)S(1)}, f32[16,32,256]{2,1,0:T(8,128)S(1)}) custom-call(bf16[16,32,256]{2,1,0:T(8,128)(2,1)} %bitcast.8, bf16[16,32,256]{2,1,0:T(8,128)(2,1)} %bitcast.9, bf16[16,256,256]{2,1,0:T(8,128)(2,1)} %bitcast.7, f32[4,128]{1,0:T(4,128)} %bitcast.11), custom_call_target="tpu_custom_call" | custom-call | tf_op jit(solution)/shard_map/pack/pallas_call | solution.py:317
  2.8 0.0 copy-start
  2.8 0.0 copy-start.1
  2.8 9.3 %all-to-all-start.1 = ((bf16[16,96,256]{2,1,0:T(8,128)(2,1)}), bf16[16,96,256]{2,1,0:T(8,128)(2,1)S(1)}, u32[]{:S(2)}, u32[]{:S(2)}) async-start(bf16[16,96,256]{2,1,0:T(8,128)(2,1)} %get-tuple-element.7), calls=%async_computation.1 | async-start | bytes 1572864 | tf_op jit(solution)/shard_map/all_to_all | solution.py:428
  12.1 0.7 collective-permute-start
  12.8 3.8 %collective-permute-done = f32[8,256]{1,0:T(8,128)S(1)} collective-permute-done((f32[8,256]{1,0:T(8,128)S(1)}, f32[8,256]{1,0:T(8,128)S(1)}, u32[]{:S(2)}, u32[]{:S(2)}) %collective-permute-start) | collective-permute-done | bytes 8224 | tf_op jit(solution)/shard_map/ppermute | solution.py:362
  16.6 2.9 %collective-permute-start.3 = (f32[8,256]{1,0:T(8,128)S(1)}, f32[8,256]{1,0:T(8,128)S(1)}, u32[]{:S(2)}, u32[]{:S(2)}) collective-permute-start(f32[8,256]{1,0:T(8,128)S(1)} %add.3.s0), channel_id=1, source_target_pairs={{0,2},{1,3},{2,0},{3,1},{4,6},{5,7},{6,4},{7,5},{8,10},{9,11},{10,... | collective-permute-start | bytes 24584 | tf_op jit(solution)/shard_map/ppermute | solution.py:362
  19.5 0.8 collective-permute-start.2
  20.3 0.7 collective-permute-start.1
  21.0 0.0 collective-permute-done.3.s3
  21.0 1.3 %collective-permute-done.2.s2 = f32[8,256]{1,0:T(8,128)S(1)} collective-permute-done((f32[8,256]{1,0:T(8,128)S(1)}, f32[8,256]{1,0:T(8,128)S(1)}, u32[]{:S(2)}, u32[]{:S(2)}) %collective-permute-start.2) | collective-permute-done | bytes 8224 | tf_op jit(solution)/shard_map/ppermute | solution.py:362
  22.3 1.7 %collective-permute-done.1.s1 = f32[8,256]{1,0:T(8,128)S(1)} collective-permute-done((f32[8,256]{1,0:T(8,128)S(1)}, f32[8,256]{1,0:T(8,128)S(1)}, u32[]{:S(2)}, u32[]{:S(2)}) %collective-permute-start.1) | collective-permute-done | bytes 8224 | tf_op jit(solution)/shard_map/ppermute | solution.py:362
  24.0 1.8 %normalise.1 = bf16[16,64,256]{2,1,0:T(8,128)(2,1)} custom-call(f32[16,32,256]{2,1,0:T(8,128)S(1)} %get-tuple-element.5.lifted_ref, f32[8,256]{1,0:T(8,128)S(1)} %add.3.s0, f32[8,256]{1,0:T(8,128)S(1)} %collective-permute-done.1.s1, f32[8,256]{1,0:T(8,128)S(1)} %collective-permute-done.2.s2, f32[8,256]{1,0:T(8,128)S(1)} %collective-permute-done.3.s3, ...), custom_call_target="tpu_custom_call" | custom-call | tf_op jit(solution)/shard_map/normalise/pallas_call | solution.py:337
  25.8 0.6 all-to-all-done.1.got_ref
  26.3 15.3 %all-to-all-start = ((bf16[16,64,256]{2,1,0:T(8,128)(2,1)}), bf16[16,64,256]{2,1,0:T(8,128)(2,1)S(1)}, u32[]{:S(2)}, u32[]{:S(2)}) async-start(bf16[16,64,256]{2,1,0:T(8,128)(2,1)} %normalise.1), calls=%async_computation | async-start | bytes 1048576 | tf_op jit(solution)/shard_map/all_to_all | solution.py:428
  41.6 6.3 %filter_spectrum.1.spec_hbm = f32[32,32,256]{2,1,0:T(8,128)} custom-call(bf16[16,96,256]{2,1,0:T(8,128)(2,1)S(1)} %all-to-all-done.1.got_ref, f32[512,128]{1,0:T(8,128)S(1)} %copy-done, f32[1,512]{1,0:T(1,128)S(1)} %bitcast.6, f32[2,32,128]{2,1,0:T(8,128)} %constant.4.clone.turn_hbm, bf16[2,768,256]{2,1,0:T(8,128)(2,1)} %constant.5.clone.inner_hbm), custom_call_target="tpu_custom_call" | custom-call | flops 2000000000 | bytes 3000000 | tf_op jit(solution)/shard_map/filter_spectrum/pallas_call | solution.py:257
  47.9 4.7 %all-to-all-done.got_ref = bf16[16,64,256]{2,1,0:T(8,128)(2,1)S(1)} async-done(((bf16[16,64,256]{2,1,0:T(8,128)(2,1)}), bf16[16,64,256]{2,1,0:T(8,128)(2,1)S(1)}, u32[]{:S(2)}, u32[]{:S(2)}) %all-to-all-start) | async-done | bytes 524320 | tf_op jit(solution)/shard_map/all_to_all | solution.py:428
  52.6 4.4 %shard_map.104.refs_0_ = bf16[16,32,256]{2,1,0:T(8,128)(2,1)S(1)} custom-call(bf16[16,64,256]{2,1,0:T(8,128)(2,1)S(1)} %all-to-all-done.got_ref, f32[32,32,256]{2,1,0:T(8,128)} %filter_spectrum.1.spec_hbm, f32[2,32,128]{2,1,0:T(8,128)} %constant.4.clone.turn_hbm, bf16[2,768,256]{2,1,0:T(8,128)(2,1)} %constant.5.clone.inner_hbm), custom_call_target="tpu_custom_call" | custom-call | flops 1000000000 | bytes 3000000 | tf_op jit(solution)/shard_map/pallas_call | solution.py:270
  57.0 1.4 %collective-permute-start.11 = (bf16[16,32,256]{2,1,0:T(8,128)(2,1)S(1)}, bf16[16,32,256]{2,1,0:T(8,128)(2,1)S(1)}, u32[]{:S(2)}, u32[]{:S(2)}) collective-permute-start(bf16[16,32,256]{2,1,0:T(8,128)(2,1)S(1)} %shard_map.104.refs_0_), channel_id=1, source_target_pairs={{0,32},{8,40},{16,48},{24,56},{32,0},{40,8},{48,16},{56,24},{64,96... | collective-permute-start | bytes 786440 | tf_op jit(solution)/shard_map/ppermute | solution.py:357
  58.4 1.0 collective-permute-start.9
  59.4 0.5 collective-permute-start.7
  59.9 0.3 collective-permute-start.21
  60.2 1.7 %collective-permute-start.20 = (bf16[16,64,256]{2,1,0:T(8,128)(2,1)S(1)}, bf16[16,64,256]{2,1,0:T(8,128)(2,1)S(1)}, u32[]{:S(2)}, u32[]{:S(2)}) collective-permute-start(bf16[16,64,256]{2,1,0:T(8,128)(2,1)S(1)} %slice.4.refs_16_), channel_id=1, source_target_pairs={{0,3},{1,0},{2,1},{3,2},{4,7},{5,4},{6,5},{7,6},{8,11},{9,8},{10,9... | collective-permute-start | bytes 1572872 | tf_op jit(solution)/shard_map/ppermute | solution.py:362
  61.9 3.2 %collective-permute-done.11.refs_8_ = bf16[16,32,256]{2,1,0:T(8,128)(2,1)S(1)} collective-permute-done((bf16[16,32,256]{2,1,0:T(8,128)(2,1)S(1)}, bf16[16,32,256]{2,1,0:T(8,128)(2,1)S(1)}, u32[]{:S(2)}, u32[]{:S(2)}) %collective-permute-start.11) | collective-permute-done | bytes 262176 | tf_op jit(solution)/shard_map/ppermute | solution.py:357
  65.1 0.0 collective-permute-start.19
  65.1 6.4 %collective-permute-done.9.refs_6_ = bf16[16,32,256]{2,1,0:T(8,128)(2,1)S(1)} collective-permute-done((bf16[16,32,256]{2,1,0:T(8,128)(2,1)S(1)}, bf16[16,32,256]{2,1,0:T(8,128)(2,1)S(1)}, u32[]{:S(2)}, u32[]{:S(2)}) %collective-permute-start.9) | collective-permute-done | bytes 262176 | tf_op jit(solution)/shard_map/ppermute | solution.py:357
  71.5 0.0 collective-permute-start.5
  71.5 1.0 collective-permute-done.7.refs_4_
  72.5 0.4 collective-permute-start.4
  72.9 7.3 %collective-permute-done.5.refs_2_ = bf16[16,32,256]{2,1,0:T(8,128)(2,1)S(1)} collective-permute-done((bf16[16,32,256]{2,1,0:T(8,128)(2,1)S(1)}, bf16[16,32,256]{2,1,0:T(8,128)(2,1)S(1)}, u32[]{:S(2)}, u32[]{:S(2)}) %collective-permute-start.5) | collective-permute-done | bytes 262176 | tf_op jit(solution)/shard_map/ppermute | solution.py:357
  80.2 0.0 collective-permute-start.17
  80.2 0.0 collective-permute-done.4.refs_1_
  80.2 1.8 %collective-permute-start.12 = (bf16[16,32,256]{2,1,0:T(8,128)(2,1)S(1)}, bf16[16,32,256]{2,1,0:T(8,128)(2,1)S(1)}, u32[]{:S(2)}, u32[]{:S(2)}) collective-permute-start(bf16[16,32,256]{2,1,0:T(8,128)(2,1)S(1)} %collective-permute-done.11.refs_8_), channel_id=1, source_target_pairs={{0,8},{8,0},{16,24},{24,16},{32,40},{40,32},{48,56},{56,48},{64,72... | collective-permute-start | bytes 786440 | tf_op jit(solution)/shard_map/ppermute | solution.py:357
  82.0 0.1 collective-permute-start.10
  82.1 0.8 collective-permute-done.20.refs_18_
  82.9 2.5 %collective-permute-start.15 = (bf16[16,32,256]{2,1,0:T(8,128)(2,1)S(1)}, bf16[16,32,256]{2,1,0:T(8,128)(2,1)S(1)}, u32[]{:S(2)}, u32[]{:S(2)}) collective-permute-start(bf16[16,32,256]{2,1,0:T(8,128)(2,1)S(1)} %collective-permute-done.5.refs_2_), channel_id=1, source_target_pairs={{0,48},{8,56},{16,0},{24,8},{32,16},{40,24},{48,32},{56,40},{64,11... | collective-permute-start | bytes 786440 | tf_op jit(solution)/shard_map/ppermute | solution.py:357
  85.4 1.2 %collective-permute-done.19.refs_17_ = bf16[16,64,256]{2,1,0:T(8,128)(2,1)S(1)} collective-permute-done((bf16[16,64,256]{2,1,0:T(8,128)(2,1)S(1)}, bf16[16,64,256]{2,1,0:T(8,128)(2,1)S(1)}, u32[]{:S(2)}, u32[]{:S(2)}) %collective-permute-start.19) | collective-permute-done | bytes 524320 | tf_op jit(solution)/shard_map/ppermute | solution.py:362
  86.6 0.8 collective-permute-start.13
  87.4 0.6 collective-permute-done.17.refs_14_
  88.0 2.4 %collective-permute-start.6 = (bf16[16,32,256]{2,1,0:T(8,128)(2,1)S(1)}, bf16[16,32,256]{2,1,0:T(8,128)(2,1)S(1)}, u32[]{:S(2)}, u32[]{:S(2)}) collective-permute-start(bf16[16,32,256]{2,1,0:T(8,128)(2,1)S(1)} %collective-permute-done.5.refs_2_), channel_id=1, source_target_pairs={{0,8},{8,0},{16,24},{24,16},{32,40},{40,32},{48,56},{56,48},{64,72... | collective-permute-start | bytes 786440 | tf_op jit(solution)/shard_map/ppermute | solution.py:357
  90.4 0.0 collective-permute-start.8
  90.4 0.5 collective-permute-start.18
  90.9 1.0 %collective-permute-start.16 = (bf16[16,32,256]{2,1,0:T(8,128)(2,1)S(1)}, bf16[16,32,256]{2,1,0:T(8,128)(2,1)S(1)}, u32[]{:S(2)}, u32[]{:S(2)}) collective-permute-start(bf16[16,32,256]{2,1,0:T(8,128)(2,1)S(1)} %collective-permute-done.15.refs_12_), channel_id=1, source_target_pairs={{0,8},{8,0},{16,24},{24,16},{32,40},{40,32},{48,56},{56,48},{64,72... | collective-permute-start | bytes 786440 | tf_op jit(solution)/shard_map/ppermute | solution.py:357
  92.0 3.2 %collective-permute-done.13.refs_10_ = bf16[16,32,256]{2,1,0:T(8,128)(2,1)S(1)} collective-permute-done((bf16[16,32,256]{2,1,0:T(8,128)(2,1)S(1)}, bf16[16,32,256]{2,1,0:T(8,128)(2,1)S(1)}, u32[]{:S(2)}, u32[]{:S(2)}) %collective-permute-start.13) | collective-permute-done | bytes 262176 | tf_op jit(solution)/shard_map/ppermute | solution.py:357
  95.2 1.3 %collective-permute-start.14 = (bf16[16,32,256]{2,1,0:T(8,128)(2,1)S(1)}, bf16[16,32,256]{2,1,0:T(8,128)(2,1)S(1)}, u32[]{:S(2)}, u32[]{:S(2)}) collective-permute-start(bf16[16,32,256]{2,1,0:T(8,128)(2,1)S(1)} %collective-permute-done.13.refs_10_), channel_id=1, source_target_pairs={{0,8},{8,0},{16,24},{24,16},{32,40},{40,32},{48,56},{56,48},{64,72... | collective-permute-start | bytes 786440 | tf_op jit(solution)/shard_map/ppermute | solution.py:357
  96.5 0.0 collective-permute-done.16.refs_13_
  96.5 1.1 %collective-permute-done.14.refs_11_ = bf16[16,32,256]{2,1,0:T(8,128)(2,1)S(1)} collective-permute-done((bf16[16,32,256]{2,1,0:T(8,128)(2,1)S(1)}, bf16[16,32,256]{2,1,0:T(8,128)(2,1)S(1)}, u32[]{:S(2)}, u32[]{:S(2)}) %collective-permute-start.14) | collective-permute-done | bytes 262176 | tf_op jit(solution)/shard_map/ppermute | solution.py:357
  97.7 2.3 %weight_gradient.1 = (bf16[512,256]{1,0:T(8,128)(2,1)}, f32[256,512]{1,0:T(8,128)}) custom-call(bf16[16,32,256]{2,1,0:T(8,128)(2,1)S(1)} %shard_map.104.refs_0_, bf16[16,32,256]{2,1,0:T(8,128)(2,1)S(1)} %collective-permute-done.4.refs_1_, bf16[16,32,256]{2,1,0:T(8,128)(2,1)S(1)} %collective-permute-done.5.refs_2_, ...), custom_call_target="tpu_custom_call" | custom-call | flops 1000000000 | bytes 7000000 | tf_op jit(solution)/shard_map/weight_gradient/pallas_call | solution.py:415
  (11 shorter events, 0.1 us)
Async XLA Ops:
  2.8 38.8 %copy-start = (f32[512,128]{1,0:T(8,128)S(1)}, f32[512,128]{1,0:T(8,128)}, u32[]{:S(2)}) copy-start(f32[512,128]{1,0:T(8,128)} %taps_ref.1) | copy-start | bytes 786436
  2.8 38.8 %copy-start.1 = (f32[512]{0:T(512)S(1)}, f32[512]{0:T(512)}, u32[]{:S(2)}) copy-start(f32[512]{0:T(512)} %param.13) | copy-start | bytes 6148
  2.8 23.5 %all-to-all-start.1 = ((bf16[16,96,256]{2,1,0:T(8,128)(2,1)}), bf16[16,96,256]{2,1,0:T(8,128)(2,1)S(1)}, u32[]{:S(2)}, u32[]{:S(2)}) async-start(bf16[16,96,256]{2,1,0:T(8,128)(2,1)} %get-tuple-element.7), calls=%async_computation.1 | async-start | bytes 1572864 | tf_op jit(solution)/shard_map/all_to_all | solution.py:428
  12.1 4.5 %collective-permute-start = (f32[8,256]{1,0:T(8,128)S(1)}, f32[8,256]{1,0:T(8,128)S(1)}, u32[]{:S(2)}, u32[]{:S(2)}) collective-permute-start(f32[8,256]{1,0:T(8,128)S(1)} %get-tuple-element.6), channel_id=1, source_target_pairs={{0,4},{1,5},{2,6},{3,7},{4,0},{5,1},{6,2},{7,3},{8,12},{9,13},{10,... | collective-permute-start | bytes 24584 | tf_op jit(solution)/shard_map/ppermute | solution.py:362
  16.6 4.4 %collective-permute-start.3 = (f32[8,256]{1,0:T(8,128)S(1)}, f32[8,256]{1,0:T(8,128)S(1)}, u32[]{:S(2)}, u32[]{:S(2)}) collective-permute-start(f32[8,256]{1,0:T(8,128)S(1)} %add.3.s0), channel_id=1, source_target_pairs={{0,2},{1,3},{2,0},{3,1},{4,6},{5,7},{6,4},{7,5},{8,10},{9,11},{10,... | collective-permute-start | bytes 24584 | tf_op jit(solution)/shard_map/ppermute | solution.py:362
  19.5 2.8 %collective-permute-start.2 = (f32[8,256]{1,0:T(8,128)S(1)}, f32[8,256]{1,0:T(8,128)S(1)}, u32[]{:S(2)}, u32[]{:S(2)}) collective-permute-start(f32[8,256]{1,0:T(8,128)S(1)} %add.3.s0), channel_id=1, source_target_pairs={{0,3},{1,0},{2,1},{3,2},{4,7},{5,4},{6,5},{7,6},{8,11},{9,8},{10,9... | collective-permute-start | bytes 24584 | tf_op jit(solution)/shard_map/ppermute | solution.py:362
  20.3 3.7 %collective-permute-start.1 = (f32[8,256]{1,0:T(8,128)S(1)}, f32[8,256]{1,0:T(8,128)S(1)}, u32[]{:S(2)}, u32[]{:S(2)}) collective-permute-start(f32[8,256]{1,0:T(8,128)S(1)} %add.3.s0), channel_id=1, source_target_pairs={{0,1},{1,2},{2,3},{3,0},{4,5},{5,6},{6,7},{7,4},{8,9},{9,10},{10,1... | collective-permute-start | bytes 24584 | tf_op jit(solution)/shard_map/ppermute | solution.py:362
  26.3 26.3 %all-to-all-start = ((bf16[16,64,256]{2,1,0:T(8,128)(2,1)}), bf16[16,64,256]{2,1,0:T(8,128)(2,1)S(1)}, u32[]{:S(2)}, u32[]{:S(2)}) async-start(bf16[16,64,256]{2,1,0:T(8,128)(2,1)} %normalise.1), calls=%async_computation | async-start | bytes 1048576 | tf_op jit(solution)/shard_map/all_to_all | solution.py:428
  57.0 8.0 %collective-permute-start.11 = (bf16[16,32,256]{2,1,0:T(8,128)(2,1)S(1)}, bf16[16,32,256]{2,1,0:T(8,128)(2,1)S(1)}, u32[]{:S(2)}, u32[]{:S(2)}) collective-permute-start(bf16[16,32,256]{2,1,0:T(8,128)(2,1)S(1)} %shard_map.104.refs_0_), channel_id=1, source_target_pairs={{0,32},{8,40},{16,48},{24,56},{32,0},{40,8},{48,16},{56,24},{64,96... | collective-permute-start | bytes 786440 | tf_op jit(solution)/shard_map/ppermute | solution.py:357
  58.4 13.1 %collective-permute-start.9 = (bf16[16,32,256]{2,1,0:T(8,128)(2,1)S(1)}, bf16[16,32,256]{2,1,0:T(8,128)(2,1)S(1)}, u32[]{:S(2)}, u32[]{:S(2)}) collective-permute-start(bf16[16,32,256]{2,1,0:T(8,128)(2,1)S(1)} %shard_map.104.refs_0_), channel_id=1, source_target_pairs={{0,48},{8,56},{16,0},{24,8},{32,16},{40,24},{48,32},{56,40},{64,11... | collective-permute-start | bytes 786440 | tf_op jit(solution)/shard_map/ppermute | solution.py:357
  59.4 13.1 %collective-permute-start.7 = (bf16[16,32,256]{2,1,0:T(8,128)(2,1)S(1)}, bf16[16,32,256]{2,1,0:T(8,128)(2,1)S(1)}, u32[]{:S(2)}, u32[]{:S(2)}) collective-permute-start(bf16[16,32,256]{2,1,0:T(8,128)(2,1)S(1)} %shard_map.104.refs_0_), channel_id=1, source_target_pairs={{0,16},{8,24},{16,32},{24,40},{32,48},{40,56},{48,0},{56,8},{64,80... | collective-permute-start | bytes 786440 | tf_op jit(solution)/shard_map/ppermute | solution.py:357
  59.9 22.1 %collective-permute-start.21 = (bf16[16,64,256]{2,1,0:T(8,128)(2,1)S(1)}, bf16[16,64,256]{2,1,0:T(8,128)(2,1)S(1)}, u32[]{:S(2)}, u32[]{:S(2)}) collective-permute-start(bf16[16,64,256]{2,1,0:T(8,128)(2,1)S(1)} %slice.4.refs_16_), channel_id=1, source_target_pairs={{0,2},{1,3},{2,0},{3,1},{4,6},{5,7},{6,4},{7,5},{8,10},{9,11},{10,... | collective-permute-start | bytes 1572872 | tf_op jit(solution)/shard_map/ppermute | solution.py:362
  60.2 22.7 %collective-permute-start.20 = (bf16[16,64,256]{2,1,0:T(8,128)(2,1)S(1)}, bf16[16,64,256]{2,1,0:T(8,128)(2,1)S(1)}, u32[]{:S(2)}, u32[]{:S(2)}) collective-permute-start(bf16[16,64,256]{2,1,0:T(8,128)(2,1)S(1)} %slice.4.refs_16_), channel_id=1, source_target_pairs={{0,3},{1,0},{2,1},{3,2},{4,7},{5,4},{6,5},{7,6},{8,11},{9,8},{10,9... | collective-permute-start | bytes 1572872 | tf_op jit(solution)/shard_map/ppermute | solution.py:362
  65.1 21.5 %collective-permute-start.19 = (bf16[16,64,256]{2,1,0:T(8,128)(2,1)S(1)}, bf16[16,64,256]{2,1,0:T(8,128)(2,1)S(1)}, u32[]{:S(2)}, u32[]{:S(2)}) collective-permute-start(bf16[16,64,256]{2,1,0:T(8,128)(2,1)S(1)} %slice.4.refs_16_), channel_id=1, source_target_pairs={{0,1},{1,2},{2,3},{3,0},{4,5},{5,6},{6,7},{7,4},{8,9},{9,10},{10,1... | collective-permute-start | bytes 1572872 | tf_op jit(solution)/shard_map/ppermute | solution.py:362
  71.5 8.7 %collective-permute-start.5 = (bf16[16,32,256]{2,1,0:T(8,128)(2,1)S(1)}, bf16[16,32,256]{2,1,0:T(8,128)(2,1)S(1)}, u32[]{:S(2)}, u32[]{:S(2)}) collective-permute-start(bf16[16,32,256]{2,1,0:T(8,128)(2,1)S(1)} %shard_map.104.refs_0_), channel_id=1, source_target_pairs={{0,64},{8,72},{16,80},{24,88},{32,96},{40,104},{48,112},{56,120},{... | collective-permute-start | bytes 786440 | tf_op jit(solution)/shard_map/ppermute | solution.py:357
  72.5 7.7 %collective-permute-start.4 = (bf16[16,32,256]{2,1,0:T(8,128)(2,1)S(1)}, bf16[16,32,256]{2,1,0:T(8,128)(2,1)S(1)}, u32[]{:S(2)}, u32[]{:S(2)}) collective-permute-start(bf16[16,32,256]{2,1,0:T(8,128)(2,1)S(1)} %shard_map.104.refs_0_), channel_id=1, source_target_pairs={{0,8},{8,0},{16,24},{24,16},{32,40},{40,32},{48,56},{56,48},{64,72... | collective-permute-start | bytes 786440 | tf_op jit(solution)/shard_map/ppermute | solution.py:357
  80.2 7.8 %collective-permute-start.17 = (bf16[16,32,256]{2,1,0:T(8,128)(2,1)S(1)}, bf16[16,32,256]{2,1,0:T(8,128)(2,1)S(1)}, u32[]{:S(2)}, u32[]{:S(2)}) collective-permute-start(bf16[16,32,256]{2,1,0:T(8,128)(2,1)S(1)} %collective-permute-done.11.refs_8_), channel_id=1, source_target_pairs={{0,64},{8,72},{16,80},{24,88},{32,96},{40,104},{48,112},{56,120},{... | collective-permute-start | bytes 786440 | tf_op jit(solution)/shard_map/ppermute | solution.py:357
  80.2 10.2 %collective-permute-start.12 = (bf16[16,32,256]{2,1,0:T(8,128)(2,1)S(1)}, bf16[16,32,256]{2,1,0:T(8,128)(2,1)S(1)}, u32[]{:S(2)}, u32[]{:S(2)}) collective-permute-start(bf16[16,32,256]{2,1,0:T(8,128)(2,1)S(1)} %collective-permute-done.11.refs_8_), channel_id=1, source_target_pairs={{0,8},{8,0},{16,24},{24,16},{32,40},{40,32},{48,56},{56,48},{64,72... | collective-permute-start | bytes 786440 | tf_op jit(solution)/shard_map/ppermute | solution.py:357
  82.0 8.4 %collective-permute-start.10 = (bf16[16,32,256]{2,1,0:T(8,128)(2,1)S(1)}, bf16[16,32,256]{2,1,0:T(8,128)(2,1)S(1)}, u32[]{:S(2)}, u32[]{:S(2)}) collective-permute-start(bf16[16,32,256]{2,1,0:T(8,128)(2,1)S(1)} %collective-permute-done.9.refs_6_), channel_id=1, source_target_pairs={{0,8},{8,0},{16,24},{24,16},{32,40},{40,32},{48,56},{56,48},{64,72... | collective-permute-start | bytes 786440 | tf_op jit(solution)/shard_map/ppermute | solution.py:357
  82.9 8.0 %collective-permute-start.15 = (bf16[16,32,256]{2,1,0:T(8,128)(2,1)S(1)}, bf16[16,32,256]{2,1,0:T(8,128)(2,1)S(1)}, u32[]{:S(2)}, u32[]{:S(2)}) collective-permute-start(bf16[16,32,256]{2,1,0:T(8,128)(2,1)S(1)} %collective-permute-done.5.refs_2_), channel_id=1, source_target_pairs={{0,48},{8,56},{16,0},{24,8},{32,16},{40,24},{48,32},{56,40},{64,11... | collective-permute-start | bytes 786440 | tf_op jit(solution)/shard_map/ppermute | solution.py:357
  86.6 8.6 %collective-permute-start.13 = (bf16[16,32,256]{2,1,0:T(8,128)(2,1)S(1)}, bf16[16,32,256]{2,1,0:T(8,128)(2,1)S(1)}, u32[]{:S(2)}, u32[]{:S(2)}) collective-permute-start(bf16[16,32,256]{2,1,0:T(8,128)(2,1)S(1)} %collective-permute-done.5.refs_2_), channel_id=1, source_target_pairs={{0,16},{8,24},{16,32},{24,40},{32,48},{40,56},{48,0},{56,8},{64,80... | collective-permute-start | bytes 786440 | tf_op jit(solution)/shard_map/ppermute | solution.py:357
  88.0 8.5 %collective-permute-start.6 = (bf16[16,32,256]{2,1,0:T(8,128)(2,1)S(1)}, bf16[16,32,256]{2,1,0:T(8,128)(2,1)S(1)}, u32[]{:S(2)}, u32[]{:S(2)}) collective-permute-start(bf16[16,32,256]{2,1,0:T(8,128)(2,1)S(1)} %collective-permute-done.5.refs_2_), channel_id=1, source_target_pairs={{0,8},{8,0},{16,24},{24,16},{32,40},{40,32},{48,56},{56,48},{64,72... | collective-permute-start | bytes 786440 | tf_op jit(solution)/shard_map/ppermute | solution.py:357
  90.4 6.1 %collective-permute-start.8 = (bf16[16,32,256]{2,1,0:T(8,128)(2,1)S(1)}, bf16[16,32,256]{2,1,0:T(8,128)(2,1)S(1)}, u32[]{:S(2)}, u32[]{:S(2)}) collective-permute-start(bf16[16,32,256]{2,1,0:T(8,128)(2,1)S(1)} %collective-permute-done.7.refs_4_), channel_id=1, source_target_pairs={{0,8},{8,0},{16,24},{24,16},{32,40},{40,32},{48,56},{56,48},{64,72... | collective-permute-start | bytes 786440 | tf_op jit(solution)/shard_map/ppermute | solution.py:357
  90.4 6.1 %collective-permute-start.18 = (bf16[16,32,256]{2,1,0:T(8,128)(2,1)S(1)}, bf16[16,32,256]{2,1,0:T(8,128)(2,1)S(1)}, u32[]{:S(2)}, u32[]{:S(2)}) collective-permute-start(bf16[16,32,256]{2,1,0:T(8,128)(2,1)S(1)} %collective-permute-done.17.refs_14_), channel_id=1, source_target_pairs={{0,8},{8,0},{16,24},{24,16},{32,40},{40,32},{48,56},{56,48},{64,72... | collective-permute-start | bytes 786440 | tf_op jit(solution)/shard_map/ppermute | solution.py:357
  90.9 5.6 %collective-permute-start.16 = (bf16[16,32,256]{2,1,0:T(8,128)(2,1)S(1)}, bf16[16,32,256]{2,1,0:T(8,128)(2,1)S(1)}, u32[]{:S(2)}, u32[]{:S(2)}) collective-permute-start(bf16[16,32,256]{2,1,0:T(8,128)(2,1)S(1)} %collective-permute-done.15.refs_12_), channel_id=1, source_target_pairs={{0,8},{8,0},{16,24},{24,16},{32,40},{40,32},{48,56},{56,48},{64,72... | collective-permute-start | bytes 786440 | tf_op jit(solution)/shard_map/ppermute | solution.py:357
  95.2 2.5 %collective-permute-start.14 = (bf16[16,32,256]{2,1,0:T(8,128)(2,1)S(1)}, bf16[16,32,256]{2,1,0:T(8,128)(2,1)S(1)}, u32[]{:S(2)}, u32[]{:S(2)}) collective-permute-start(bf16[16,32,256]{2,1,0:T(8,128)(2,1)S(1)} %collective-permute-done.13.refs_10_), channel_id=1, source_target_pairs={{0,8},{8,0},{16,24},{24,16},{32,40},{40,32},{48,56},{56,48},{64,72... | collective-permute-start | bytes 786440 | tf_op jit(solution)/shard_map/ppermute | solution.py:357

commit v4 on v3

--- a/solution.py
+++ b/solution.py
@@ -30,7 +30,7 @@
     for table in (ahead, back):
         upper = table.astype(BF16)
         lower = (table - upper.astype(np.float64)).astype(BF16)
-        parts.append(np.concatenate([upper, lower, upper]))
+        parts.append(np.concatenate([upper, lower]))
     return [np.stack([np.cos(turn), -np.sin(turn)]).astype(np.float32), np.stack(parts)]
 
 
@@ -67,59 +67,66 @@
     return first + second
 
 
-def in_two_passes(load, store, half_ref, sign):
+def first_pass(load, half_ref, sign):
     for q in range(4):
         for k, value in enumerate(transform([load(4 * p + q) for p in range(8)], sign)):
             half_ref[q, k, 0], half_ref[q, k, 1] = turned(value, q * k, OUTER, sign)
+
+
+def second_pass(store, half_ref, sign):
     for k in range(8):
         for j, value in enumerate(transform([(half_ref[q, k, 0], half_ref[q, k, 1]) for q in range(4)], sign)):
             store(k + 8 * j, value)
 
 
-def groups_of_rows(body):
-    for g in range(4):
-        body(slice(8 * g, 8 * g + 8), g)
-
-
-def outer_ahead(time_ref, mid_ref, half_ref, twr_ref, twi_ref):
-    def group(rows, g):
-        def load(n):
+def row_groups():
+    return [(g, slice(8 * g, 8 * g + 8)) for g in range(4)]
+
+
+def outer_ahead(time_ref, mid_ref, half_ref, turn_ref, ready=None):
+    for g, rows in row_groups():
+
+        def load(n, rows=rows):
             x = time_ref[n, rows, :]
             angle = 2.0 * math.pi * n / (4 * OUTER)
             return x * math.cos(angle), x * -math.sin(angle)
 
-        def store(k, value):
+        first_pass(load, half_ref.at[g], -1)
+    if ready is not None:
+        ready.wait()
+    for g, rows in row_groups():
+
+        def store(k, value, rows=rows):
             re, im = value
-            tr, ti = twr_ref[k : k + 1, :], twi_ref[k : k + 1, :]
+            tr, ti = turn_ref[0, k : k + 1, :], turn_ref[1, k : k + 1, :]
             mid_ref[k, rows, 0:INNER] = re * tr - im * ti
             mid_ref[k, rows, INNER:] = re * ti + im * tr
 
-        in_two_passes(load, store, half_ref.at[g], -1)
-
-    groups_of_rows(group)
-
-
-def outer_back(mid_ref, time_ref, half_ref, twr_ref, twi_ref):
-    def group(rows, g):
-        def load(k):
+        second_pass(store, half_ref.at[g], -1)
+
+
+def outer_back(mid_ref, time_ref, half_ref, turn_ref):
+    for g, rows in row_groups():
+
+        def load(k, rows=rows):
             re, im = mid_ref[k, rows, 0:INNER], mid_ref[k, rows, INNER:]
-            tr, ti = twr_ref[k : k + 1, :], twi_ref[k : k + 1, :]
+            tr, ti = turn_ref[0, k : k + 1, :], turn_ref[1, k : k + 1, :]
             return re * tr + im * ti, im * tr - re * ti
 
-        def store(n, value):
+        def store(n, value, rows=rows):
             re, im = value
             angle = 2.0 * math.pi * n / (4 * OUTER)
             time_ref[n, rows, :] = re * (math.cos(angle) / LENGTH) - im * (math.sin(angle) / LENGTH)
 
-        in_two_passes(load, store, half_ref.at[g], 1)
-
-    groups_of_rows(group)
+        first_pass(load, half_ref.at[g], 1)
+        second_pass(store, half_ref.at[g], 1)
 
 
 def product(rows, table_ref):
     upper = rows.astype(BF16)
     lower = (rows - upper.astype(F32)).astype(BF16)
-    return jnp.dot(jnp.concatenate([upper, upper, lower], axis=1), table_ref[...], preferred_element_type=F32)
+    dot = functools.partial(jnp.dot, preferred_element_type=F32)
+    return dot(jnp.concatenate([upper, upper], axis=1), table_ref[...]) + dot(lower, table_ref[0 : 2 * INNER])
 
 
 def complex_product(a, b):
@@ -127,12 +134,11 @@
     return jnp.concatenate([ar * br - ai * bi, ar * bi + ai * br], axis=1)
 
 
-def chunks(body):
-    def step(j, carry):
-        body(pl.ds(pl.multiple_of(j * 8, 8), 8))
-        return carry
-
-    lax.fori_loop(0, OUTER // 8, step, 0)
+CHUNK = 16
+
+
+def chunks():
+    return [slice(k, k + CHUNK) for k in range(0, OUTER, CHUNK)]
 
 
 def flat(value):
@@ -148,7 +154,7 @@
 
 def filter_kernel(
     got_ref,
-    taps_ref,
+    taps_hbm,
     bias_ref,
     turn_hbm,
     inner_hbm,
@@ -158,65 +164,70 @@
     half_ref,
     turn_ref,
     inner_ref,
+    spec_ref,
     sems,
-    spec_ref,
-    out_sems,
+    spec_sems,
+    taps_ref,
 ):
-    turn_copy, inner_copy = fetch((turn_hbm, inner_hbm), (turn_ref, inner_ref), sems)
-    twr_ref, twi_ref, ahead, back = turn_ref.at[0], turn_ref.at[1], inner_ref.at[0], inner_ref.at[1]
     first = pl.multiple_of(lax.axis_index("seq") * 32, 32)
-    bias = column_of(bias_ref, first)
-    own_taps = taps_ref[pl.ds(first, 32), :]
+    sources = (turn_hbm, taps_hbm.at[pl.ds(first, 32), :], inner_hbm)
+    copies = fetch(sources, (turn_ref, taps_ref, inner_ref), sems)
+    ahead, back = inner_ref.at[0], inner_ref.at[1]
     for b in range(16):
         for h in range(2):
             time_ref[2 * b + h] = got_ref[b, 0:32, h * INNER : (h + 1) * INNER].astype(F32)
-    turn_copy.wait()
-    outer_ahead(time_ref, mid_ref, half_ref, twr_ref, twi_ref)
-    inner_copy.wait()
-
-    def combine(ks):
+    bias = column_of(bias_ref, first)
+    lift = jnp.concatenate([jnp.broadcast_to(bias, (32, INNER)), jnp.zeros((32, INNER), F32)], axis=1)
+    outer_ahead(time_ref, mid_ref, half_ref, turn_ref, copies[0])
+    copies[1].wait()
+    copies[2].wait()
+    for ks in chunks():
         long = product(flat(mid_ref[ks]), ahead)
-        lift = jnp.concatenate([jnp.broadcast_to(bias, (32, INNER)), jnp.zeros((32, INNER), F32)], axis=1)
-        long = long + jnp.tile(lift, (8, 1))
-        taps = own_taps[None]
-        tr, ti = twr_ref[ks, :][:, None, :], twi_ref[ks, :][:, None, :]
+        long = long + jnp.tile(lift, (CHUNK, 1))
+        taps = taps_ref[...][None]
+        tr, ti = turn_ref[0, ks, :][:, None, :], turn_ref[1, ks, :][:, None, :]
         short = product(flat(jnp.concatenate([taps * tr, taps * ti], axis=2)), ahead)
-        mid_ref[ks] = product(complex_product(long, short), back).reshape(8, 32, 2 * INNER)
-
-    chunks(combine)
-    outer_back(mid_ref, time_ref, half_ref, twr_ref, twi_ref)
-    outer_ahead(time_ref, mid_ref, half_ref, twr_ref, twi_ref)
-
-    copies = []
-    for j in range(OUTER // 8):
-        ks = slice(8 * j, 8 * j + 8)
-        spec_ref[ks] = product(flat(mid_ref[ks]), ahead).reshape(8, 32, 2 * INNER)
-        copies.append(pltpu.make_async_copy(spec_ref.at[ks], spec_hbm.at[ks], out_sems.at[j]))
-        copies[-1].start()
-    for copy in copies:
+        mid_ref[ks] = product(complex_product(long, short), back).reshape(CHUNK, 32, 2 * INNER)
+    outer_back(mid_ref, time_ref, half_ref, turn_ref)
+    outer_ahead(time_ref, mid_ref, half_ref, turn_ref)
+    written = []
+    for j, ks in enumerate(chunks()):
+        spec_ref[ks] = product(flat(mid_ref[ks]), ahead).reshape(CHUNK, 32, 2 * INNER)
+        written.append(pltpu.make_async_copy(spec_ref.at[ks], spec_hbm.at[ks], spec_sems.at[j]))
+        written[-1].start()
+    for copy in written:
         copy.wait()
 
 
 def signal_kernel(
-    got_ref, spec_hbm, turn_hbm, inner_hbm, mixed_ref, time_ref, mid_ref, half_ref, turn_ref, inner_ref, sems, spec_ref
+    got_ref,
+    spec_hbm,
+    turn_hbm,
+    inner_hbm,
+    mixed_ref,
+    time_ref,
+    mid_ref,
+    half_ref,
+    turn_ref,
+    inner_ref,
+    spec_ref,
+    sems,
+    spec_sems,
 ):
-    copies = fetch((turn_hbm, inner_hbm, spec_hbm), (turn_ref, inner_ref, spec_ref), sems)
-    twr_ref, twi_ref, ahead, back = turn_ref.at[0], turn_ref.at[1], inner_ref.at[0], inner_ref.at[1]
+    copies = fetch((turn_hbm, inner_hbm), (turn_ref, inner_ref), sems)
+    spec_copies = fetch([spec_hbm.at[ks] for ks in chunks()], [spec_ref.at[ks] for ks in chunks()], spec_sems)
+    ahead, back = inner_ref.at[0], inner_ref.at[1]
     for b in range(16):
         for h in range(2):
             time_ref[2 * b + h] = got_ref[b, 0:32, h * INNER : (h + 1) * INNER].astype(F32)
-    copies[0].wait()
-    outer_ahead(time_ref, mid_ref, half_ref, twr_ref, twi_ref)
+    outer_ahead(time_ref, mid_ref, half_ref, turn_ref, copies[0])
     copies[1].wait()
-    copies[2].wait()
-
-    def combine(ks):
+    for ks, copy in zip(chunks(), spec_copies, strict=True):
         spec = product(flat(mid_ref[ks]), ahead)
+        copy.wait()
         joint = complex_product(spec, flat(spec_ref[ks]))
-        mid_ref[ks] = product(joint, back).reshape(8, 32, 2 * INNER)
-
-    chunks(combine)
-    outer_back(mid_ref, time_ref, half_ref, twr_ref, twi_ref)
+        mid_ref[ks] = product(joint, back).reshape(CHUNK, 32, 2 * INNER)
+    outer_back(mid_ref, time_ref, half_ref, turn_ref)
     for b in range(16):
         for h in range(2):
             cols = slice(h * INNER, (h + 1) * INNER)
@@ -248,8 +259,10 @@
     pltpu.VMEM((OUTER, 32, 2 * INNER), F32),
     pltpu.VMEM((4, 4, 8, 2, 8, INNER), F32),
     pltpu.VMEM((2, OUTER, INNER), F32),
-    pltpu.VMEM((2, 6 * INNER, 2 * INNER), BF16),
+    pltpu.VMEM((2, 4 * INNER, 2 * INNER), BF16),
+    pltpu.VMEM((OUTER, 32, 2 * INNER), F32),
     pltpu.SemaphoreType.DMA((3,)),
+    pltpu.SemaphoreType.DMA((OUTER // CHUNK,)),
 ]
 
 
@@ -257,13 +270,13 @@
     return pl.pallas_call(
         filter_kernel,
         out_shape=pltpu.HBM((OUTER, 32, 2 * INNER), F32),
-        in_specs=vmem(3) + hbm(2),
+        in_specs=[*vmem(1), *hbm(1), *vmem(1), *hbm(2)],
         out_specs=hbm(1)[0],
-        scratch_shapes=[*SCRATCH, pltpu.VMEM((OUTER, 32, 2 * INNER), F32), pltpu.SemaphoreType.DMA((4,))],
+        scratch_shapes=[*SCRATCH, pltpu.VMEM((32, INNER), F32)],
         cost_estimate=pl.CostEstimate(flops=2_000_000_000, bytes_accessed=3_000_000, transcendentals=0),
         compiler_params=limit(8),
         name="filter_spectrum",
-    )(got, taps, bias, *[stay(value) for value in consts])
+    )(got, stay(taps), bias, *[stay(value) for value in consts])
 
 
 def gated_convolution(got, spec, consts):
@@ -272,7 +285,7 @@
         out_shape=jax.ShapeDtypeStruct((16, 32, 256), BF16),
         in_specs=vmem(1) + hbm(3),
         out_specs=vmem(1)[0],
-        scratch_shapes=[*SCRATCH, pltpu.VMEM((OUTER, 32, 2 * INNER), F32)],
+        scratch_shapes=SCRATCH,
         cost_estimate=pl.CostEstimate(flops=1_000_000_000, bytes_accessed=3_000_000, transcendentals=0),
         compiler_params=limit(8),
     )(got, stay(spec), *[stay(value) for value in consts])

time: 100 us -> 99.2 us (level)
  Pallas kernels: 16.9 us -> 14.7 us
  waiting for transfers between devices: 36.8 us -> 38 us
    all_to_all x2, waiting for transfers between devices: 5.22 us -> 6.34 us  [exchange(): return lax.all_to_all(value, axis, split_axis=0, concat_axis=0, tiled=True)]
    pallas_call x1, Pallas kernels: 6.3 us -> 5.19 us  [filter_spectrum(): pl.pallas_call(filter_kernel, out_shape=pltpu.HBM((OUTER, 32, 2 * INNER),...]
    pallas_call x1, Pallas kernels: 4.43 us -> 3.34 us  [gated_convolution(): pl.pallas_call(signal_kernel, out_shape=jax.ShapeDtypeStruct((16, 32, 256...]
  transfers between devices with their start and end apart: 24 -> 24, of which waited for: 14 -> 14; matrix products, arithmetic and copies ran while one was open for 0% -> 0% of each run, Pallas kernels for 8% -> 7%
where the time goes in v4:
time: 99.2 us; the launch traced here: 98.7 us
  starting transfers between devices  45.3 us (46%)
  waiting for transfers between devices  38 us (38%)
  Pallas kernels  14.7 us (15%)
    all_to_all x2, starting transfers between devices, exchange(): return lax.all_to_all(value, axis, split_axis=0, concat_axis=0, tiled=True)  24.4 us
    ppermute x15, waiting for transfers between devices, over_seq(): return lax.ppermute(value, 'seq', pairs)  22.9 us
    ppermute x15, starting transfers between devices, over_seq(): return lax.ppermute(value, 'seq', pairs)  13.8 us
    ppermute x7, waiting for transfers between devices, over_chan(): return lax.ppermute(value, 'chan', pairs)  8.72 us
    ppermute x7, starting transfers between devices, over_chan(): return lax.ppermute(value, 'chan', pairs)  7.06 us
    all_to_all x2, waiting for transfers between devices, exchange(): return lax.all_to_all(value, axis, split_axis=0, concat_axis=0, tiled=True)  6.34 us
    pallas_call x1, Pallas kernels, filter_spectrum(): pl.pallas_call(filter_kernel, out_shape=pltpu.HBM((OUTER, 32, 2 * INNER),...  5.19 us
    pallas_call x1, Pallas kernels, gated_convolution(): pl.pallas_call(signal_kernel, out_shape=jax.ShapeDtypeStruct((16, 32, 256...  3.34 us
  transfers between devices with their start and end apart: 24, of which 14 were waited for; matrix products, arithmetic and copies ran while one was open for 0% of the time, Pallas kernels for 7%

profile of v4, /device:TPU:1, one launch (start us, length us, event | category | flops | bytes accessed | tf_op | source)
XLA Modules:
  0.0 98.7 jit_solution(15129239106758015583)
XLA Ops:
  0.6 2.1 %pack.1 = (bf16[16,96,256]{2,1,0:T(8,128)(2,1)}, f32[8,256]{1,0:T(8,128)S(1)}, f32[16,32,256]{2,1,0:T(8,128)S(1)}) custom-call(bf16[16,32,256]{2,1,0:T(8,128)(2,1)} %bitcast.8, bf16[16,32,256]{2,1,0:T(8,128)(2,1)} %bitcast.9, bf16[16,256,256]{2,1,0:T(8,128)(2,1)} %bitcast.7, f32[4,128]{1,0:T(4,128)} %bitcast.11), custom_call_target="tpu_custom_call" | custom-call | tf_op jit(solution)/shard_map/pack/pallas_call | solution.py:330
  2.8 0.0 copy-start
  2.8 9.1 %all-to-all-start.1 = ((bf16[16,96,256]{2,1,0:T(8,128)(2,1)}), bf16[16,96,256]{2,1,0:T(8,128)(2,1)S(1)}, u32[]{:S(2)}, u32[]{:S(2)}) async-start(bf16[16,96,256]{2,1,0:T(8,128)(2,1)} %get-tuple-element.7), calls=%async_computation.1 | async-start | bytes 1572864 | tf_op jit(solution)/shard_map/all_to_all | solution.py:441
  11.9 0.7 collective-permute-start
  12.7 3.8 %collective-permute-done = f32[8,256]{1,0:T(8,128)S(1)} collective-permute-done((f32[8,256]{1,0:T(8,128)S(1)}, f32[8,256]{1,0:T(8,128)S(1)}, u32[]{:S(2)}, u32[]{:S(2)}) %collective-permute-start) | collective-permute-done | bytes 8224 | tf_op jit(solution)/shard_map/ppermute | solution.py:375
  16.4 2.9 %collective-permute-start.3 = (f32[8,256]{1,0:T(8,128)S(1)}, f32[8,256]{1,0:T(8,128)S(1)}, u32[]{:S(2)}, u32[]{:S(2)}) collective-permute-start(f32[8,256]{1,0:T(8,128)S(1)} %add.3.s0), channel_id=1, source_target_pairs={{0,2},{1,3},{2,0},{3,1},{4,6},{5,7},{6,4},{7,5},{8,10},{9,11},{10,... | collective-permute-start | bytes 24584 | tf_op jit(solution)/shard_map/ppermute | solution.py:375
  19.3 0.8 collective-permute-start.2
  20.1 0.7 collective-permute-start.1
  20.8 0.0 collective-permute-done.3.s3
  20.8 1.3 %collective-permute-done.2.s2 = f32[8,256]{1,0:T(8,128)S(1)} collective-permute-done((f32[8,256]{1,0:T(8,128)S(1)}, f32[8,256]{1,0:T(8,128)S(1)}, u32[]{:S(2)}, u32[]{:S(2)}) %collective-permute-start.2) | collective-permute-done | bytes 8224 | tf_op jit(solution)/shard_map/ppermute | solution.py:375
  22.1 1.7 %collective-permute-done.1.s1 = f32[8,256]{1,0:T(8,128)S(1)} collective-permute-done((f32[8,256]{1,0:T(8,128)S(1)}, f32[8,256]{1,0:T(8,128)S(1)}, u32[]{:S(2)}, u32[]{:S(2)}) %collective-permute-start.1) | collective-permute-done | bytes 8224 | tf_op jit(solution)/shard_map/ppermute | solution.py:375
  23.8 1.8 %normalise.1 = bf16[16,64,256]{2,1,0:T(8,128)(2,1)} custom-call(f32[16,32,256]{2,1,0:T(8,128)S(1)} %get-tuple-element.5.lifted_ref, f32[8,256]{1,0:T(8,128)S(1)} %add.3.s0, f32[8,256]{1,0:T(8,128)S(1)} %collective-permute-done.1.s1, f32[8,256]{1,0:T(8,128)S(1)} %collective-permute-done.2.s2, f32[8,256]{1,0:T(8,128)S(1)} %collective-permute-done.3.s3, ...), custom_call_target="tpu_custom_call" | custom-call | tf_op jit(solution)/shard_map/normalise/pallas_call | solution.py:350
  25.6 0.6 all-to-all-done.1.got_ref
  26.1 15.3 %all-to-all-start = ((bf16[16,64,256]{2,1,0:T(8,128)(2,1)}), bf16[16,64,256]{2,1,0:T(8,128)(2,1)S(1)}, u32[]{:S(2)}, u32[]{:S(2)}) async-start(bf16[16,64,256]{2,1,0:T(8,128)(2,1)} %normalise.1), calls=%async_computation | async-start | bytes 1048576 | tf_op jit(solution)/shard_map/all_to_all | solution.py:441
  41.4 5.2 %filter_spectrum.1.spec_hbm = f32[32,32,256]{2,1,0:T(8,128)} custom-call(bf16[16,96,256]{2,1,0:T(8,128)(2,1)S(1)} %all-to-all-done.1.got_ref, f32[512,128]{1,0:T(8,128)} %taps_hbm.1, f32[1,512]{1,0:T(1,128)S(1)} %bitcast.6, f32[2,32,128]{2,1,0:T(8,128)} %constant.4.clone.turn_hbm, bf16[2,512,256]{2,1,0:T(8,128)(2,1)} %constant.5.clone.inner_hbm), custom_call_target="tpu_custom_call" | custom-call | flops 2000000000 | bytes 3000000 | tf_op jit(solution)/shard_map/filter_spectrum/pallas_call | solution.py:270
  46.6 5.8 %all-to-all-done.got_ref = bf16[16,64,256]{2,1,0:T(8,128)(2,1)S(1)} async-done(((bf16[16,64,256]{2,1,0:T(8,128)(2,1)}), bf16[16,64,256]{2,1,0:T(8,128)(2,1)S(1)}, u32[]{:S(2)}, u32[]{:S(2)}) %all-to-all-start) | async-done | bytes 524320 | tf_op jit(solution)/shard_map/all_to_all | solution.py:441
  52.4 3.3 %shard_map.104.refs_0_ = bf16[16,32,256]{2,1,0:T(8,128)(2,1)S(1)} custom-call(bf16[16,64,256]{2,1,0:T(8,128)(2,1)S(1)} %all-to-all-done.got_ref, f32[32,32,256]{2,1,0:T(8,128)} %filter_spectrum.1.spec_hbm, f32[2,32,128]{2,1,0:T(8,128)} %constant.4.clone.turn_hbm, bf16[2,512,256]{2,1,0:T(8,128)(2,1)} %constant.5.clone.inner_hbm), custom_call_target="tpu_custom_call" | custom-call | flops 1000000000 | bytes 3000000 | tf_op jit(solution)/shard_map/pallas_call | solution.py:283
  55.8 1.4 %collective-permute-start.11 = (bf16[16,32,256]{2,1,0:T(8,128)(2,1)S(1)}, bf16[16,32,256]{2,1,0:T(8,128)(2,1)S(1)}, u32[]{:S(2)}, u32[]{:S(2)}) collective-permute-start(bf16[16,32,256]{2,1,0:T(8,128)(2,1)S(1)} %shard_map.104.refs_0_), channel_id=1, source_target_pairs={{0,32},{8,40},{16,48},{24,56},{32,0},{40,8},{48,16},{56,24},{64,96... | collective-permute-start | bytes 786440 | tf_op jit(solution)/shard_map/ppermute | solution.py:370
  57.2 0.9 collective-permute-start.9
  58.1 0.5 collective-permute-start.7
  58.7 0.3 collective-permute-start.21
  59.0 1.7 %collective-permute-start.20 = (bf16[16,64,256]{2,1,0:T(8,128)(2,1)S(1)}, bf16[16,64,256]{2,1,0:T(8,128)(2,1)S(1)}, u32[]{:S(2)}, u32[]{:S(2)}) collective-permute-start(bf16[16,64,256]{2,1,0:T(8,128)(2,1)S(1)} %slice.4.refs_16_), channel_id=1, source_target_pairs={{0,3},{1,0},{2,1},{3,2},{4,7},{5,4},{6,5},{7,6},{8,11},{9,8},{10,9... | collective-permute-start | bytes 1572872 | tf_op jit(solution)/shard_map/ppermute | solution.py:375
  60.6 3.2 %collective-permute-done.11.refs_8_ = bf16[16,32,256]{2,1,0:T(8,128)(2,1)S(1)} collective-permute-done((bf16[16,32,256]{2,1,0:T(8,128)(2,1)S(1)}, bf16[16,32,256]{2,1,0:T(8,128)(2,1)S(1)}, u32[]{:S(2)}, u32[]{:S(2)}) %collective-permute-start.11) | collective-permute-done | bytes 262176 | tf_op jit(solution)/shard_map/ppermute | solution.py:370
  63.8 0.0 collective-permute-start.19
  63.8 6.5 %collective-permute-done.9.refs_6_ = bf16[16,32,256]{2,1,0:T(8,128)(2,1)S(1)} collective-permute-done((bf16[16,32,256]{2,1,0:T(8,128)(2,1)S(1)}, bf16[16,32,256]{2,1,0:T(8,128)(2,1)S(1)}, u32[]{:S(2)}, u32[]{:S(2)}) %collective-permute-start.9) | collective-permute-done | bytes 262176 | tf_op jit(solution)/shard_map/ppermute | solution.py:370
  70.3 0.0 collective-permute-start.5
  70.3 1.0 collective-permute-done.7.refs_4_
  71.3 0.4 collective-permute-start.4
  71.7 7.3 %collective-permute-done.5.refs_2_ = bf16[16,32,256]{2,1,0:T(8,128)(2,1)S(1)} collective-permute-done((bf16[16,32,256]{2,1,0:T(8,128)(2,1)S(1)}, bf16[16,32,256]{2,1,0:T(8,128)(2,1)S(1)}, u32[]{:S(2)}, u32[]{:S(2)}) %collective-permute-start.5) | collective-permute-done | bytes 262176 | tf_op jit(solution)/shard_map/ppermute | solution.py:370
  79.0 1.8 %collective-permute-start.12 = (bf16[16,32,256]{2,1,0:T(8,128)(2,1)S(1)}, bf16[16,32,256]{2,1,0:T(8,128)(2,1)S(1)}, u32[]{:S(2)}, u32[]{:S(2)}) collective-permute-start(bf16[16,32,256]{2,1,0:T(8,128)(2,1)S(1)} %collective-permute-done.11.refs_8_), channel_id=1, source_target_pairs={{0,8},{8,0},{16,24},{24,16},{32,40},{40,32},{48,56},{56,48},{64,72... | collective-permute-start | bytes 786440 | tf_op jit(solution)/shard_map/ppermute | solution.py:370
  80.8 0.1 collective-permute-start.10
  80.9 0.8 collective-permute-done.20.refs_18_
  81.7 2.6 %collective-permute-start.15 = (bf16[16,32,256]{2,1,0:T(8,128)(2,1)S(1)}, bf16[16,32,256]{2,1,0:T(8,128)(2,1)S(1)}, u32[]{:S(2)}, u32[]{:S(2)}) collective-permute-start(bf16[16,32,256]{2,1,0:T(8,128)(2,1)S(1)} %collective-permute-done.5.refs_2_), channel_id=1, source_target_pairs={{0,48},{8,56},{16,0},{24,8},{32,16},{40,24},{48,32},{56,40},{64,11... | collective-permute-start | bytes 786440 | tf_op jit(solution)/shard_map/ppermute | solution.py:370
  84.2 1.1 %collective-permute-done.19.refs_17_ = bf16[16,64,256]{2,1,0:T(8,128)(2,1)S(1)} collective-permute-done((bf16[16,64,256]{2,1,0:T(8,128)(2,1)S(1)}, bf16[16,64,256]{2,1,0:T(8,128)(2,1)S(1)}, u32[]{:S(2)}, u32[]{:S(2)}) %collective-permute-start.19) | collective-permute-done | bytes 524320 | tf_op jit(solution)/shard_map/ppermute | solution.py:375
  85.4 0.8 collective-permute-start.13
  86.2 0.7 collective-permute-done.17.refs_14_
  86.9 2.4 %collective-permute-start.6 = (bf16[16,32,256]{2,1,0:T(8,128)(2,1)S(1)}, bf16[16,32,256]{2,1,0:T(8,128)(2,1)S(1)}, u32[]{:S(2)}, u32[]{:S(2)}) collective-permute-start(bf16[16,32,256]{2,1,0:T(8,128)(2,1)S(1)} %collective-permute-done.5.refs_2_), channel_id=1, source_target_pairs={{0,8},{8,0},{16,24},{24,16},{32,40},{40,32},{48,56},{56,48},{64,72... | collective-permute-start | bytes 786440 | tf_op jit(solution)/shard_map/ppermute | solution.py:370
  89.2 0.0 collective-permute-start.8
  89.2 0.0 collective-permute-done.10.refs_7_
  89.2 0.5 collective-permute-start.18
  89.8 1.0 collective-permute-start.16
  90.7 3.2 %collective-permute-done.13.refs_10_ = bf16[16,32,256]{2,1,0:T(8,128)(2,1)S(1)} collective-permute-done((bf16[16,32,256]{2,1,0:T(8,128)(2,1)S(1)}, bf16[16,32,256]{2,1,0:T(8,128)(2,1)S(1)}, u32[]{:S(2)}, u32[]{:S(2)}) %collective-permute-start.13) | collective-permute-done | bytes 262176 | tf_op jit(solution)/shard_map/ppermute | solution.py:370
  93.9 1.3 %collective-permute-start.14 = (bf16[16,32,256]{2,1,0:T(8,128)(2,1)S(1)}, bf16[16,32,256]{2,1,0:T(8,128)(2,1)S(1)}, u32[]{:S(2)}, u32[]{:S(2)}) collective-permute-start(bf16[16,32,256]{2,1,0:T(8,128)(2,1)S(1)} %collective-permute-done.13.refs_10_), channel_id=1, source_target_pairs={{0,8},{8,0},{16,24},{24,16},{32,40},{40,32},{48,56},{56,48},{64,72... | collective-permute-start | bytes 786440 | tf_op jit(solution)/shard_map/ppermute | solution.py:370
  95.3 0.0 collective-permute-done.8.refs_5_
  95.3 0.0 collective-permute-done.6.refs_3_
  95.3 0.0 collective-permute-done.18.refs_15_
  95.3 1.1 %collective-permute-done.14.refs_11_ = bf16[16,32,256]{2,1,0:T(8,128)(2,1)S(1)} collective-permute-done((bf16[16,32,256]{2,1,0:T(8,128)(2,1)S(1)}, bf16[16,32,256]{2,1,0:T(8,128)(2,1)S(1)}, u32[]{:S(2)}, u32[]{:S(2)}) %collective-permute-start.14) | collective-permute-done | bytes 262176 | tf_op jit(solution)/shard_map/ppermute | solution.py:370
  96.5 2.3 %weight_gradient.1 = (bf16[512,256]{1,0:T(8,128)(2,1)}, f32[256,512]{1,0:T(8,128)}) custom-call(bf16[16,32,256]{2,1,0:T(8,128)(2,1)S(1)} %shard_map.104.refs_0_, bf16[16,32,256]{2,1,0:T(8,128)(2,1)S(1)} %collective-permute-done.4.refs_1_, bf16[16,32,256]{2,1,0:T(8,128)(2,1)S(1)} %collective-permute-done.5.refs_2_, ...), custom_call_target="tpu_custom_call" | custom-call | flops 1000000000 | bytes 7000000 | tf_op jit(solution)/shard_map/weight_gradient/pallas_call | solution.py:428
  (9 shorter events, 0.1 us)
Async XLA Ops:
  2.8 38.7 %copy-start = (f32[512]{0:T(512)S(1)}, f32[512]{0:T(512)}, u32[]{:S(2)}) copy-start(f32[512]{0:T(512)} %param.13) | copy-start | bytes 6148
  2.8 23.4 %all-to-all-start.1 = ((bf16[16,96,256]{2,1,0:T(8,128)(2,1)}), bf16[16,96,256]{2,1,0:T(8,128)(2,1)S(1)}, u32[]{:S(2)}, u32[]{:S(2)}) async-start(bf16[16,96,256]{2,1,0:T(8,128)(2,1)} %get-tuple-element.7), calls=%async_computation.1 | async-start | bytes 1572864 | tf_op jit(solution)/shard_map/all_to_all | solution.py:441
  11.9 4.5 %collective-permute-start = (f32[8,256]{1,0:T(8,128)S(1)}, f32[8,256]{1,0:T(8,128)S(1)}, u32[]{:S(2)}, u32[]{:S(2)}) collective-permute-start(f32[8,256]{1,0:T(8,128)S(1)} %get-tuple-element.6), channel_id=1, source_target_pairs={{0,4},{1,5},{2,6},{3,7},{4,0},{5,1},{6,2},{7,3},{8,12},{9,13},{10,... | collective-permute-start | bytes 24584 | tf_op jit(solution)/shard_map/ppermute | solution.py:375
  16.4 4.4 %collective-permute-start.3 = (f32[8,256]{1,0:T(8,128)S(1)}, f32[8,256]{1,0:T(8,128)S(1)}, u32[]{:S(2)}, u32[]{:S(2)}) collective-permute-start(f32[8,256]{1,0:T(8,128)S(1)} %add.3.s0), channel_id=1, source_target_pairs={{0,2},{1,3},{2,0},{3,1},{4,6},{5,7},{6,4},{7,5},{8,10},{9,11},{10,... | collective-permute-start | bytes 24584 | tf_op jit(solution)/shard_map/ppermute | solution.py:375
  19.3 2.8 %collective-permute-start.2 = (f32[8,256]{1,0:T(8,128)S(1)}, f32[8,256]{1,0:T(8,128)S(1)}, u32[]{:S(2)}, u32[]{:S(2)}) collective-permute-start(f32[8,256]{1,0:T(8,128)S(1)} %add.3.s0), channel_id=1, source_target_pairs={{0,3},{1,0},{2,1},{3,2},{4,7},{5,4},{6,5},{7,6},{8,11},{9,8},{10,9... | collective-permute-start | bytes 24584 | tf_op jit(solution)/shard_map/ppermute | solution.py:375
  20.1 3.7 %collective-permute-start.1 = (f32[8,256]{1,0:T(8,128)S(1)}, f32[8,256]{1,0:T(8,128)S(1)}, u32[]{:S(2)}, u32[]{:S(2)}) collective-permute-start(f32[8,256]{1,0:T(8,128)S(1)} %add.3.s0), channel_id=1, source_target_pairs={{0,1},{1,2},{2,3},{3,0},{4,5},{5,6},{6,7},{7,4},{8,9},{9,10},{10,1... | collective-permute-start | bytes 24584 | tf_op jit(solution)/shard_map/ppermute | solution.py:375
  26.1 26.3 %all-to-all-start = ((bf16[16,64,256]{2,1,0:T(8,128)(2,1)}), bf16[16,64,256]{2,1,0:T(8,128)(2,1)S(1)}, u32[]{:S(2)}, u32[]{:S(2)}) async-start(bf16[16,64,256]{2,1,0:T(8,128)(2,1)} %normalise.1), calls=%async_computation | async-start | bytes 1048576 | tf_op jit(solution)/shard_map/all_to_all | solution.py:441
  55.8 8.0 %collective-permute-start.11 = (bf16[16,32,256]{2,1,0:T(8,128)(2,1)S(1)}, bf16[16,32,256]{2,1,0:T(8,128)(2,1)S(1)}, u32[]{:S(2)}, u32[]{:S(2)}) collective-permute-start(bf16[16,32,256]{2,1,0:T(8,128)(2,1)S(1)} %shard_map.104.refs_0_), channel_id=1, source_target_pairs={{0,32},{8,40},{16,48},{24,56},{32,0},{40,8},{48,16},{56,24},{64,96... | collective-permute-start | bytes 786440 | tf_op jit(solution)/shard_map/ppermute | solution.py:370
  57.2 13.1 %collective-permute-start.9 = (bf16[16,32,256]{2,1,0:T(8,128)(2,1)S(1)}, bf16[16,32,256]{2,1,0:T(8,128)(2,1)S(1)}, u32[]{:S(2)}, u32[]{:S(2)}) collective-permute-start(bf16[16,32,256]{2,1,0:T(8,128)(2,1)S(1)} %shard_map.104.refs_0_), channel_id=1, source_target_pairs={{0,48},{8,56},{16,0},{24,8},{32,16},{40,24},{48,32},{56,40},{64,11... | collective-permute-start | bytes 786440 | tf_op jit(solution)/shard_map/ppermute | solution.py:370
  58.1 13.1 %collective-permute-start.7 = (bf16[16,32,256]{2,1,0:T(8,128)(2,1)S(1)}, bf16[16,32,256]{2,1,0:T(8,128)(2,1)S(1)}, u32[]{:S(2)}, u32[]{:S(2)}) collective-permute-start(bf16[16,32,256]{2,1,0:T(8,128)(2,1)S(1)} %shard_map.104.refs_0_), channel_id=1, source_target_pairs={{0,16},{8,24},{16,32},{24,40},{32,48},{40,56},{48,0},{56,8},{64,80... | collective-permute-start | bytes 786440 | tf_op jit(solution)/shard_map/ppermute | solution.py:370
  58.7 22.1 %collective-permute-start.21 = (bf16[16,64,256]{2,1,0:T(8,128)(2,1)S(1)}, bf16[16,64,256]{2,1,0:T(8,128)(2,1)S(1)}, u32[]{:S(2)}, u32[]{:S(2)}) collective-permute-start(bf16[16,64,256]{2,1,0:T(8,128)(2,1)S(1)} %slice.4.refs_16_), channel_id=1, source_target_pairs={{0,2},{1,3},{2,0},{3,1},{4,6},{5,7},{6,4},{7,5},{8,10},{9,11},{10,... | collective-permute-start | bytes 1572872 | tf_op jit(solution)/shard_map/ppermute | solution.py:375
  59.0 22.7 %collective-permute-start.20 = (bf16[16,64,256]{2,1,0:T(8,128)(2,1)S(1)}, bf16[16,64,256]{2,1,0:T(8,128)(2,1)S(1)}, u32[]{:S(2)}, u32[]{:S(2)}) collective-permute-start(bf16[16,64,256]{2,1,0:T(8,128)(2,1)S(1)} %slice.4.refs_16_), channel_id=1, source_target_pairs={{0,3},{1,0},{2,1},{3,2},{4,7},{5,4},{6,5},{7,6},{8,11},{9,8},{10,9... | collective-permute-start | bytes 1572872 | tf_op jit(solution)/shard_map/ppermute | solution.py:375
  63.8 21.6 %collective-permute-start.19 = (bf16[16,64,256]{2,1,0:T(8,128)(2,1)S(1)}, bf16[16,64,256]{2,1,0:T(8,128)(2,1)S(1)}, u32[]{:S(2)}, u32[]{:S(2)}) collective-permute-start(bf16[16,64,256]{2,1,0:T(8,128)(2,1)S(1)} %slice.4.refs_16_), channel_id=1, source_target_pairs={{0,1},{1,2},{2,3},{3,0},{4,5},{5,6},{6,7},{7,4},{8,9},{9,10},{10,1... | collective-permute-start | bytes 1572872 | tf_op jit(solution)/shard_map/ppermute | solution.py:375
  70.3 8.7 %collective-permute-start.5 = (bf16[16,32,256]{2,1,0:T(8,128)(2,1)S(1)}, bf16[16,32,256]{2,1,0:T(8,128)(2,1)S(1)}, u32[]{:S(2)}, u32[]{:S(2)}) collective-permute-start(bf16[16,32,256]{2,1,0:T(8,128)(2,1)S(1)} %shard_map.104.refs_0_), channel_id=1, source_target_pairs={{0,64},{8,72},{16,80},{24,88},{32,96},{40,104},{48,112},{56,120},{... | collective-permute-start | bytes 786440 | tf_op jit(solution)/shard_map/ppermute | solution.py:370
  71.3 7.8 %collective-permute-start.4 = (bf16[16,32,256]{2,1,0:T(8,128)(2,1)S(1)}, bf16[16,32,256]{2,1,0:T(8,128)(2,1)S(1)}, u32[]{:S(2)}, u32[]{:S(2)}) collective-permute-start(bf16[16,32,256]{2,1,0:T(8,128)(2,1)S(1)} %shard_map.104.refs_0_), channel_id=1, source_target_pairs={{0,8},{8,0},{16,24},{24,16},{32,40},{40,32},{48,56},{56,48},{64,72... | collective-permute-start | bytes 786440 | tf_op jit(solution)/shard_map/ppermute | solution.py:370
  79.0 7.9 %collective-permute-start.17 = (bf16[16,32,256]{2,1,0:T(8,128)(2,1)S(1)}, bf16[16,32,256]{2,1,0:T(8,128)(2,1)S(1)}, u32[]{:S(2)}, u32[]{:S(2)}) collective-permute-start(bf16[16,32,256]{2,1,0:T(8,128)(2,1)S(1)} %collective-permute-done.11.refs_8_), channel_id=1, source_target_pairs={{0,64},{8,72},{16,80},{24,88},{32,96},{40,104},{48,112},{56,120},{... | collective-permute-start | bytes 786440 | tf_op jit(solution)/shard_map/ppermute | solution.py:370
  79.0 10.2 %collective-permute-start.12 = (bf16[16,32,256]{2,1,0:T(8,128)(2,1)S(1)}, bf16[16,32,256]{2,1,0:T(8,128)(2,1)S(1)}, u32[]{:S(2)}, u32[]{:S(2)}) collective-permute-start(bf16[16,32,256]{2,1,0:T(8,128)(2,1)S(1)} %collective-permute-done.11.refs_8_), channel_id=1, source_target_pairs={{0,8},{8,0},{16,24},{24,16},{32,40},{40,32},{48,56},{56,48},{64,72... | collective-permute-start | bytes 786440 | tf_op jit(solution)/shard_map/ppermute | solution.py:370
  80.8 8.4 %collective-permute-start.10 = (bf16[16,32,256]{2,1,0:T(8,128)(2,1)S(1)}, bf16[16,32,256]{2,1,0:T(8,128)(2,1)S(1)}, u32[]{:S(2)}, u32[]{:S(2)}) collective-permute-start(bf16[16,32,256]{2,1,0:T(8,128)(2,1)S(1)} %collective-permute-done.9.refs_6_), channel_id=1, source_target_pairs={{0,8},{8,0},{16,24},{24,16},{32,40},{40,32},{48,56},{56,48},{64,72... | collective-permute-start | bytes 786440 | tf_op jit(solution)/shard_map/ppermute | solution.py:370
  81.7 8.1 %collective-permute-start.15 = (bf16[16,32,256]{2,1,0:T(8,128)(2,1)S(1)}, bf16[16,32,256]{2,1,0:T(8,128)(2,1)S(1)}, u32[]{:S(2)}, u32[]{:S(2)}) collective-permute-start(bf16[16,32,256]{2,1,0:T(8,128)(2,1)S(1)} %collective-permute-done.5.refs_2_), channel_id=1, source_target_pairs={{0,48},{8,56},{16,0},{24,8},{32,16},{40,24},{48,32},{56,40},{64,11... | collective-permute-start | bytes 786440 | tf_op jit(solution)/shard_map/ppermute | solution.py:370
  85.4 8.6 %collective-permute-start.13 = (bf16[16,32,256]{2,1,0:T(8,128)(2,1)S(1)}, bf16[16,32,256]{2,1,0:T(8,128)(2,1)S(1)}, u32[]{:S(2)}, u32[]{:S(2)}) collective-permute-start(bf16[16,32,256]{2,1,0:T(8,128)(2,1)S(1)} %collective-permute-done.5.refs_2_), channel_id=1, source_target_pairs={{0,16},{8,24},{16,32},{24,40},{32,48},{40,56},{48,0},{56,8},{64,80... | collective-permute-start | bytes 786440 | tf_op jit(solution)/shard_map/ppermute | solution.py:370
  86.9 8.4 %collective-permute-start.6 = (bf16[16,32,256]{2,1,0:T(8,128)(2,1)S(1)}, bf16[16,32,256]{2,1,0:T(8,128)(2,1)S(1)}, u32[]{:S(2)}, u32[]{:S(2)}) collective-permute-start(bf16[16,32,256]{2,1,0:T(8,128)(2,1)S(1)} %collective-permute-done.5.refs_2_), channel_id=1, source_target_pairs={{0,8},{8,0},{16,24},{24,16},{32,40},{40,32},{48,56},{56,48},{64,72... | collective-permute-start | bytes 786440 | tf_op jit(solution)/shard_map/ppermute | solution.py:370
  89.2 6.1 %collective-permute-start.8 = (bf16[16,32,256]{2,1,0:T(8,128)(2,1)S(1)}, bf16[16,32,256]{2,1,0:T(8,128)(2,1)S(1)}, u32[]{:S(2)}, u32[]{:S(2)}) collective-permute-start(bf16[16,32,256]{2,1,0:T(8,128)(2,1)S(1)} %collective-permute-done.7.refs_4_), channel_id=1, source_target_pairs={{0,8},{8,0},{16,24},{24,16},{32,40},{40,32},{48,56},{56,48},{64,72... | collective-permute-start | bytes 786440 | tf_op jit(solution)/shard_map/ppermute | solution.py:370
  89.2 6.1 %collective-permute-start.18 = (bf16[16,32,256]{2,1,0:T(8,128)(2,1)S(1)}, bf16[16,32,256]{2,1,0:T(8,128)(2,1)S(1)}, u32[]{:S(2)}, u32[]{:S(2)}) collective-permute-start(bf16[16,32,256]{2,1,0:T(8,128)(2,1)S(1)} %collective-permute-done.17.refs_14_), channel_id=1, source_target_pairs={{0,8},{8,0},{16,24},{24,16},{32,40},{40,32},{48,56},{56,48},{64,72... | collective-permute-start | bytes 786440 | tf_op jit(solution)/shard_map/ppermute | solution.py:370
  89.8 5.6 %collective-permute-start.16 = (bf16[16,32,256]{2,1,0:T(8,128)(2,1)S(1)}, bf16[16,32,256]{2,1,0:T(8,128)(2,1)S(1)}, u32[]{:S(2)}, u32[]{:S(2)}) collective-permute-start(bf16[16,32,256]{2,1,0:T(8,128)(2,1)S(1)} %collective-permute-done.15.refs_12_), channel_id=1, source_target_pairs={{0,8},{8,0},{16,24},{24,16},{32,40},{40,32},{48,56},{56,48},{64,72... | collective-permute-start | bytes 786440 | tf_op jit(solution)/shard_map/ppermute | solution.py:370
  93.9 2.5 %collective-permute-start.14 = (bf16[16,32,256]{2,1,0:T(8,128)(2,1)S(1)}, bf16[16,32,256]{2,1,0:T(8,128)(2,1)S(1)}, u32[]{:S(2)}, u32[]{:S(2)}) collective-permute-start(bf16[16,32,256]{2,1,0:T(8,128)(2,1)S(1)} %collective-permute-done.13.refs_10_), channel_id=1, source_target_pairs={{0,8},{8,0},{16,24},{24,16},{32,40},{40,32},{48,56},{56,48},{64,72... | collective-permute-start | bytes 786440 | tf_op jit(solution)/shard_map/ppermute | solution.py:370

commit v5 on v4

--- a/solution.py
+++ b/solution.py
@@ -291,14 +291,23 @@
     )(got, stay(spec), *[stay(value) for value in consts])
 
 
-def pack_kernel(hidden_hbm, long_ref, up_ref, gain_hbm, payload_ref, squares_ref, lifted_ref, hidden, gain_ref, sems):
+def pack_kernel(
+    hidden_hbm, long_ref, up_ref, gain_hbm, payload_hbm, squares_ref, lifted_ref, hidden, gain_ref, held, sems, out_sems
+):
     chan = lax.axis_index("chan")
     pair = [pl.ds(pl.multiple_of((lax.bitwise_and(chan, 3) + 4 * z) * 32, 32), 32) for z in range(2)]
     sources = [gain_hbm, hidden_hbm, long_ref, up_ref.at[:, pair[0], :], up_ref.at[:, pair[1], :]]
-    targets = [gain_ref, hidden, *[payload_ref.at[:, 32 * i : 32 * i + 32, :] for i in range(3)]]
+    targets = [gain_ref, hidden, *[held.at[i] for i in range(3)]]
     copies = fetch(sources, targets, sems)
     copies[0].wait()
     gains = [jnp.broadcast_to(gain_ref[q : q + 1, :], (INNER, INNER)).T for q in range(4)]
+    leaving = []
+    for i in range(3):
+        copies[2 + i].wait()
+        leaving.append(
+            pltpu.make_async_copy(held.at[i], payload_hbm.at[:, 32 * i : 32 * i + 32, :], out_sems.at[i])
+        )
+        leaving[-1].start()
     copies[1].wait()
     total = jnp.zeros((8, 256), F32)
     for b in range(16):
@@ -309,7 +318,7 @@
         gain = gains[b // 4][32 * (b % 4) : 32 * (b % 4) + 32]
         lifted_ref[b] = states * jnp.concatenate([gain, gain], axis=1)
     squares_ref[...] = total
-    for copy in copies[2:]:
+    for copy in leaving:
         copy.wait()
 
 
@@ -335,11 +344,13 @@
             jax.ShapeDtypeStruct((16, 32, 256), F32),
         ),
         in_specs=hbm(4),
-        out_specs=tuple(vmem(3)),
+        out_specs=(*hbm(1), *vmem(2)),
         scratch_shapes=[
             pltpu.VMEM((16, 32, 256), BF16),
             pltpu.VMEM((4, INNER), F32),
+            pltpu.VMEM((3, 16, 32, 256), BF16),
             pltpu.SemaphoreType.DMA((5,)),
+            pltpu.SemaphoreType.DMA((3,)),
         ],
         compiler_params=limit(6),
         name="pack",
@@ -403,8 +414,7 @@
 def grad_kernel(mixed_keys, up_keys, *refs):
     seq, chan = lax.axis_index("seq"), lax.axis_index("chan")
     mixed_refs, up_refs = refs[: len(mixed_keys)], refs[len(mixed_keys) : len(mixed_keys) + len(up_keys)]
-    mixed_ref, grad_ref, rows_ref = refs[len(mixed_keys) + len(up_keys) :]
-    total = lax.dot_general(whole_rows(mixed_refs), whole_rows(up_refs), (((1,), (1,)), ((), ())), preferred_element_type=F32)
+    mixed_hbm, grad_hbm, rows_ref, grad_ref, mixed_sems, grad_sems = refs[len(mixed_keys) + len(up_keys) :]
 
     def source_place(dk, dz, dx):
         z = lax.bitwise_xor(seq // 8, dz)
@@ -412,15 +422,25 @@
         k = lax.bitwise_xor(lax.bitwise_and(seq, 1), dk)
         return pl.ds(pl.multiple_of((z * 8 + x * 2 + k) * 32, 32), 32)
 
-    for i, (ref, key) in enumerate(zip(mixed_refs, mixed_keys, strict=True)):
-        place = source_place(*key)
+    places = [source_place(*key) for key in mixed_keys]
+    sources = [ref.at[seq] for ref in mixed_refs]
+    copies = fetch(sources, [mixed_hbm.at[place, :] for place in places], mixed_sems)
+    total = lax.dot_general(
+        whole_rows(mixed_refs), whole_rows(up_refs), (((1,), (1,)), ((), ())), preferred_element_type=F32
+    )
+    for i, place in enumerate(places):
         rows_ref[place, :] = total[32 * i : 32 * i + 32]
-        mixed_ref[place, :] = ref[seq]
     turned_rows = rows_ref[...].T
     for i, (dy,) in enumerate(up_keys):
         for z in range(2):
+            n = 2 * i + z
             place = pl.ds(pl.multiple_of((4 * z + lax.bitwise_and(chan + dy, 3)) * 32, 32), 32)
-            grad_ref[place, :] = turned_rows[64 * i + 32 * z : 64 * i + 32 * z + 32]
+            grad_ref[32 * n : 32 * n + 32, :] = turned_rows[32 * n : 32 * n + 32]
+            source = grad_ref.at[32 * n : 32 * n + 32, :]
+            copies.append(pltpu.make_async_copy(source, grad_hbm.at[place, :], grad_sems.at[n]))
+            copies[-1].start()
+    for copy in copies:
+        copy.wait()
 
 
 def weight_gradient(mixed, up):
@@ -429,8 +449,13 @@
         functools.partial(grad_kernel, mixed_keys, up_keys),
         out_shape=(jax.ShapeDtypeStruct((512, 256), BF16), jax.ShapeDtypeStruct((256, 512), F32)),
         in_specs=vmem(len(mixed) + len(up)),
-        out_specs=tuple(vmem(2)),
-        scratch_shapes=[pltpu.VMEM((512, 256), F32)],
+        out_specs=tuple(hbm(2)),
+        scratch_shapes=[
+            pltpu.VMEM((512, 256), F32),
+            pltpu.VMEM((256, 512), F32),
+            pltpu.SemaphoreType.DMA((len(mixed),)),
+            pltpu.SemaphoreType.DMA((2 * len(up),)),
+        ],
         cost_estimate=pl.CostEstimate(flops=1_000_000_000, bytes_accessed=7_000_000, transcendentals=0),
         compiler_params=limit(16),
         name="weight_gradient",

time: 99.2 us -> 99.2 us (level)
  no operation moved by 1% of the time
where the time goes in v5:
time: 99.2 us; the launch traced here: 98.8 us
  starting transfers between devices  45.2 us (46%)
  waiting for transfers between devices  38.1 us (38%)
  Pallas kernels  14.8 us (15%)
    all_to_all x2, starting transfers between devices, exchange(): return lax.all_to_all(value, axis, split_axis=0, concat_axis=0, tiled=True)  24.4 us
    ppermute x15, waiting for transfers between devices, over_seq(): return lax.ppermute(value, 'seq', pairs)  23 us
    ppermute x15, starting transfers between devices, over_seq(): return lax.ppermute(value, 'seq', pairs)  13.7 us
    ppermute x7, waiting for transfers between devices, over_chan(): return lax.ppermute(value, 'chan', pairs)  8.76 us
    ppermute x7, starting transfers between devices, over_chan(): return lax.ppermute(value, 'chan', pairs)  7.06 us
    all_to_all x2, waiting for transfers between devices, exchange(): return lax.all_to_all(value, axis, split_axis=0, concat_axis=0, tiled=True)  6.34 us
    pallas_call x1, Pallas kernels, filter_spectrum(): pl.pallas_call(filter_kernel, out_shape=pltpu.HBM((OUTER, 32, 2 * INNER),...  5.19 us
    pallas_call x1, Pallas kernels, gated_convolution(): pl.pallas_call(signal_kernel, out_shape=jax.ShapeDtypeStruct((16, 32, 256...  3.34 us
  transfers between devices with their start and end apart: 24, of which 14 were waited for; matrix products, arithmetic and copies ran while one was open for 0% of the time, Pallas kernels for 7%

profile of v5, /device:TPU:1, one launch (start us, length us, event | category | flops | bytes accessed | tf_op | source)
XLA Modules:
  0.0 98.8 jit_solution(10609930265792612572)
XLA Ops:
  0.6 2.0 %pack.1 = (bf16[16,96,256]{2,1,0:T(8,128)(2,1)}, f32[8,256]{1,0:T(8,128)S(1)}, f32[16,32,256]{2,1,0:T(8,128)S(1)}) custom-call(bf16[16,32,256]{2,1,0:T(8,128)(2,1)} %bitcast.8, bf16[16,32,256]{2,1,0:T(8,128)(2,1)} %bitcast.9, bf16[16,256,256]{2,1,0:T(8,128)(2,1)} %bitcast.7, f32[4,128]{1,0:T(4,128)} %bitcast.11), custom_call_target="tpu_custom_call" | custom-call | tf_op jit(solution)/shard_map/pack/pallas_call | solution.py:339
  2.7 0.0 copy-start
  2.7 9.1 %all-to-all-start.1 = ((bf16[16,96,256]{2,1,0:T(8,128)(2,1)}), bf16[16,96,256]{2,1,0:T(8,128)(2,1)S(1)}, u32[]{:S(2)}, u32[]{:S(2)}) async-start(bf16[16,96,256]{2,1,0:T(8,128)(2,1)} %get-tuple-element.7), calls=%async_computation.1 | async-start | bytes 1572864 | tf_op jit(solution)/shard_map/all_to_all | solution.py:466
  11.8 0.7 collective-permute-start
  12.5 3.8 %collective-permute-done = f32[8,256]{1,0:T(8,128)S(1)} collective-permute-done((f32[8,256]{1,0:T(8,128)S(1)}, f32[8,256]{1,0:T(8,128)S(1)}, u32[]{:S(2)}, u32[]{:S(2)}) %collective-permute-start) | collective-permute-done | bytes 8224 | tf_op jit(solution)/shard_map/ppermute | solution.py:386
  16.3 2.9 %collective-permute-start.3 = (f32[8,256]{1,0:T(8,128)S(1)}, f32[8,256]{1,0:T(8,128)S(1)}, u32[]{:S(2)}, u32[]{:S(2)}) collective-permute-start(f32[8,256]{1,0:T(8,128)S(1)} %add.3.s0), channel_id=1, source_target_pairs={{0,2},{1,3},{2,0},{3,1},{4,6},{5,7},{6,4},{7,5},{8,10},{9,11},{10,... | collective-permute-start | bytes 24584 | tf_op jit(solution)/shard_map/ppermute | solution.py:386
  19.2 0.8 collective-permute-start.2
  20.0 0.7 collective-permute-start.1
  20.7 0.0 collective-permute-done.3.s3
  20.7 1.3 %collective-permute-done.2.s2 = f32[8,256]{1,0:T(8,128)S(1)} collective-permute-done((f32[8,256]{1,0:T(8,128)S(1)}, f32[8,256]{1,0:T(8,128)S(1)}, u32[]{:S(2)}, u32[]{:S(2)}) %collective-permute-start.2) | collective-permute-done | bytes 8224 | tf_op jit(solution)/shard_map/ppermute | solution.py:386
  22.0 1.7 %collective-permute-done.1.s1 = f32[8,256]{1,0:T(8,128)S(1)} collective-permute-done((f32[8,256]{1,0:T(8,128)S(1)}, f32[8,256]{1,0:T(8,128)S(1)}, u32[]{:S(2)}, u32[]{:S(2)}) %collective-permute-start.1) | collective-permute-done | bytes 8224 | tf_op jit(solution)/shard_map/ppermute | solution.py:386
  23.7 1.8 %normalise.1 = bf16[16,64,256]{2,1,0:T(8,128)(2,1)} custom-call(f32[16,32,256]{2,1,0:T(8,128)S(1)} %get-tuple-element.5.lifted_ref, f32[8,256]{1,0:T(8,128)S(1)} %add.3.s0, f32[8,256]{1,0:T(8,128)S(1)} %collective-permute-done.1.s1, f32[8,256]{1,0:T(8,128)S(1)} %collective-permute-done.2.s2, f32[8,256]{1,0:T(8,128)S(1)} %collective-permute-done.3.s3, ...), custom_call_target="tpu_custom_call" | custom-call | tf_op jit(solution)/shard_map/normalise/pallas_call | solution.py:361
  25.5 0.6 all-to-all-done.1.got_ref
  26.0 15.3 %all-to-all-start = ((bf16[16,64,256]{2,1,0:T(8,128)(2,1)}), bf16[16,64,256]{2,1,0:T(8,128)(2,1)S(1)}, u32[]{:S(2)}, u32[]{:S(2)}) async-start(bf16[16,64,256]{2,1,0:T(8,128)(2,1)} %normalise.1), calls=%async_computation | async-start | bytes 1048576 | tf_op jit(solution)/shard_map/all_to_all | solution.py:466
  41.3 5.2 %filter_spectrum.1.spec_hbm = f32[32,32,256]{2,1,0:T(8,128)} custom-call(bf16[16,96,256]{2,1,0:T(8,128)(2,1)S(1)} %all-to-all-done.1.got_ref, f32[512,128]{1,0:T(8,128)} %taps_hbm.1, f32[1,512]{1,0:T(1,128)S(1)} %bitcast.6, f32[2,32,128]{2,1,0:T(8,128)} %constant.4.clone.turn_hbm, bf16[2,512,256]{2,1,0:T(8,128)(2,1)} %constant.5.clone.inner_hbm), custom_call_target="tpu_custom_call" | custom-call | flops 2000000000 | bytes 3000000 | tf_op jit(solution)/shard_map/filter_spectrum/pallas_call | solution.py:270
  46.5 5.8 %all-to-all-done.got_ref = bf16[16,64,256]{2,1,0:T(8,128)(2,1)S(1)} async-done(((bf16[16,64,256]{2,1,0:T(8,128)(2,1)}), bf16[16,64,256]{2,1,0:T(8,128)(2,1)S(1)}, u32[]{:S(2)}, u32[]{:S(2)}) %all-to-all-start) | async-done | bytes 524320 | tf_op jit(solution)/shard_map/all_to_all | solution.py:466
  52.3 3.3 %shard_map.104.refs_0_ = bf16[16,32,256]{2,1,0:T(8,128)(2,1)S(1)} custom-call(bf16[16,64,256]{2,1,0:T(8,128)(2,1)S(1)} %all-to-all-done.got_ref, f32[32,32,256]{2,1,0:T(8,128)} %filter_spectrum.1.spec_hbm, f32[2,32,128]{2,1,0:T(8,128)} %constant.4.clone.turn_hbm, bf16[2,512,256]{2,1,0:T(8,128)(2,1)} %constant.5.clone.inner_hbm), custom_call_target="tpu_custom_call" | custom-call | flops 1000000000 | bytes 3000000 | tf_op jit(solution)/shard_map/pallas_call | solution.py:283
  55.7 1.4 %collective-permute-start.11 = (bf16[16,32,256]{2,1,0:T(8,128)(2,1)S(1)}, bf16[16,32,256]{2,1,0:T(8,128)(2,1)S(1)}, u32[]{:S(2)}, u32[]{:S(2)}) collective-permute-start(bf16[16,32,256]{2,1,0:T(8,128)(2,1)S(1)} %shard_map.104.refs_0_), channel_id=1, source_target_pairs={{0,32},{8,40},{16,48},{24,56},{32,0},{40,8},{48,16},{56,24},{64,96... | collective-permute-start | bytes 786440 | tf_op jit(solution)/shard_map/ppermute | solution.py:381
  57.1 0.9 collective-permute-start.9
  58.0 0.5 collective-permute-start.7
  58.6 0.3 collective-permute-start.21
  58.9 1.7 %collective-permute-start.20 = (bf16[16,64,256]{2,1,0:T(8,128)(2,1)S(1)}, bf16[16,64,256]{2,1,0:T(8,128)(2,1)S(1)}, u32[]{:S(2)}, u32[]{:S(2)}) collective-permute-start(bf16[16,64,256]{2,1,0:T(8,128)(2,1)S(1)} %slice.4.refs_16_), channel_id=1, source_target_pairs={{0,3},{1,0},{2,1},{3,2},{4,7},{5,4},{6,5},{7,6},{8,11},{9,8},{10,9... | collective-permute-start | bytes 1572872 | tf_op jit(solution)/shard_map/ppermute | solution.py:386
  60.5 3.2 %collective-permute-done.11.refs_8_ = bf16[16,32,256]{2,1,0:T(8,128)(2,1)S(1)} collective-permute-done((bf16[16,32,256]{2,1,0:T(8,128)(2,1)S(1)}, bf16[16,32,256]{2,1,0:T(8,128)(2,1)S(1)}, u32[]{:S(2)}, u32[]{:S(2)}) %collective-permute-start.11) | collective-permute-done | bytes 262176 | tf_op jit(solution)/shard_map/ppermute | solution.py:381
  63.7 0.0 collective-permute-start.19
  63.7 6.5 %collective-permute-done.9.refs_6_ = bf16[16,32,256]{2,1,0:T(8,128)(2,1)S(1)} collective-permute-done((bf16[16,32,256]{2,1,0:T(8,128)(2,1)S(1)}, bf16[16,32,256]{2,1,0:T(8,128)(2,1)S(1)}, u32[]{:S(2)}, u32[]{:S(2)}) %collective-permute-start.9) | collective-permute-done | bytes 262176 | tf_op jit(solution)/shard_map/ppermute | solution.py:381
  70.2 0.0 collective-permute-start.5
  70.2 1.0 collective-permute-done.7.refs_4_
  71.1 0.4 collective-permute-start.4
  71.6 7.3 %collective-permute-done.5.refs_2_ = bf16[16,32,256]{2,1,0:T(8,128)(2,1)S(1)} collective-permute-done((bf16[16,32,256]{2,1,0:T(8,128)(2,1)S(1)}, bf16[16,32,256]{2,1,0:T(8,128)(2,1)S(1)}, u32[]{:S(2)}, u32[]{:S(2)}) %collective-permute-start.5) | collective-permute-done | bytes 262176 | tf_op jit(solution)/shard_map/ppermute | solution.py:381
  78.9 1.8 %collective-permute-start.12 = (bf16[16,32,256]{2,1,0:T(8,128)(2,1)S(1)}, bf16[16,32,256]{2,1,0:T(8,128)(2,1)S(1)}, u32[]{:S(2)}, u32[]{:S(2)}) collective-permute-start(bf16[16,32,256]{2,1,0:T(8,128)(2,1)S(1)} %collective-permute-done.11.refs_8_), channel_id=1, source_target_pairs={{0,8},{8,0},{16,24},{24,16},{32,40},{40,32},{48,56},{56,48},{64,72... | collective-permute-start | bytes 786440 | tf_op jit(solution)/shard_map/ppermute | solution.py:381
  80.7 0.1 collective-permute-start.10
  80.8 0.8 collective-permute-done.20.refs_18_
  81.6 2.5 %collective-permute-start.15 = (bf16[16,32,256]{2,1,0:T(8,128)(2,1)S(1)}, bf16[16,32,256]{2,1,0:T(8,128)(2,1)S(1)}, u32[]{:S(2)}, u32[]{:S(2)}) collective-permute-start(bf16[16,32,256]{2,1,0:T(8,128)(2,1)S(1)} %collective-permute-done.5.refs_2_), channel_id=1, source_target_pairs={{0,48},{8,56},{16,0},{24,8},{32,16},{40,24},{48,32},{56,40},{64,11... | collective-permute-start | bytes 786440 | tf_op jit(solution)/shard_map/ppermute | solution.py:381
  84.1 1.2 %collective-permute-done.19.refs_17_ = bf16[16,64,256]{2,1,0:T(8,128)(2,1)S(1)} collective-permute-done((bf16[16,64,256]{2,1,0:T(8,128)(2,1)S(1)}, bf16[16,64,256]{2,1,0:T(8,128)(2,1)S(1)}, u32[]{:S(2)}, u32[]{:S(2)}) %collective-permute-start.19) | collective-permute-done | bytes 524320 | tf_op jit(solution)/shard_map/ppermute | solution.py:386
  85.3 0.8 collective-permute-start.13
  86.1 0.7 collective-permute-done.17.refs_14_
  86.8 2.4 %collective-permute-start.6 = (bf16[16,32,256]{2,1,0:T(8,128)(2,1)S(1)}, bf16[16,32,256]{2,1,0:T(8,128)(2,1)S(1)}, u32[]{:S(2)}, u32[]{:S(2)}) collective-permute-start(bf16[16,32,256]{2,1,0:T(8,128)(2,1)S(1)} %collective-permute-done.5.refs_2_), channel_id=1, source_target_pairs={{0,8},{8,0},{16,24},{24,16},{32,40},{40,32},{48,56},{56,48},{64,72... | collective-permute-start | bytes 786440 | tf_op jit(solution)/shard_map/ppermute | solution.py:381
  89.1 0.0 collective-permute-start.8
  89.1 0.0 collective-permute-done.10.refs_7_
  89.1 0.5 collective-permute-start.18
  89.6 1.0 collective-permute-start.16
  90.6 3.2 %collective-permute-done.13.refs_10_ = bf16[16,32,256]{2,1,0:T(8,128)(2,1)S(1)} collective-permute-done((bf16[16,32,256]{2,1,0:T(8,128)(2,1)S(1)}, bf16[16,32,256]{2,1,0:T(8,128)(2,1)S(1)}, u32[]{:S(2)}, u32[]{:S(2)}) %collective-permute-start.13) | collective-permute-done | bytes 262176 | tf_op jit(solution)/shard_map/ppermute | solution.py:381
  93.8 1.3 %collective-permute-start.14 = (bf16[16,32,256]{2,1,0:T(8,128)(2,1)S(1)}, bf16[16,32,256]{2,1,0:T(8,128)(2,1)S(1)}, u32[]{:S(2)}, u32[]{:S(2)}) collective-permute-start(bf16[16,32,256]{2,1,0:T(8,128)(2,1)S(1)} %collective-permute-done.13.refs_10_), channel_id=1, source_target_pairs={{0,8},{8,0},{16,24},{24,16},{32,40},{40,32},{48,56},{56,48},{64,72... | collective-permute-start | bytes 786440 | tf_op jit(solution)/shard_map/ppermute | solution.py:381
  95.2 0.0 collective-permute-done.8.refs_5_
  95.2 0.0 collective-permute-done.6.refs_3_
  95.2 0.0 collective-permute-done.16.refs_13_
  95.2 1.1 %collective-permute-done.14.refs_11_ = bf16[16,32,256]{2,1,0:T(8,128)(2,1)S(1)} collective-permute-done((bf16[16,32,256]{2,1,0:T(8,128)(2,1)S(1)}, bf16[16,32,256]{2,1,0:T(8,128)(2,1)S(1)}, u32[]{:S(2)}, u32[]{:S(2)}) %collective-permute-start.14) | collective-permute-done | bytes 262176 | tf_op jit(solution)/shard_map/ppermute | solution.py:381
  96.4 2.4 %weight_gradient.1 = (bf16[512,256]{1,0:T(8,128)(2,1)}, f32[256,512]{1,0:T(8,128)}) custom-call(bf16[16,32,256]{2,1,0:T(8,128)(2,1)S(1)} %shard_map.104.refs_0_, bf16[16,32,256]{2,1,0:T(8,128)(2,1)S(1)} %collective-permute-done.4.refs_1_, bf16[16,32,256]{2,1,0:T(8,128)(2,1)S(1)} %collective-permute-done.5.refs_2_, ...), custom_call_target="tpu_custom_call" | custom-call | flops 1000000000 | bytes 7000000 | tf_op jit(solution)/shard_map/weight_gradient/pallas_call | solution.py:448
  (9 shorter events, 0.1 us)
Async XLA Ops:
  2.7 38.7 %copy-start = (f32[512]{0:T(512)S(1)}, f32[512]{0:T(512)}, u32[]{:S(2)}) copy-start(f32[512]{0:T(512)} %param.13) | copy-start | bytes 6148
  2.7 23.4 %all-to-all-start.1 = ((bf16[16,96,256]{2,1,0:T(8,128)(2,1)}), bf16[16,96,256]{2,1,0:T(8,128)(2,1)S(1)}, u32[]{:S(2)}, u32[]{:S(2)}) async-start(bf16[16,96,256]{2,1,0:T(8,128)(2,1)} %get-tuple-element.7), calls=%async_computation.1 | async-start | bytes 1572864 | tf_op jit(solution)/shard_map/all_to_all | solution.py:466
  11.8 4.5 %collective-permute-start = (f32[8,256]{1,0:T(8,128)S(1)}, f32[8,256]{1,0:T(8,128)S(1)}, u32[]{:S(2)}, u32[]{:S(2)}) collective-permute-start(f32[8,256]{1,0:T(8,128)S(1)} %get-tuple-element.6), channel_id=1, source_target_pairs={{0,4},{1,5},{2,6},{3,7},{4,0},{5,1},{6,2},{7,3},{8,12},{9,13},{10,... | collective-permute-start | bytes 24584 | tf_op jit(solution)/shard_map/ppermute | solution.py:386
  16.3 4.4 %collective-permute-start.3 = (f32[8,256]{1,0:T(8,128)S(1)}, f32[8,256]{1,0:T(8,128)S(1)}, u32[]{:S(2)}, u32[]{:S(2)}) collective-permute-start(f32[8,256]{1,0:T(8,128)S(1)} %add.3.s0), channel_id=1, source_target_pairs={{0,2},{1,3},{2,0},{3,1},{4,6},{5,7},{6,4},{7,5},{8,10},{9,11},{10,... | collective-permute-start | bytes 24584 | tf_op jit(solution)/shard_map/ppermute | solution.py:386
  19.2 2.8 %collective-permute-start.2 = (f32[8,256]{1,0:T(8,128)S(1)}, f32[8,256]{1,0:T(8,128)S(1)}, u32[]{:S(2)}, u32[]{:S(2)}) collective-permute-start(f32[8,256]{1,0:T(8,128)S(1)} %add.3.s0), channel_id=1, source_target_pairs={{0,3},{1,0},{2,1},{3,2},{4,7},{5,4},{6,5},{7,6},{8,11},{9,8},{10,9... | collective-permute-start | bytes 24584 | tf_op jit(solution)/shard_map/ppermute | solution.py:386
  20.0 3.7 %collective-permute-start.1 = (f32[8,256]{1,0:T(8,128)S(1)}, f32[8,256]{1,0:T(8,128)S(1)}, u32[]{:S(2)}, u32[]{:S(2)}) collective-permute-start(f32[8,256]{1,0:T(8,128)S(1)} %add.3.s0), channel_id=1, source_target_pairs={{0,1},{1,2},{2,3},{3,0},{4,5},{5,6},{6,7},{7,4},{8,9},{9,10},{10,1... | collective-permute-start | bytes 24584 | tf_op jit(solution)/shard_map/ppermute | solution.py:386
  26.0 26.3 %all-to-all-start = ((bf16[16,64,256]{2,1,0:T(8,128)(2,1)}), bf16[16,64,256]{2,1,0:T(8,128)(2,1)S(1)}, u32[]{:S(2)}, u32[]{:S(2)}) async-start(bf16[16,64,256]{2,1,0:T(8,128)(2,1)} %normalise.1), calls=%async_computation | async-start | bytes 1048576 | tf_op jit(solution)/shard_map/all_to_all | solution.py:466
  55.7 8.0 %collective-permute-start.11 = (bf16[16,32,256]{2,1,0:T(8,128)(2,1)S(1)}, bf16[16,32,256]{2,1,0:T(8,128)(2,1)S(1)}, u32[]{:S(2)}, u32[]{:S(2)}) collective-permute-start(bf16[16,32,256]{2,1,0:T(8,128)(2,1)S(1)} %shard_map.104.refs_0_), channel_id=1, source_target_pairs={{0,32},{8,40},{16,48},{24,56},{32,0},{40,8},{48,16},{56,24},{64,96... | collective-permute-start | bytes 786440 | tf_op jit(solution)/shard_map/ppermute | solution.py:381
  57.1 13.1 %collective-permute-start.9 = (bf16[16,32,256]{2,1,0:T(8,128)(2,1)S(1)}, bf16[16,32,256]{2,1,0:T(8,128)(2,1)S(1)}, u32[]{:S(2)}, u32[]{:S(2)}) collective-permute-start(bf16[16,32,256]{2,1,0:T(8,128)(2,1)S(1)} %shard_map.104.refs_0_), channel_id=1, source_target_pairs={{0,48},{8,56},{16,0},{24,8},{32,16},{40,24},{48,32},{56,40},{64,11... | collective-permute-start | bytes 786440 | tf_op jit(solution)/shard_map/ppermute | solution.py:381
  58.0 13.1 %collective-permute-start.7 = (bf16[16,32,256]{2,1,0:T(8,128)(2,1)S(1)}, bf16[16,32,256]{2,1,0:T(8,128)(2,1)S(1)}, u32[]{:S(2)}, u32[]{:S(2)}) collective-permute-start(bf16[16,32,256]{2,1,0:T(8,128)(2,1)S(1)} %shard_map.104.refs_0_), channel_id=1, source_target_pairs={{0,16},{8,24},{16,32},{24,40},{32,48},{40,56},{48,0},{56,8},{64,80... | collective-permute-start | bytes 786440 | tf_op jit(solution)/shard_map/ppermute | solution.py:381
  58.6 22.1 %collective-permute-start.21 = (bf16[16,64,256]{2,1,0:T(8,128)(2,1)S(1)}, bf16[16,64,256]{2,1,0:T(8,128)(2,1)S(1)}, u32[]{:S(2)}, u32[]{:S(2)}) collective-permute-start(bf16[16,64,256]{2,1,0:T(8,128)(2,1)S(1)} %slice.4.refs_16_), channel_id=1, source_target_pairs={{0,2},{1,3},{2,0},{3,1},{4,6},{5,7},{6,4},{7,5},{8,10},{9,11},{10,... | collective-permute-start | bytes 1572872 | tf_op jit(solution)/shard_map/ppermute | solution.py:386
  58.9 22.7 %collective-permute-start.20 = (bf16[16,64,256]{2,1,0:T(8,128)(2,1)S(1)}, bf16[16,64,256]{2,1,0:T(8,128)(2,1)S(1)}, u32[]{:S(2)}, u32[]{:S(2)}) collective-permute-start(bf16[16,64,256]{2,1,0:T(8,128)(2,1)S(1)} %slice.4.refs_16_), channel_id=1, source_target_pairs={{0,3},{1,0},{2,1},{3,2},{4,7},{5,4},{6,5},{7,6},{8,11},{9,8},{10,9... | collective-permute-start | bytes 1572872 | tf_op jit(solution)/shard_map/ppermute | solution.py:386
  63.7 21.6 %collective-permute-start.19 = (bf16[16,64,256]{2,1,0:T(8,128)(2,1)S(1)}, bf16[16,64,256]{2,1,0:T(8,128)(2,1)S(1)}, u32[]{:S(2)}, u32[]{:S(2)}) collective-permute-start(bf16[16,64,256]{2,1,0:T(8,128)(2,1)S(1)} %slice.4.refs_16_), channel_id=1, source_target_pairs={{0,1},{1,2},{2,3},{3,0},{4,5},{5,6},{6,7},{7,4},{8,9},{9,10},{10,1... | collective-permute-start | bytes 1572872 | tf_op jit(solution)/shard_map/ppermute | solution.py:386
  70.2 8.7 %collective-permute-start.5 = (bf16[16,32,256]{2,1,0:T(8,128)(2,1)S(1)}, bf16[16,32,256]{2,1,0:T(8,128)(2,1)S(1)}, u32[]{:S(2)}, u32[]{:S(2)}) collective-permute-start(bf16[16,32,256]{2,1,0:T(8,128)(2,1)S(1)} %shard_map.104.refs_0_), channel_id=1, source_target_pairs={{0,64},{8,72},{16,80},{24,88},{32,96},{40,104},{48,112},{56,120},{... | collective-permute-start | bytes 786440 | tf_op jit(solution)/shard_map/ppermute | solution.py:381
  71.1 7.8 %collective-permute-start.4 = (bf16[16,32,256]{2,1,0:T(8,128)(2,1)S(1)}, bf16[16,32,256]{2,1,0:T(8,128)(2,1)S(1)}, u32[]{:S(2)}, u32[]{:S(2)}) collective-permute-start(bf16[16,32,256]{2,1,0:T(8,128)(2,1)S(1)} %shard_map.104.refs_0_), channel_id=1, source_target_pairs={{0,8},{8,0},{16,24},{24,16},{32,40},{40,32},{48,56},{56,48},{64,72... | collective-permute-start | bytes 786440 | tf_op jit(solution)/shard_map/ppermute | solution.py:381
  78.9 7.9 %collective-permute-start.17 = (bf16[16,32,256]{2,1,0:T(8,128)(2,1)S(1)}, bf16[16,32,256]{2,1,0:T(8,128)(2,1)S(1)}, u32[]{:S(2)}, u32[]{:S(2)}) collective-permute-start(bf16[16,32,256]{2,1,0:T(8,128)(2,1)S(1)} %collective-permute-done.11.refs_8_), channel_id=1, source_target_pairs={{0,64},{8,72},{16,80},{24,88},{32,96},{40,104},{48,112},{56,120},{... | collective-permute-start | bytes 786440 | tf_op jit(solution)/shard_map/ppermute | solution.py:381
  78.9 10.2 %collective-permute-start.12 = (bf16[16,32,256]{2,1,0:T(8,128)(2,1)S(1)}, bf16[16,32,256]{2,1,0:T(8,128)(2,1)S(1)}, u32[]{:S(2)}, u32[]{:S(2)}) collective-permute-start(bf16[16,32,256]{2,1,0:T(8,128)(2,1)S(1)} %collective-permute-done.11.refs_8_), channel_id=1, source_target_pairs={{0,8},{8,0},{16,24},{24,16},{32,40},{40,32},{48,56},{56,48},{64,72... | collective-permute-start | bytes 786440 | tf_op jit(solution)/shard_map/ppermute | solution.py:381
  80.7 8.4 %collective-permute-start.10 = (bf16[16,32,256]{2,1,0:T(8,128)(2,1)S(1)}, bf16[16,32,256]{2,1,0:T(8,128)(2,1)S(1)}, u32[]{:S(2)}, u32[]{:S(2)}) collective-permute-start(bf16[16,32,256]{2,1,0:T(8,128)(2,1)S(1)} %collective-permute-done.9.refs_6_), channel_id=1, source_target_pairs={{0,8},{8,0},{16,24},{24,16},{32,40},{40,32},{48,56},{56,48},{64,72... | collective-permute-start | bytes 786440 | tf_op jit(solution)/shard_map/ppermute | solution.py:381
  81.6 8.1 %collective-permute-start.15 = (bf16[16,32,256]{2,1,0:T(8,128)(2,1)S(1)}, bf16[16,32,256]{2,1,0:T(8,128)(2,1)S(1)}, u32[]{:S(2)}, u32[]{:S(2)}) collective-permute-start(bf16[16,32,256]{2,1,0:T(8,128)(2,1)S(1)} %collective-permute-done.5.refs_2_), channel_id=1, source_target_pairs={{0,48},{8,56},{16,0},{24,8},{32,16},{40,24},{48,32},{56,40},{64,11... | collective-permute-start | bytes 786440 | tf_op jit(solution)/shard_map/ppermute | solution.py:381
  85.3 8.6 %collective-permute-start.13 = (bf16[16,32,256]{2,1,0:T(8,128)(2,1)S(1)}, bf16[16,32,256]{2,1,0:T(8,128)(2,1)S(1)}, u32[]{:S(2)}, u32[]{:S(2)}) collective-permute-start(bf16[16,32,256]{2,1,0:T(8,128)(2,1)S(1)} %collective-permute-done.5.refs_2_), channel_id=1, source_target_pairs={{0,16},{8,24},{16,32},{24,40},{32,48},{40,56},{48,0},{56,8},{64,80... | collective-permute-start | bytes 786440 | tf_op jit(solution)/shard_map/ppermute | solution.py:381
  86.8 8.4 %collective-permute-start.6 = (bf16[16,32,256]{2,1,0:T(8,128)(2,1)S(1)}, bf16[16,32,256]{2,1,0:T(8,128)(2,1)S(1)}, u32[]{:S(2)}, u32[]{:S(2)}) collective-permute-start(bf16[16,32,256]{2,1,0:T(8,128)(2,1)S(1)} %collective-permute-done.5.refs_2_), channel_id=1, source_target_pairs={{0,8},{8,0},{16,24},{24,16},{32,40},{40,32},{48,56},{56,48},{64,72... | collective-permute-start | bytes 786440 | tf_op jit(solution)/shard_map/ppermute | solution.py:381
  89.1 6.1 %collective-permute-start.8 = (bf16[16,32,256]{2,1,0:T(8,128)(2,1)S(1)}, bf16[16,32,256]{2,1,0:T(8,128)(2,1)S(1)}, u32[]{:S(2)}, u32[]{:S(2)}) collective-permute-start(bf16[16,32,256]{2,1,0:T(8,128)(2,1)S(1)} %collective-permute-done.7.refs_4_), channel_id=1, source_target_pairs={{0,8},{8,0},{16,24},{24,16},{32,40},{40,32},{48,56},{56,48},{64,72... | collective-permute-start | bytes 786440 | tf_op jit(solution)/shard_map/ppermute | solution.py:381
  89.1 6.1 %collective-permute-start.18 = (bf16[16,32,256]{2,1,0:T(8,128)(2,1)S(1)}, bf16[16,32,256]{2,1,0:T(8,128)(2,1)S(1)}, u32[]{:S(2)}, u32[]{:S(2)}) collective-permute-start(bf16[16,32,256]{2,1,0:T(8,128)(2,1)S(1)} %collective-permute-done.17.refs_14_), channel_id=1, source_target_pairs={{0,8},{8,0},{16,24},{24,16},{32,40},{40,32},{48,56},{56,48},{64,72... | collective-permute-start | bytes 786440 | tf_op jit(solution)/shard_map/ppermute | solution.py:381
  89.6 5.6 %collective-permute-start.16 = (bf16[16,32,256]{2,1,0:T(8,128)(2,1)S(1)}, bf16[16,32,256]{2,1,0:T(8,128)(2,1)S(1)}, u32[]{:S(2)}, u32[]{:S(2)}) collective-permute-start(bf16[16,32,256]{2,1,0:T(8,128)(2,1)S(1)} %collective-permute-done.15.refs_12_), channel_id=1, source_target_pairs={{0,8},{8,0},{16,24},{24,16},{32,40},{40,32},{48,56},{56,48},{64,72... | collective-permute-start | bytes 786440 | tf_op jit(solution)/shard_map/ppermute | solution.py:381
  93.8 2.5 %collective-permute-start.14 = (bf16[16,32,256]{2,1,0:T(8,128)(2,1)S(1)}, bf16[16,32,256]{2,1,0:T(8,128)(2,1)S(1)}, u32[]{:S(2)}, u32[]{:S(2)}) collective-permute-start(bf16[16,32,256]{2,1,0:T(8,128)(2,1)S(1)} %collective-permute-done.13.refs_10_), channel_id=1, source_target_pairs={{0,8},{8,0},{16,24},{24,16},{32,40},{40,32},{48,56},{56,48},{64,72... | collective-permute-start | bytes 786440 | tf_op jit(solution)/shard_map/ppermute | solution.py:381

commit v6 on v5

--- a/solution.py
+++ b/solution.py
@@ -414,7 +414,7 @@
 def grad_kernel(mixed_keys, up_keys, *refs):
     seq, chan = lax.axis_index("seq"), lax.axis_index("chan")
     mixed_refs, up_refs = refs[: len(mixed_keys)], refs[len(mixed_keys) : len(mixed_keys) + len(up_keys)]
-    mixed_hbm, grad_hbm, rows_ref, grad_ref, mixed_sems, grad_sems = refs[len(mixed_keys) + len(up_keys) :]
+    mixed_hbm, grad_ref, rows_ref, mixed_sems = refs[len(mixed_keys) + len(up_keys) :]
 
     def source_place(dk, dz, dx):
         z = lax.bitwise_xor(seq // 8, dz)
@@ -435,10 +435,7 @@
         for z in range(2):
             n = 2 * i + z
             place = pl.ds(pl.multiple_of((4 * z + lax.bitwise_and(chan + dy, 3)) * 32, 32), 32)
-            grad_ref[32 * n : 32 * n + 32, :] = turned_rows[32 * n : 32 * n + 32]
-            source = grad_ref.at[32 * n : 32 * n + 32, :]
-            copies.append(pltpu.make_async_copy(source, grad_hbm.at[place, :], grad_sems.at[n]))
-            copies[-1].start()
+            grad_ref[place, :] = turned_rows[32 * n : 32 * n + 32]
     for copy in copies:
         copy.wait()
 
@@ -449,12 +446,10 @@
         functools.partial(grad_kernel, mixed_keys, up_keys),
         out_shape=(jax.ShapeDtypeStruct((512, 256), BF16), jax.ShapeDtypeStruct((256, 512), F32)),
         in_specs=vmem(len(mixed) + len(up)),
-        out_specs=tuple(hbm(2)),
+        out_specs=(*hbm(1), *vmem(1)),
         scratch_shapes=[
             pltpu.VMEM((512, 256), F32),
-            pltpu.VMEM((256, 512), F32),
             pltpu.SemaphoreType.DMA((len(mixed),)),
-            pltpu.SemaphoreType.DMA((2 * len(up),)),
         ],
         cost_estimate=pl.CostEstimate(flops=1_000_000_000, bytes_accessed=7_000_000, transcendentals=0),
         compiler_params=limit(16),

time: 99.2 us -> 99.8 us (level)
  no operation moved by 1% of the time
where the time goes in v6:
time: 99.8 us; the launch traced here: 99.4 us
  starting transfers between devices  45.2 us (45%)
  waiting for transfers between devices  38.1 us (38%)
  Pallas kernels  15.3 us (15%)
    all_to_all x2, starting transfers between devices, exchange(): return lax.all_to_all(value, axis, split_axis=0, concat_axis=0, tiled=True)  24.4 us
    ppermute x15, waiting for transfers between devices, over_seq(): return lax.ppermute(value, 'seq', pairs)  23 us
    ppermute x15, starting transfers between devices, over_seq(): return lax.ppermute(value, 'seq', pairs)  13.7 us
    ppermute x7, waiting for transfers between devices, over_chan(): return lax.ppermute(value, 'chan', pairs)  8.76 us
    ppermute x7, starting transfers between devices, over_chan(): return lax.ppermute(value, 'chan', pairs)  7.06 us
    all_to_all x2, waiting for transfers between devices, exchange(): return lax.all_to_all(value, axis, split_axis=0, concat_axis=0, tiled=True)  6.34 us
    pallas_call x1, Pallas kernels, filter_spectrum(): pl.pallas_call(filter_kernel, out_shape=pltpu.HBM((OUTER, 32, 2 * INNER),...  5.19 us
    pallas_call x1, Pallas kernels, gated_convolution(): pl.pallas_call(signal_kernel, out_shape=jax.ShapeDtypeStruct((16, 32, 256...  3.34 us
  transfers between devices with their start and end apart: 24, of which 14 were waited for; matrix products, arithmetic and copies ran while one was open for 0% of the time, Pallas kernels for 7%

profile of v6, /device:TPU:1, one launch (start us, length us, event | category | flops | bytes accessed | tf_op | source)
XLA Modules:
  0.0 99.4 jit_solution(4024007561424600042)
XLA Ops:
  0.6 2.0 %pack.1 = (bf16[16,96,256]{2,1,0:T(8,128)(2,1)}, f32[8,256]{1,0:T(8,128)S(1)}, f32[16,32,256]{2,1,0:T(8,128)S(1)}) custom-call(bf16[16,32,256]{2,1,0:T(8,128)(2,1)} %bitcast.8, bf16[16,32,256]{2,1,0:T(8,128)(2,1)} %bitcast.9, bf16[16,256,256]{2,1,0:T(8,128)(2,1)} %bitcast.7, f32[4,128]{1,0:T(4,128)} %bitcast.11), custom_call_target="tpu_custom_call" | custom-call | tf_op jit(solution)/shard_map/pack/pallas_call | solution.py:339
  2.7 0.0 copy-start
  2.7 9.1 %all-to-all-start.1 = ((bf16[16,96,256]{2,1,0:T(8,128)(2,1)}), bf16[16,96,256]{2,1,0:T(8,128)(2,1)S(1)}, u32[]{:S(2)}, u32[]{:S(2)}) async-start(bf16[16,96,256]{2,1,0:T(8,128)(2,1)} %get-tuple-element.7), calls=%async_computation.1 | async-start | bytes 1572864 | tf_op jit(solution)/shard_map/all_to_all | solution.py:461
  11.8 0.7 collective-permute-start
  12.5 3.8 %collective-permute-done = f32[8,256]{1,0:T(8,128)S(1)} collective-permute-done((f32[8,256]{1,0:T(8,128)S(1)}, f32[8,256]{1,0:T(8,128)S(1)}, u32[]{:S(2)}, u32[]{:S(2)}) %collective-permute-start) | collective-permute-done | bytes 8224 | tf_op jit(solution)/shard_map/ppermute | solution.py:386
  16.3 2.9 %collective-permute-start.3 = (f32[8,256]{1,0:T(8,128)S(1)}, f32[8,256]{1,0:T(8,128)S(1)}, u32[]{:S(2)}, u32[]{:S(2)}) collective-permute-start(f32[8,256]{1,0:T(8,128)S(1)} %add.3.s0), channel_id=1, source_target_pairs={{0,2},{1,3},{2,0},{3,1},{4,6},{5,7},{6,4},{7,5},{8,10},{9,11},{10,... | collective-permute-start | bytes 24584 | tf_op jit(solution)/shard_map/ppermute | solution.py:386
  19.2 0.8 collective-permute-start.2
  20.0 0.7 collective-permute-start.1
  20.7 0.0 collective-permute-done.3.s3
  20.7 1.3 %collective-permute-done.2.s2 = f32[8,256]{1,0:T(8,128)S(1)} collective-permute-done((f32[8,256]{1,0:T(8,128)S(1)}, f32[8,256]{1,0:T(8,128)S(1)}, u32[]{:S(2)}, u32[]{:S(2)}) %collective-permute-start.2) | collective-permute-done | bytes 8224 | tf_op jit(solution)/shard_map/ppermute | solution.py:386
  22.0 1.7 %collective-permute-done.1.s1 = f32[8,256]{1,0:T(8,128)S(1)} collective-permute-done((f32[8,256]{1,0:T(8,128)S(1)}, f32[8,256]{1,0:T(8,128)S(1)}, u32[]{:S(2)}, u32[]{:S(2)}) %collective-permute-start.1) | collective-permute-done | bytes 8224 | tf_op jit(solution)/shard_map/ppermute | solution.py:386
  23.7 1.8 %normalise.1 = bf16[16,64,256]{2,1,0:T(8,128)(2,1)} custom-call(f32[16,32,256]{2,1,0:T(8,128)S(1)} %get-tuple-element.5.lifted_ref, f32[8,256]{1,0:T(8,128)S(1)} %add.3.s0, f32[8,256]{1,0:T(8,128)S(1)} %collective-permute-done.1.s1, f32[8,256]{1,0:T(8,128)S(1)} %collective-permute-done.2.s2, f32[8,256]{1,0:T(8,128)S(1)} %collective-permute-done.3.s3, ...), custom_call_target="tpu_custom_call" | custom-call | tf_op jit(solution)/shard_map/normalise/pallas_call | solution.py:361
  25.5 0.6 all-to-all-done.1.got_ref
  26.0 15.3 %all-to-all-start = ((bf16[16,64,256]{2,1,0:T(8,128)(2,1)}), bf16[16,64,256]{2,1,0:T(8,128)(2,1)S(1)}, u32[]{:S(2)}, u32[]{:S(2)}) async-start(bf16[16,64,256]{2,1,0:T(8,128)(2,1)} %normalise.1), calls=%async_computation | async-start | bytes 1048576 | tf_op jit(solution)/shard_map/all_to_all | solution.py:461
  41.3 5.2 %filter_spectrum.1.spec_hbm = f32[32,32,256]{2,1,0:T(8,128)} custom-call(bf16[16,96,256]{2,1,0:T(8,128)(2,1)S(1)} %all-to-all-done.1.got_ref, f32[512,128]{1,0:T(8,128)} %taps_hbm.1, f32[1,512]{1,0:T(1,128)S(1)} %bitcast.6, f32[2,32,128]{2,1,0:T(8,128)} %constant.4.clone.turn_hbm, bf16[2,512,256]{2,1,0:T(8,128)(2,1)} %constant.5.clone.inner_hbm), custom_call_target="tpu_custom_call" | custom-call | flops 2000000000 | bytes 3000000 | tf_op jit(solution)/shard_map/filter_spectrum/pallas_call | solution.py:270
  46.5 5.8 %all-to-all-done.got_ref = bf16[16,64,256]{2,1,0:T(8,128)(2,1)S(1)} async-done(((bf16[16,64,256]{2,1,0:T(8,128)(2,1)}), bf16[16,64,256]{2,1,0:T(8,128)(2,1)S(1)}, u32[]{:S(2)}, u32[]{:S(2)}) %all-to-all-start) | async-done | bytes 524320 | tf_op jit(solution)/shard_map/all_to_all | solution.py:461
  52.3 3.3 %shard_map.104.refs_0_ = bf16[16,32,256]{2,1,0:T(8,128)(2,1)S(1)} custom-call(bf16[16,64,256]{2,1,0:T(8,128)(2,1)S(1)} %all-to-all-done.got_ref, f32[32,32,256]{2,1,0:T(8,128)} %filter_spectrum.1.spec_hbm, f32[2,32,128]{2,1,0:T(8,128)} %constant.4.clone.turn_hbm, bf16[2,512,256]{2,1,0:T(8,128)(2,1)} %constant.5.clone.inner_hbm), custom_call_target="tpu_custom_call" | custom-call | flops 1000000000 | bytes 3000000 | tf_op jit(solution)/shard_map/pallas_call | solution.py:283
  55.7 1.4 %collective-permute-start.11 = (bf16[16,32,256]{2,1,0:T(8,128)(2,1)S(1)}, bf16[16,32,256]{2,1,0:T(8,128)(2,1)S(1)}, u32[]{:S(2)}, u32[]{:S(2)}) collective-permute-start(bf16[16,32,256]{2,1,0:T(8,128)(2,1)S(1)} %shard_map.104.refs_0_), channel_id=1, source_target_pairs={{0,32},{8,40},{16,48},{24,56},{32,0},{40,8},{48,16},{56,24},{64,96... | collective-permute-start | bytes 786440 | tf_op jit(solution)/shard_map/ppermute | solution.py:381
  57.1 0.9 collective-permute-start.9
  58.0 0.5 collective-permute-start.7
  58.6 0.3 collective-permute-start.21
  58.9 1.7 %collective-permute-start.20 = (bf16[16,64,256]{2,1,0:T(8,128)(2,1)S(1)}, bf16[16,64,256]{2,1,0:T(8,128)(2,1)S(1)}, u32[]{:S(2)}, u32[]{:S(2)}) collective-permute-start(bf16[16,64,256]{2,1,0:T(8,128)(2,1)S(1)} %slice.4.refs_16_), channel_id=1, source_target_pairs={{0,3},{1,0},{2,1},{3,2},{4,7},{5,4},{6,5},{7,6},{8,11},{9,8},{10,9... | collective-permute-start | bytes 1572872 | tf_op jit(solution)/shard_map/ppermute | solution.py:386
  60.5 3.2 %collective-permute-done.11.refs_8_ = bf16[16,32,256]{2,1,0:T(8,128)(2,1)S(1)} collective-permute-done((bf16[16,32,256]{2,1,0:T(8,128)(2,1)S(1)}, bf16[16,32,256]{2,1,0:T(8,128)(2,1)S(1)}, u32[]{:S(2)}, u32[]{:S(2)}) %collective-permute-start.11) | collective-permute-done | bytes 262176 | tf_op jit(solution)/shard_map/ppermute | solution.py:381
  63.7 0.0 collective-permute-start.19
  63.7 6.5 %collective-permute-done.9.refs_6_ = bf16[16,32,256]{2,1,0:T(8,128)(2,1)S(1)} collective-permute-done((bf16[16,32,256]{2,1,0:T(8,128)(2,1)S(1)}, bf16[16,32,256]{2,1,0:T(8,128)(2,1)S(1)}, u32[]{:S(2)}, u32[]{:S(2)}) %collective-permute-start.9) | collective-permute-done | bytes 262176 | tf_op jit(solution)/shard_map/ppermute | solution.py:381
  70.2 0.0 collective-permute-start.5
  70.2 1.0 collective-permute-done.7.refs_4_
  71.1 0.4 collective-permute-start.4
  71.6 7.3 %collective-permute-done.5.refs_2_ = bf16[16,32,256]{2,1,0:T(8,128)(2,1)S(1)} collective-permute-done((bf16[16,32,256]{2,1,0:T(8,128)(2,1)S(1)}, bf16[16,32,256]{2,1,0:T(8,128)(2,1)S(1)}, u32[]{:S(2)}, u32[]{:S(2)}) %collective-permute-start.5) | collective-permute-done | bytes 262176 | tf_op jit(solution)/shard_map/ppermute | solution.py:381
  78.9 1.8 %collective-permute-start.12 = (bf16[16,32,256]{2,1,0:T(8,128)(2,1)S(1)}, bf16[16,32,256]{2,1,0:T(8,128)(2,1)S(1)}, u32[]{:S(2)}, u32[]{:S(2)}) collective-permute-start(bf16[16,32,256]{2,1,0:T(8,128)(2,1)S(1)} %collective-permute-done.11.refs_8_), channel_id=1, source_target_pairs={{0,8},{8,0},{16,24},{24,16},{32,40},{40,32},{48,56},{56,48},{64,72... | collective-permute-start | bytes 786440 | tf_op jit(solution)/shard_map/ppermute | solution.py:381
  80.7 0.1 collective-permute-start.10
  80.8 0.8 collective-permute-done.20.refs_18_
  81.6 2.5 %collective-permute-start.15 = (bf16[16,32,256]{2,1,0:T(8,128)(2,1)S(1)}, bf16[16,32,256]{2,1,0:T(8,128)(2,1)S(1)}, u32[]{:S(2)}, u32[]{:S(2)}) collective-permute-start(bf16[16,32,256]{2,1,0:T(8,128)(2,1)S(1)} %collective-permute-done.5.refs_2_), channel_id=1, source_target_pairs={{0,48},{8,56},{16,0},{24,8},{32,16},{40,24},{48,32},{56,40},{64,11... | collective-permute-start | bytes 786440 | tf_op jit(solution)/shard_map/ppermute | solution.py:381
  84.1 1.2 %collective-permute-done.19.refs_17_ = bf16[16,64,256]{2,1,0:T(8,128)(2,1)S(1)} collective-permute-done((bf16[16,64,256]{2,1,0:T(8,128)(2,1)S(1)}, bf16[16,64,256]{2,1,0:T(8,128)(2,1)S(1)}, u32[]{:S(2)}, u32[]{:S(2)}) %collective-permute-start.19) | collective-permute-done | bytes 524320 | tf_op jit(solution)/shard_map/ppermute | solution.py:386
  85.3 0.8 collective-permute-start.13
  86.1 0.7 collective-permute-done.17.refs_14_
  86.8 2.4 %collective-permute-start.6 = (bf16[16,32,256]{2,1,0:T(8,128)(2,1)S(1)}, bf16[16,32,256]{2,1,0:T(8,128)(2,1)S(1)}, u32[]{:S(2)}, u32[]{:S(2)}) collective-permute-start(bf16[16,32,256]{2,1,0:T(8,128)(2,1)S(1)} %collective-permute-done.5.refs_2_), channel_id=1, source_target_pairs={{0,8},{8,0},{16,24},{24,16},{32,40},{40,32},{48,56},{56,48},{64,72... | collective-permute-start | bytes 786440 | tf_op jit(solution)/shard_map/ppermute | solution.py:381
  89.1 0.0 collective-permute-start.8
  89.1 0.0 collective-permute-done.10.refs_7_
  89.1 0.5 collective-permute-start.18
  89.6 1.0 collective-permute-start.16
  90.6 3.2 %collective-permute-done.13.refs_10_ = bf16[16,32,256]{2,1,0:T(8,128)(2,1)S(1)} collective-permute-done((bf16[16,32,256]{2,1,0:T(8,128)(2,1)S(1)}, bf16[16,32,256]{2,1,0:T(8,128)(2,1)S(1)}, u32[]{:S(2)}, u32[]{:S(2)}) %collective-permute-start.13) | collective-permute-done | bytes 262176 | tf_op jit(solution)/shard_map/ppermute | solution.py:381
  93.8 1.3 %collective-permute-start.14 = (bf16[16,32,256]{2,1,0:T(8,128)(2,1)S(1)}, bf16[16,32,256]{2,1,0:T(8,128)(2,1)S(1)}, u32[]{:S(2)}, u32[]{:S(2)}) collective-permute-start(bf16[16,32,256]{2,1,0:T(8,128)(2,1)S(1)} %collective-permute-done.13.refs_10_), channel_id=1, source_target_pairs={{0,8},{8,0},{16,24},{24,16},{32,40},{40,32},{48,56},{56,48},{64,72... | collective-permute-start | bytes 786440 | tf_op jit(solution)/shard_map/ppermute | solution.py:381
  95.2 0.0 collective-permute-done.8.refs_5_
  95.2 0.0 collective-permute-done.6.refs_3_
  95.2 0.0 collective-permute-done.16.refs_13_
  95.2 1.1 %collective-permute-done.14.refs_11_ = bf16[16,32,256]{2,1,0:T(8,128)(2,1)S(1)} collective-permute-done((bf16[16,32,256]{2,1,0:T(8,128)(2,1)S(1)}, bf16[16,32,256]{2,1,0:T(8,128)(2,1)S(1)}, u32[]{:S(2)}, u32[]{:S(2)}) %collective-permute-start.14) | collective-permute-done | bytes 262176 | tf_op jit(solution)/shard_map/ppermute | solution.py:381
  96.4 3.0 %weight_gradient.1 = (bf16[512,256]{1,0:T(8,128)(2,1)}, f32[256,512]{1,0:T(8,128)}) custom-call(bf16[16,32,256]{2,1,0:T(8,128)(2,1)S(1)} %shard_map.104.refs_0_, bf16[16,32,256]{2,1,0:T(8,128)(2,1)S(1)} %collective-permute-done.4.refs_1_, bf16[16,32,256]{2,1,0:T(8,128)(2,1)S(1)} %collective-permute-done.5.refs_2_, ...), custom_call_target="tpu_custom_call" | custom-call | flops 1000000000 | bytes 7000000 | tf_op jit(solution)/shard_map/weight_gradient/pallas_call | solution.py:445
  (9 shorter events, 0.1 us)
Async XLA Ops:
  2.7 38.7 %copy-start = (f32[512]{0:T(512)S(1)}, f32[512]{0:T(512)}, u32[]{:S(2)}) copy-start(f32[512]{0:T(512)} %param.13) | copy-start | bytes 6148
  2.7 23.4 %all-to-all-start.1 = ((bf16[16,96,256]{2,1,0:T(8,128)(2,1)}), bf16[16,96,256]{2,1,0:T(8,128)(2,1)S(1)}, u32[]{:S(2)}, u32[]{:S(2)}) async-start(bf16[16,96,256]{2,1,0:T(8,128)(2,1)} %get-tuple-element.7), calls=%async_computation.1 | async-start | bytes 1572864 | tf_op jit(solution)/shard_map/all_to_all | solution.py:461
  11.8 4.5 %collective-permute-start = (f32[8,256]{1,0:T(8,128)S(1)}, f32[8,256]{1,0:T(8,128)S(1)}, u32[]{:S(2)}, u32[]{:S(2)}) collective-permute-start(f32[8,256]{1,0:T(8,128)S(1)} %get-tuple-element.6), channel_id=1, source_target_pairs={{0,4},{1,5},{2,6},{3,7},{4,0},{5,1},{6,2},{7,3},{8,12},{9,13},{10,... | collective-permute-start | bytes 24584 | tf_op jit(solution)/shard_map/ppermute | solution.py:386
  16.3 4.4 %collective-permute-start.3 = (f32[8,256]{1,0:T(8,128)S(1)}, f32[8,256]{1,0:T(8,128)S(1)}, u32[]{:S(2)}, u32[]{:S(2)}) collective-permute-start(f32[8,256]{1,0:T(8,128)S(1)} %add.3.s0), channel_id=1, source_target_pairs={{0,2},{1,3},{2,0},{3,1},{4,6},{5,7},{6,4},{7,5},{8,10},{9,11},{10,... | collective-permute-start | bytes 24584 | tf_op jit(solution)/shard_map/ppermute | solution.py:386
  19.2 2.8 %collective-permute-start.2 = (f32[8,256]{1,0:T(8,128)S(1)}, f32[8,256]{1,0:T(8,128)S(1)}, u32[]{:S(2)}, u32[]{:S(2)}) collective-permute-start(f32[8,256]{1,0:T(8,128)S(1)} %add.3.s0), channel_id=1, source_target_pairs={{0,3},{1,0},{2,1},{3,2},{4,7},{5,4},{6,5},{7,6},{8,11},{9,8},{10,9... | collective-permute-start | bytes 24584 | tf_op jit(solution)/shard_map/ppermute | solution.py:386
  20.0 3.7 %collective-permute-start.1 = (f32[8,256]{1,0:T(8,128)S(1)}, f32[8,256]{1,0:T(8,128)S(1)}, u32[]{:S(2)}, u32[]{:S(2)}) collective-permute-start(f32[8,256]{1,0:T(8,128)S(1)} %add.3.s0), channel_id=1, source_target_pairs={{0,1},{1,2},{2,3},{3,0},{4,5},{5,6},{6,7},{7,4},{8,9},{9,10},{10,1... | collective-permute-start | bytes 24584 | tf_op jit(solution)/shard_map/ppermute | solution.py:386
  26.0 26.3 %all-to-all-start = ((bf16[16,64,256]{2,1,0:T(8,128)(2,1)}), bf16[16,64,256]{2,1,0:T(8,128)(2,1)S(1)}, u32[]{:S(2)}, u32[]{:S(2)}) async-start(bf16[16,64,256]{2,1,0:T(8,128)(2,1)} %normalise.1), calls=%async_computation | async-start | bytes 1048576 | tf_op jit(solution)/shard_map/all_to_all | solution.py:461
  55.7 8.0 %collective-permute-start.11 = (bf16[16,32,256]{2,1,0:T(8,128)(2,1)S(1)}, bf16[16,32,256]{2,1,0:T(8,128)(2,1)S(1)}, u32[]{:S(2)}, u32[]{:S(2)}) collective-permute-start(bf16[16,32,256]{2,1,0:T(8,128)(2,1)S(1)} %shard_map.104.refs_0_), channel_id=1, source_target_pairs={{0,32},{8,40},{16,48},{24,56},{32,0},{40,8},{48,16},{56,24},{64,96... | collective-permute-start | bytes 786440 | tf_op jit(solution)/shard_map/ppermute | solution.py:381
  57.1 13.1 %collective-permute-start.9 = (bf16[16,32,256]{2,1,0:T(8,128)(2,1)S(1)}, bf16[16,32,256]{2,1,0:T(8,128)(2,1)S(1)}, u32[]{:S(2)}, u32[]{:S(2)}) collective-permute-start(bf16[16,32,256]{2,1,0:T(8,128)(2,1)S(1)} %shard_map.104.refs_0_), channel_id=1, source_target_pairs={{0,48},{8,56},{16,0},{24,8},{32,16},{40,24},{48,32},{56,40},{64,11... | collective-permute-start | bytes 786440 | tf_op jit(solution)/shard_map/ppermute | solution.py:381
  58.0 13.1 %collective-permute-start.7 = (bf16[16,32,256]{2,1,0:T(8,128)(2,1)S(1)}, bf16[16,32,256]{2,1,0:T(8,128)(2,1)S(1)}, u32[]{:S(2)}, u32[]{:S(2)}) collective-permute-start(bf16[16,32,256]{2,1,0:T(8,128)(2,1)S(1)} %shard_map.104.refs_0_), channel_id=1, source_target_pairs={{0,16},{8,24},{16,32},{24,40},{32,48},{40,56},{48,0},{56,8},{64,80... | collective-permute-start | bytes 786440 | tf_op jit(solution)/shard_map/ppermute | solution.py:381
  58.6 22.1 %collective-permute-start.21 = (bf16[16,64,256]{2,1,0:T(8,128)(2,1)S(1)}, bf16[16,64,256]{2,1,0:T(8,128)(2,1)S(1)}, u32[]{:S(2)}, u32[]{:S(2)}) collective-permute-start(bf16[16,64,256]{2,1,0:T(8,128)(2,1)S(1)} %slice.4.refs_16_), channel_id=1, source_target_pairs={{0,2},{1,3},{2,0},{3,1},{4,6},{5,7},{6,4},{7,5},{8,10},{9,11},{10,... | collective-permute-start | bytes 1572872 | tf_op jit(solution)/shard_map/ppermute | solution.py:386
  58.9 22.7 %collective-permute-start.20 = (bf16[16,64,256]{2,1,0:T(8,128)(2,1)S(1)}, bf16[16,64,256]{2,1,0:T(8,128)(2,1)S(1)}, u32[]{:S(2)}, u32[]{:S(2)}) collective-permute-start(bf16[16,64,256]{2,1,0:T(8,128)(2,1)S(1)} %slice.4.refs_16_), channel_id=1, source_target_pairs={{0,3},{1,0},{2,1},{3,2},{4,7},{5,4},{6,5},{7,6},{8,11},{9,8},{10,9... | collective-permute-start | bytes 1572872 | tf_op jit(solution)/shard_map/ppermute | solution.py:386
  63.7 21.6 %collective-permute-start.19 = (bf16[16,64,256]{2,1,0:T(8,128)(2,1)S(1)}, bf16[16,64,256]{2,1,0:T(8,128)(2,1)S(1)}, u32[]{:S(2)}, u32[]{:S(2)}) collective-permute-start(bf16[16,64,256]{2,1,0:T(8,128)(2,1)S(1)} %slice.4.refs_16_), channel_id=1, source_target_pairs={{0,1},{1,2},{2,3},{3,0},{4,5},{5,6},{6,7},{7,4},{8,9},{9,10},{10,1... | collective-permute-start | bytes 1572872 | tf_op jit(solution)/shard_map/ppermute | solution.py:386
  70.2 8.7 %collective-permute-start.5 = (bf16[16,32,256]{2,1,0:T(8,128)(2,1)S(1)}, bf16[16,32,256]{2,1,0:T(8,128)(2,1)S(1)}, u32[]{:S(2)}, u32[]{:S(2)}) collective-permute-start(bf16[16,32,256]{2,1,0:T(8,128)(2,1)S(1)} %shard_map.104.refs_0_), channel_id=1, source_target_pairs={{0,64},{8,72},{16,80},{24,88},{32,96},{40,104},{48,112},{56,120},{... | collective-permute-start | bytes 786440 | tf_op jit(solution)/shard_map/ppermute | solution.py:381
  71.1 7.8 %collective-permute-start.4 = (bf16[16,32,256]{2,1,0:T(8,128)(2,1)S(1)}, bf16[16,32,256]{2,1,0:T(8,128)(2,1)S(1)}, u32[]{:S(2)}, u32[]{:S(2)}) collective-permute-start(bf16[16,32,256]{2,1,0:T(8,128)(2,1)S(1)} %shard_map.104.refs_0_), channel_id=1, source_target_pairs={{0,8},{8,0},{16,24},{24,16},{32,40},{40,32},{48,56},{56,48},{64,72... | collective-permute-start | bytes 786440 | tf_op jit(solution)/shard_map/ppermute | solution.py:381
  78.9 7.9 %collective-permute-start.17 = (bf16[16,32,256]{2,1,0:T(8,128)(2,1)S(1)}, bf16[16,32,256]{2,1,0:T(8,128)(2,1)S(1)}, u32[]{:S(2)}, u32[]{:S(2)}) collective-permute-start(bf16[16,32,256]{2,1,0:T(8,128)(2,1)S(1)} %collective-permute-done.11.refs_8_), channel_id=1, source_target_pairs={{0,64},{8,72},{16,80},{24,88},{32,96},{40,104},{48,112},{56,120},{... | collective-permute-start | bytes 786440 | tf_op jit(solution)/shard_map/ppermute | solution.py:381
  78.9 10.2 %collective-permute-start.12 = (bf16[16,32,256]{2,1,0:T(8,128)(2,1)S(1)}, bf16[16,32,256]{2,1,0:T(8,128)(2,1)S(1)}, u32[]{:S(2)}, u32[]{:S(2)}) collective-permute-start(bf16[16,32,256]{2,1,0:T(8,128)(2,1)S(1)} %collective-permute-done.11.refs_8_), channel_id=1, source_target_pairs={{0,8},{8,0},{16,24},{24,16},{32,40},{40,32},{48,56},{56,48},{64,72... | collective-permute-start | bytes 786440 | tf_op jit(solution)/shard_map/ppermute | solution.py:381
  80.7 8.4 %collective-permute-start.10 = (bf16[16,32,256]{2,1,0:T(8,128)(2,1)S(1)}, bf16[16,32,256]{2,1,0:T(8,128)(2,1)S(1)}, u32[]{:S(2)}, u32[]{:S(2)}) collective-permute-start(bf16[16,32,256]{2,1,0:T(8,128)(2,1)S(1)} %collective-permute-done.9.refs_6_), channel_id=1, source_target_pairs={{0,8},{8,0},{16,24},{24,16},{32,40},{40,32},{48,56},{56,48},{64,72... | collective-permute-start | bytes 786440 | tf_op jit(solution)/shard_map/ppermute | solution.py:381
  81.6 8.1 %collective-permute-start.15 = (bf16[16,32,256]{2,1,0:T(8,128)(2,1)S(1)}, bf16[16,32,256]{2,1,0:T(8,128)(2,1)S(1)}, u32[]{:S(2)}, u32[]{:S(2)}) collective-permute-start(bf16[16,32,256]{2,1,0:T(8,128)(2,1)S(1)} %collective-permute-done.5.refs_2_), channel_id=1, source_target_pairs={{0,48},{8,56},{16,0},{24,8},{32,16},{40,24},{48,32},{56,40},{64,11... | collective-permute-start | bytes 786440 | tf_op jit(solution)/shard_map/ppermute | solution.py:381
  85.3 8.6 %collective-permute-start.13 = (bf16[16,32,256]{2,1,0:T(8,128)(2,1)S(1)}, bf16[16,32,256]{2,1,0:T(8,128)(2,1)S(1)}, u32[]{:S(2)}, u32[]{:S(2)}) collective-permute-start(bf16[16,32,256]{2,1,0:T(8,128)(2,1)S(1)} %collective-permute-done.5.refs_2_), channel_id=1, source_target_pairs={{0,16},{8,24},{16,32},{24,40},{32,48},{40,56},{48,0},{56,8},{64,80... | collective-permute-start | bytes 786440 | tf_op jit(solution)/shard_map/ppermute | solution.py:381
  86.8 8.4 %collective-permute-start.6 = (bf16[16,32,256]{2,1,0:T(8,128)(2,1)S(1)}, bf16[16,32,256]{2,1,0:T(8,128)(2,1)S(1)}, u32[]{:S(2)}, u32[]{:S(2)}) collective-permute-start(bf16[16,32,256]{2,1,0:T(8,128)(2,1)S(1)} %collective-permute-done.5.refs_2_), channel_id=1, source_target_pairs={{0,8},{8,0},{16,24},{24,16},{32,40},{40,32},{48,56},{56,48},{64,72... | collective-permute-start | bytes 786440 | tf_op jit(solution)/shard_map/ppermute | solution.py:381
  89.1 6.1 %collective-permute-start.8 = (bf16[16,32,256]{2,1,0:T(8,128)(2,1)S(1)}, bf16[16,32,256]{2,1,0:T(8,128)(2,1)S(1)}, u32[]{:S(2)}, u32[]{:S(2)}) collective-permute-start(bf16[16,32,256]{2,1,0:T(8,128)(2,1)S(1)} %collective-permute-done.7.refs_4_), channel_id=1, source_target_pairs={{0,8},{8,0},{16,24},{24,16},{32,40},{40,32},{48,56},{56,48},{64,72... | collective-permute-start | bytes 786440 | tf_op jit(solution)/shard_map/ppermute | solution.py:381
  89.1 6.1 %collective-permute-start.18 = (bf16[16,32,256]{2,1,0:T(8,128)(2,1)S(1)}, bf16[16,32,256]{2,1,0:T(8,128)(2,1)S(1)}, u32[]{:S(2)}, u32[]{:S(2)}) collective-permute-start(bf16[16,32,256]{2,1,0:T(8,128)(2,1)S(1)} %collective-permute-done.17.refs_14_), channel_id=1, source_target_pairs={{0,8},{8,0},{16,24},{24,16},{32,40},{40,32},{48,56},{56,48},{64,72... | collective-permute-start | bytes 786440 | tf_op jit(solution)/shard_map/ppermute | solution.py:381
  89.6 5.6 %collective-permute-start.16 = (bf16[16,32,256]{2,1,0:T(8,128)(2,1)S(1)}, bf16[16,32,256]{2,1,0:T(8,128)(2,1)S(1)}, u32[]{:S(2)}, u32[]{:S(2)}) collective-permute-start(bf16[16,32,256]{2,1,0:T(8,128)(2,1)S(1)} %collective-permute-done.15.refs_12_), channel_id=1, source_target_pairs={{0,8},{8,0},{16,24},{24,16},{32,40},{40,32},{48,56},{56,48},{64,72... | collective-permute-start | bytes 786440 | tf_op jit(solution)/shard_map/ppermute | solution.py:381
  93.8 2.5 %collective-permute-start.14 = (bf16[16,32,256]{2,1,0:T(8,128)(2,1)S(1)}, bf16[16,32,256]{2,1,0:T(8,128)(2,1)S(1)}, u32[]{:S(2)}, u32[]{:S(2)}) collective-permute-start(bf16[16,32,256]{2,1,0:T(8,128)(2,1)S(1)} %collective-permute-done.13.refs_10_), channel_id=1, source_target_pairs={{0,8},{8,0},{16,24},{24,16},{32,40},{40,32},{48,56},{56,48},{64,72... | collective-permute-start | bytes 786440 | tf_op jit(solution)/shard_map/ppermute | solution.py:381
